TPU v7x, 256 devices: a whole 4x4x8 slice. The times are simulated.
256 devices in a mesh: level: 2 (over core), gx: 4 (over x), yz: 32 (over z, y).
Axes of the slice: x: 4, y: 4, z: 8, core: 2. Of those that a mesh axis runs over, the one named last changes fastest.
Arguments:
- init_field: float32 [128, 512, 256], P('gx', 'yz'), may hold values from -6 to 6
- source: float32 [128, 512, 256], P('gx', 'yz'), may hold values from -4 to 4
- damping: float32 [128, 512, 256], P('gx', 'yz'), may hold values from 0.05 to 2
Outputs:
- final_states: float32 [2, 128, 512, 256], P('level', 'gx', 'yz')
All inputs are finite; a program needn't handle non-finite values.
Results may differ from a plain program's by a relative error of at most 0.0001.
Values sent between devices are 32-bit elements; how exact they have to be, the bound alone decides.
No kernel may reach another device: no remote copies, remote signals or barrier semaphores. Data moves between devices by JAX's collectives and lax.ppermute only.
A program may use at most 64 MiB of HBM per device.

v0:
```python
import functools

import jax
import jax.numpy as jnp
from jax import lax
from jax.sharding import Mesh
from jax.sharding import PartitionSpec as P

STEPS = 3
ITERS = 3
GX_YZ = ("gx", "yz_0", "yz_1")
YZ = ("yz_0", "yz_1")


diffusion_number = 1.0


def padded_2(shard, sides, width):
    edges = {}
    for axis, dim in sides:
        size, length = (lax.axis_size(axis), shard.shape[dim])
        up = [(i, (i + 1) % size) for i in range(size - 1)]
        last = lax.slice_in_dim(shard, length - width, length, axis=dim)
        initial = lax.slice_in_dim(shard, 0, width, axis=dim)
        edges[dim] = (
            lax.ppermute(last, axis, up),
            lax.ppermute(initial, axis, [(b, a) for a, b in up]),
        )
    done = []
    for _, dim in sides:
        low, high = edges[dim]
        around = [(width, width) if d in done else (0, 0) for d in range(shard.ndim)]
        shard = jnp.concatenate([jnp.pad(low, around), shard, jnp.pad(high, around)], axis=dim)
        done.append(dim)
    return shard


def one_axis_at_a_time(shard, axes):
    return functools.reduce(lax.psum, axes, shard)


def passed_along(block, axis, distance):
    devices = range(lax.axis_size(axis))
    route = [(i - distance, i) for i in devices if i - distance in devices]
    return lax.ppermute(block, axis, route)


def stencil_from(padded, field, damping):
    beside = padded[2:, 1:-1, :] + padded[:-2, 1:-1, :]
    beside = beside + padded[1:-1, 2:, :] + padded[1:-1, :-2, :]
    zero_plane = jnp.zeros_like(field[:, :, :1])
    beside = beside + jnp.concatenate([field[:, :, 1:], zero_plane], axis=2)
    beside = beside + jnp.concatenate([zero_plane, field[:, :, :-1]], axis=2)
    return damping * field + diffusion_number * (6.0 * field - beside)


def operate(field, damping):
    padded = padded_2(field, (("gx", 0), (YZ, 1)), 1)
    return field + stencil_from(padded, field, damping)


def two_products(resid, image):
    return (
        one_axis_at_a_time(jnp.sum(resid * resid), GX_YZ),
        one_axis_at_a_time(jnp.sum(resid * image), GX_YZ),
    )


def solve(target, guess, damping):
    answer = guess
    resid = target - operate(answer, damping)
    image = operate(resid, damping)
    norm_now, product = two_products(resid, image)
    alpha = norm_now / product
    direction, along = (resid, image)
    for step in range(ITERS):
        answer = answer + alpha * direction
        resid = resid - alpha * along
        if step + 1 < ITERS:
            image = operate(resid, damping)
            norm_next, product = two_products(resid, image)
            ratio = norm_next / norm_now
            alpha = norm_next / (product - ratio * norm_next / alpha)
            direction = resid + ratio * direction
            along = image + ratio * along
            norm_now = norm_next
    return answer


def per_device(init_field, source, damping):
    upper = lax.axis_index("level") == 1
    state = init_field
    older = jnp.where(upper, init_field, jnp.zeros_like(init_field))
    for rounds in range(STEPS + 1):
        if rounds == 0:
            extra = jnp.zeros_like(init_field)
        else:
            incoming = passed_along(state, "level", 1)
            change = incoming - older
            older = incoming
            padded = padded_2(change, (("gx", 0), (YZ, 1)), 1)
            extra = 0.5 * stencil_from(padded, change, damping)
        fresh = solve(state + source + extra, state, damping)
        if rounds == 0:
            state = jnp.where(upper, state, fresh)
        elif rounds == STEPS:
            state = jnp.where(upper, fresh, state)
        else:
            state = fresh
    return state[None]


def solution(mesh):
    split = Mesh(
        mesh.devices.reshape(mesh.shape["level"], mesh.shape["gx"], 8, 4),
        ("level", "gx", "yz_0", "yz_1"),
    )
    placed = (P("gx", YZ, None), P("gx", YZ, None), P("gx", YZ, None))
    return jax.shard_map(
        per_device,
        mesh=split,
        in_specs=placed,
        out_specs=P("level", "gx", YZ, None),
        check_vma=False,
    )
```

profile of v0, /device:TPU:8, one launch (start us, length us, event | category | flops | bytes accessed | tf_op | source)
XLA Modules:
  0.0 816.0 jit_solution(3187403558633558888)
XLA Ops:
  31.1 11.0 %all-reduce.111 = (f32[]{:T(128)}, f32[]{:T(128)}) all-reduce(f32[]{:T(128)} %get-tuple-element.28, f32[]{:T(128)} %get-tuple-element.27), channel_id=1, replica_groups=mesh['level'=2,'gx'=4,'yz_0'=8,'yz_1'=4] {'gx'}, use_global_device_ids=true, to_apply=%region_1.2 | all-reduce | flops 2 | bytes 16 | tf_op jit(solution)/shard_map/psum | solution.py:39
  42.2 25.3 %all-reduce.87 = (f32[]{:T(128)}, f32[]{:T(128)}) all-reduce(f32[]{:T(128)} %get-tuple-element.99, f32[]{:T(128)} %get-tuple-element.100), channel_id=1, replica_groups=mesh['level'=2,'gx'=4,'yz_0'=8,'yz_1'=4] {'yz_0'}, use_global_device_ids=true, to_apply=%region_2.3 | all-reduce | flops 2 | bytes 16 | tf_op jit(solution)/shard_map/psum | solution.py:39
  67.4 11.3 %all-reduce.99 = (f32[]{:T(128)}, f32[]{:T(128)}) all-reduce(f32[]{:T(128)} %get-tuple-element.51, f32[]{:T(128)} %get-tuple-element.52), channel_id=1, replica_groups=mesh['level'=2,'gx'=4,'yz_0'=8,'yz_1'=4] {'yz_1'}, use_global_device_ids=true, to_apply=%region_3.4 | all-reduce | flops 2 | bytes 16 | tf_op jit(solution)/shard_map/psum | solution.py:39
  93.9 11.0 %all-reduce.110 = (f32[]{:T(128)}, f32[]{:T(128)}) all-reduce(f32[]{:T(128)} %get-tuple-element.26, f32[]{:T(128)} %get-tuple-element.25), channel_id=1, replica_groups=mesh['level'=2,'gx'=4,'yz_0'=8,'yz_1'=4] {'gx'}, use_global_device_ids=true, to_apply=%region_9.10 | all-reduce | flops 2 | bytes 16 | tf_op jit(solution)/shard_map/psum | solution.py:39
  104.9 16.3 %all-reduce.86 = (f32[]{:T(128)}, f32[]{:T(128)}) all-reduce(f32[]{:T(128)} %get-tuple-element.97, f32[]{:T(128)} %get-tuple-element.98), channel_id=1, replica_groups=mesh['level'=2,'gx'=4,'yz_0'=8,'yz_1'=4] {'yz_0'}, use_global_device_ids=true, to_apply=%region_10.11 | all-reduce | flops 2 | bytes 16 | tf_op jit(solution)/shard_map/psum | solution.py:39
  121.2 12.5 %all-reduce.98 = (f32[]{:T(128)}, f32[]{:T(128)}) all-reduce(f32[]{:T(128)} %get-tuple-element.49, f32[]{:T(128)} %get-tuple-element.50), channel_id=1, replica_groups=mesh['level'=2,'gx'=4,'yz_0'=8,'yz_1'=4] {'yz_1'}, use_global_device_ids=true, to_apply=%region_11.12 | all-reduce | flops 2 | bytes 16 | tf_op jit(solution)/shard_map/psum | solution.py:39
  150.8 11.4 %all-reduce.109 = (f32[]{:T(128)}, f32[]{:T(128)}) all-reduce(f32[]{:T(128)} %get-tuple-element.24, f32[]{:T(128)} %get-tuple-element.23), channel_id=1, replica_groups=mesh['level'=2,'gx'=4,'yz_0'=8,'yz_1'=4] {'gx'}, use_global_device_ids=true, to_apply=%region_17.18 | all-reduce | flops 2 | bytes 16 | tf_op jit(solution)/shard_map/psum | solution.py:39
  162.2 17.3 %all-reduce.85 = (f32[]{:T(128)}, f32[]{:T(128)}) all-reduce(f32[]{:T(128)} %get-tuple-element.95, f32[]{:T(128)} %get-tuple-element.96), channel_id=1, replica_groups=mesh['level'=2,'gx'=4,'yz_0'=8,'yz_1'=4] {'yz_0'}, use_global_device_ids=true, to_apply=%region_18.19 | all-reduce | flops 2 | bytes 16 | tf_op jit(solution)/shard_map/psum | solution.py:39
  179.5 11.9 %all-reduce.97 = (f32[]{:T(128)}, f32[]{:T(128)}) all-reduce(f32[]{:T(128)} %get-tuple-element.47, f32[]{:T(128)} %get-tuple-element.48), channel_id=1, replica_groups=mesh['level'=2,'gx'=4,'yz_0'=8,'yz_1'=4] {'yz_1'}, use_global_device_ids=true, to_apply=%region_19.20 | all-reduce | flops 2 | bytes 16 | tf_op jit(solution)/shard_map/psum | solution.py:39
  248.2 24.6 %all-reduce.84 = (f32[]{:T(128)}, f32[]{:T(128)}) all-reduce(f32[]{:T(128)} %get-tuple-element.93, f32[]{:T(128)} %get-tuple-element.94), channel_id=1, replica_groups=mesh['level'=2,'gx'=4,'yz_0'=8,'yz_1'=4] {'yz_0'}, use_global_device_ids=true, to_apply=%region_26.27 | all-reduce | flops 2 | bytes 16 | tf_op jit(solution)/shard_map/psum | solution.py:39
  272.8 11.7 %all-reduce.96 = (f32[]{:T(128)}, f32[]{:T(128)}) all-reduce(f32[]{:T(128)} %get-tuple-element.45, f32[]{:T(128)} %get-tuple-element.46), channel_id=1, replica_groups=mesh['level'=2,'gx'=4,'yz_0'=8,'yz_1'=4] {'yz_1'}, use_global_device_ids=true, to_apply=%region_27.28 | all-reduce | flops 2 | bytes 16 | tf_op jit(solution)/shard_map/psum | solution.py:39
  298.8 11.0 %all-reduce.107 = (f32[]{:T(128)}, f32[]{:T(128)}) all-reduce(f32[]{:T(128)} %get-tuple-element.20, f32[]{:T(128)} %get-tuple-element.19), channel_id=1, replica_groups=mesh['level'=2,'gx'=4,'yz_0'=8,'yz_1'=4] {'gx'}, use_global_device_ids=true, to_apply=%region_33.34 | all-reduce | flops 2 | bytes 16 | tf_op jit(solution)/shard_map/psum | solution.py:39
  309.8 17.8 %all-reduce.83 = (f32[]{:T(128)}, f32[]{:T(128)}) all-reduce(f32[]{:T(128)} %get-tuple-element.91, f32[]{:T(128)} %get-tuple-element.92), channel_id=1, replica_groups=mesh['level'=2,'gx'=4,'yz_0'=8,'yz_1'=4] {'yz_0'}, use_global_device_ids=true, to_apply=%region_34.35 | all-reduce | flops 2 | bytes 16 | tf_op jit(solution)/shard_map/psum | solution.py:39
  327.6 11.9 %all-reduce.95 = (f32[]{:T(128)}, f32[]{:T(128)}) all-reduce(f32[]{:T(128)} %get-tuple-element.43, f32[]{:T(128)} %get-tuple-element.44), channel_id=1, replica_groups=mesh['level'=2,'gx'=4,'yz_0'=8,'yz_1'=4] {'yz_1'}, use_global_device_ids=true, to_apply=%region_35.36 | all-reduce | flops 2 | bytes 16 | tf_op jit(solution)/shard_map/psum | solution.py:39
  368.7 17.8 %all-reduce.82 = (f32[]{:T(128)}, f32[]{:T(128)}) all-reduce(f32[]{:T(128)} %get-tuple-element.89, f32[]{:T(128)} %get-tuple-element.90), channel_id=1, replica_groups=mesh['level'=2,'gx'=4,'yz_0'=8,'yz_1'=4] {'yz_0'}, use_global_device_ids=true, to_apply=%region_42.43 | all-reduce | flops 2 | bytes 16 | tf_op jit(solution)/shard_map/psum | solution.py:39
  386.5 12.1 %all-reduce.94 = (f32[]{:T(128)}, f32[]{:T(128)}) all-reduce(f32[]{:T(128)} %get-tuple-element.41, f32[]{:T(128)} %get-tuple-element.42), channel_id=1, replica_groups=mesh['level'=2,'gx'=4,'yz_0'=8,'yz_1'=4] {'yz_1'}, use_global_device_ids=true, to_apply=%region_43.44 | all-reduce | flops 2 | bytes 16 | tf_op jit(solution)/shard_map/psum | solution.py:39
  454.4 24.6 %all-reduce.81 = (f32[]{:T(128)}, f32[]{:T(128)}) all-reduce(f32[]{:T(128)} %get-tuple-element.87, f32[]{:T(128)} %get-tuple-element.88), channel_id=1, replica_groups=mesh['level'=2,'gx'=4,'yz_0'=8,'yz_1'=4] {'yz_0'}, use_global_device_ids=true, to_apply=%region_50.51 | all-reduce | flops 2 | bytes 16 | tf_op jit(solution)/shard_map/psum | solution.py:39
  479.0 11.7 %all-reduce.93 = (f32[]{:T(128)}, f32[]{:T(128)}) all-reduce(f32[]{:T(128)} %get-tuple-element.39, f32[]{:T(128)} %get-tuple-element.40), channel_id=1, replica_groups=mesh['level'=2,'gx'=4,'yz_0'=8,'yz_1'=4] {'yz_1'}, use_global_device_ids=true, to_apply=%region_51.52 | all-reduce | flops 2 | bytes 16 | tf_op jit(solution)/shard_map/psum | solution.py:39
  505.7 11.0 %all-reduce.104 = (f32[]{:T(128)}, f32[]{:T(128)}) all-reduce(f32[]{:T(128)} %get-tuple-element.14, f32[]{:T(128)} %get-tuple-element.13), channel_id=1, replica_groups=mesh['level'=2,'gx'=4,'yz_0'=8,'yz_1'=4] {'gx'}, use_global_device_ids=true, to_apply=%region_57.58 | all-reduce | flops 2 | bytes 16 | tf_op jit(solution)/shard_map/psum | solution.py:39
  516.7 17.8 %all-reduce.80 = (f32[]{:T(128)}, f32[]{:T(128)}) all-reduce(f32[]{:T(128)} %get-tuple-element.85, f32[]{:T(128)} %get-tuple-element.86), channel_id=1, replica_groups=mesh['level'=2,'gx'=4,'yz_0'=8,'yz_1'=4] {'yz_0'}, use_global_device_ids=true, to_apply=%region_58.59 | all-reduce | flops 2 | bytes 16 | tf_op jit(solution)/shard_map/psum | solution.py:39
  534.5 11.9 %all-reduce.92 = (f32[]{:T(128)}, f32[]{:T(128)}) all-reduce(f32[]{:T(128)} %get-tuple-element.37, f32[]{:T(128)} %get-tuple-element.38), channel_id=1, replica_groups=mesh['level'=2,'gx'=4,'yz_0'=8,'yz_1'=4] {'yz_1'}, use_global_device_ids=true, to_apply=%region_59.60 | all-reduce | flops 2 | bytes 16 | tf_op jit(solution)/shard_map/psum | solution.py:39
  574.8 17.8 %all-reduce.79 = (f32[]{:T(128)}, f32[]{:T(128)}) all-reduce(f32[]{:T(128)} %get-tuple-element.83, f32[]{:T(128)} %get-tuple-element.84), channel_id=1, replica_groups=mesh['level'=2,'gx'=4,'yz_0'=8,'yz_1'=4] {'yz_0'}, use_global_device_ids=true, to_apply=%region_66.67 | all-reduce | flops 2 | bytes 16 | tf_op jit(solution)/shard_map/psum | solution.py:39
  592.6 11.9 %all-reduce.91 = (f32[]{:T(128)}, f32[]{:T(128)}) all-reduce(f32[]{:T(128)} %get-tuple-element.35, f32[]{:T(128)} %get-tuple-element.36), channel_id=1, replica_groups=mesh['level'=2,'gx'=4,'yz_0'=8,'yz_1'=4] {'yz_1'}, use_global_device_ids=true, to_apply=%region_67.68 | all-reduce | flops 2 | bytes 16 | tf_op jit(solution)/shard_map/psum | solution.py:39
  649.3 11.0 %all-reduce.102 = (f32[]{:T(128)}, f32[]{:T(128)}) all-reduce(f32[]{:T(128)} %get-tuple-element.10, f32[]{:T(128)} %get-tuple-element.9), channel_id=1, replica_groups=mesh['level'=2,'gx'=4,'yz_0'=8,'yz_1'=4] {'gx'}, use_global_device_ids=true, to_apply=%region_73.74 | all-reduce | flops 2 | bytes 16 | tf_op jit(solution)/shard_map/psum | solution.py:39
  660.4 24.6 %all-reduce.78 = (f32[]{:T(128)}, f32[]{:T(128)}) all-reduce(f32[]{:T(128)} %get-tuple-element.81, f32[]{:T(128)} %get-tuple-element.82), channel_id=1, replica_groups=mesh['level'=2,'gx'=4,'yz_0'=8,'yz_1'=4] {'yz_0'}, use_global_device_ids=true, to_apply=%region_74.75 | all-reduce | flops 2 | bytes 16 | tf_op jit(solution)/shard_map/psum | solution.py:39
  685.0 11.7 %all-reduce.90 = (f32[]{:T(128)}, f32[]{:T(128)}) all-reduce(f32[]{:T(128)} %get-tuple-element.33, f32[]{:T(128)} %get-tuple-element.34), channel_id=1, replica_groups=mesh['level'=2,'gx'=4,'yz_0'=8,'yz_1'=4] {'yz_1'}, use_global_device_ids=true, to_apply=%region_75.76 | all-reduce | flops 2 | bytes 16 | tf_op jit(solution)/shard_map/psum | solution.py:39
  711.1 11.0 %all-reduce.101 = (f32[]{:T(128)}, f32[]{:T(128)}) all-reduce(f32[]{:T(128)} %get-tuple-element.8, f32[]{:T(128)} %get-tuple-element.7), channel_id=1, replica_groups=mesh['level'=2,'gx'=4,'yz_0'=8,'yz_1'=4] {'gx'}, use_global_device_ids=true, to_apply=%region_81.82 | all-reduce | flops 2 | bytes 16 | tf_op jit(solution)/shard_map/psum | solution.py:39
  722.1 17.8 %all-reduce.77 = (f32[]{:T(128)}, f32[]{:T(128)}) all-reduce(f32[]{:T(128)} %get-tuple-element.79, f32[]{:T(128)} %get-tuple-element.80), channel_id=1, replica_groups=mesh['level'=2,'gx'=4,'yz_0'=8,'yz_1'=4] {'yz_0'}, use_global_device_ids=true, to_apply=%region_82.83 | all-reduce | flops 2 | bytes 16 | tf_op jit(solution)/shard_map/psum | solution.py:39
  739.9 11.9 %all-reduce.89 = (f32[]{:T(128)}, f32[]{:T(128)}) all-reduce(f32[]{:T(128)} %get-tuple-element.31, f32[]{:T(128)} %get-tuple-element.32), channel_id=1, replica_groups=mesh['level'=2,'gx'=4,'yz_0'=8,'yz_1'=4] {'yz_1'}, use_global_device_ids=true, to_apply=%region_83.84 | all-reduce | flops 2 | bytes 16 | tf_op jit(solution)/shard_map/psum | solution.py:39
  770.3 11.0 %all-reduce.100 = (f32[]{:T(128)}, f32[]{:T(128)}) all-reduce(f32[]{:T(128)} %get-tuple-element.6, f32[]{:T(128)} %get-tuple-element.5), channel_id=1, replica_groups=mesh['level'=2,'gx'=4,'yz_0'=8,'yz_1'=4] {'gx'}, use_global_device_ids=true, to_apply=%region_89.90 | all-reduce | flops 2 | bytes 16 | tf_op jit(solution)/shard_map/psum | solution.py:39
  781.3 17.8 %all-reduce.76 = (f32[]{:T(128)}, f32[]{:T(128)}) all-reduce(f32[]{:T(128)} %get-tuple-element.77, f32[]{:T(128)} %get-tuple-element.78), channel_id=1, replica_groups=mesh['level'=2,'gx'=4,'yz_0'=8,'yz_1'=4] {'yz_0'}, use_global_device_ids=true, to_apply=%region_90.91 | all-reduce | flops 2 | bytes 16 | tf_op jit(solution)/shard_map/psum | solution.py:39
  799.1 11.9 %all-reduce.88 = (f32[]{:T(128)}, f32[]{:T(128)}) all-reduce(f32[]{:T(128)} %get-tuple-element.29, f32[]{:T(128)} %get-tuple-element.30), channel_id=1, replica_groups=mesh['level'=2,'gx'=4,'yz_0'=8,'yz_1'=4] {'yz_1'}, use_global_device_ids=true, to_apply=%region_91.92 | all-reduce | flops 2 | bytes 16 | tf_op jit(solution)/shard_map/psum | solution.py:39
  (273 shorter events, 306.8 us)
Async XLA Ops:
  0.7 14.6 %collective-permute-start = (f32[1,16,256]{2,1,0:T(8,128)S(1)}, f32[1,16,256]{2,1,0:T(8,128)S(1)}, u32[]{:S(2)}, u32[]{:S(2)}) collective-permute-start(f32[1,16,256]{2,1,0:T(8,128)S(1)} %get-tuple-element.221), channel_id=1, source_target_pairs={{32,0},{64,32},{96,64},{33,1},{65,33},{97,65},{34,2},{66,34},{98,6... | collective-permute-start | bytes 49160 | tf_op jit(solution)/shard_map/ppermute | solution.py:27
  2.0 13.2 %collective-permute-start.1 = (f32[1,16,256]{2,1,0:T(8,128)S(1)}, f32[1,16,256]{2,1,0:T(8,128)S(1)}, u32[]{:S(2)}, u32[]{:S(2)}) collective-permute-start(f32[1,16,256]{2,1,0:T(8,128)S(1)} %get-tuple-element.222), channel_id=1, source_target_pairs={{0,32},{32,64},{64,96},{1,33},{33,65},{65,97},{2,34},{34,66},{66,9... | collective-permute-start | bytes 49160 | tf_op jit(solution)/shard_map/ppermute | solution.py:26
  18.3 9.4 %collective-permute-start.5 = (f32[1,16,256]{2,1,0:T(8,128)S(1)}, f32[1,16,256]{2,1,0:T(8,128)S(1)}, u32[]{:S(2)}, u32[]{:S(2)}) collective-permute-start(f32[1,16,256]{2,1,0:T(8,128)S(1)} %get-tuple-element.213), channel_id=1, source_target_pairs={{0,32},{32,64},{64,96},{1,33},{33,65},{65,97},{2,34},{34,66},{66,9... | collective-permute-start | bytes 49160 | tf_op jit(solution)/shard_map/ppermute | solution.py:26
  80.2 10.1 %collective-permute-start.9 = (f32[1,16,256]{2,1,0:T(8,128)S(1)}, f32[1,16,256]{2,1,0:T(8,128)S(1)}, u32[]{:S(2)}, u32[]{:S(2)}) collective-permute-start(f32[1,16,256]{2,1,0:T(8,128)S(1)} %get-tuple-element.207), channel_id=1, source_target_pairs={{0,32},{32,64},{64,96},{1,33},{33,65},{65,97},{2,34},{34,66},{66,9... | collective-permute-start | bytes 49160 | tf_op jit(solution)/shard_map/ppermute | solution.py:26
  139.4 8.7 %collective-permute-start.13 = (f32[1,16,256]{2,1,0:T(8,128)S(1)}, f32[1,16,256]{2,1,0:T(8,128)S(1)}, u32[]{:S(2)}, u32[]{:S(2)}) collective-permute-start(f32[1,16,256]{2,1,0:T(8,128)S(1)} %get-tuple-element.203), channel_id=1, source_target_pairs={{0,32},{32,64},{64,96},{1,33},{33,65},{65,97},{2,34},{34,66},{66,9... | collective-permute-start | bytes 49160 | tf_op jit(solution)/shard_map/ppermute | solution.py:26
  195.6 11.1 %collective-permute-start.16 = (f32[32,16,256]{2,1,0:T(8,128)S(1)}, f32[32,16,256]{2,1,0:T(8,128)S(1)}, u32[]{:S(2)}, u32[]{:S(2)}) collective-permute-start(f32[32,16,256]{2,1,0:T(8,128)S(1)} %add_select_fusion), channel_id=1, source_target_pairs={{0,128},{1,129},{2,130},{3,131},{4,132},{5,133},{6,134},{7,135},{8... | collective-permute-start | bytes 1572872 | tf_op jit(solution)/shard_map/ppermute | solution.py:45
  197.0 15.2 %collective-permute-start.22 = (f32[1,16,256]{2,1,0:T(8,128)S(1)}, f32[1,16,256]{2,1,0:T(8,128)S(1)}, u32[]{:S(2)}, u32[]{:S(2)}) collective-permute-start(f32[1,16,256]{2,1,0:T(8,128)S(1)} %get-tuple-element.197), channel_id=1, source_target_pairs={{0,32},{32,64},{64,96},{1,33},{33,65},{65,97},{2,34},{34,66},{66,9... | collective-permute-start | bytes 49160 | tf_op jit(solution)/shard_map/ppermute | solution.py:26
  199.3 14.2 %collective-permute-start.21 = (f32[1,16,256]{2,1,0:T(8,128)S(1)}, f32[1,16,256]{2,1,0:T(8,128)S(1)}, u32[]{:S(2)}, u32[]{:S(2)}) collective-permute-start(f32[1,16,256]{2,1,0:T(8,128)S(1)} %get-tuple-element.198), channel_id=1, source_target_pairs={{32,0},{64,32},{96,64},{33,1},{65,33},{97,65},{34,2},{66,34},{98,6... | collective-permute-start | bytes 49160 | tf_op jit(solution)/shard_map/ppermute | solution.py:27
  200.7 15.0 %collective-permute-start.23 = (f32[32,1,256]{2,1,0:T(1,128)S(1)}, f32[32,1,256]{2,1,0:T(1,128)S(1)}, u32[]{:S(2)}, u32[]{:S(2)}) collective-permute-start(f32[32,1,256]{2,1,0:T(1,128)S(1)} %get-tuple-element.195), channel_id=1, source_target_pairs={{1,0},{2,1},{3,2},{4,3},{5,4},{6,5},{7,6},{8,7},{9,8},{10,9},{11,1... | collective-permute-start | bytes 98312 | tf_op jit(solution)/shard_map/ppermute | solution.py:27
  202.9 16.8 %collective-permute-start.24 = (f32[32,1,256]{2,1,0:T(1,128)S(1)}, f32[32,1,256]{2,1,0:T(1,128)S(1)}, u32[]{:S(2)}, u32[]{:S(2)}) collective-permute-start(f32[32,1,256]{2,1,0:T(1,128)S(1)} %get-tuple-element.196), channel_id=1, source_target_pairs={{0,1},{1,2},{2,3},{3,4},{4,5},{5,6},{6,7},{7,8},{8,9},{9,10},{10,1... | collective-permute-start | bytes 98312 | tf_op jit(solution)/shard_map/ppermute | solution.py:26
  207.6 12.1 %collective-permute-start.18 = (f32[1,16,256]{2,1,0:T(8,128)S(1)}, f32[1,16,256]{2,1,0:T(8,128)S(1)}, u32[]{:S(2)}, u32[]{:S(2)}) collective-permute-start(f32[1,16,256]{2,1,0:T(8,128)S(1)} %get-tuple-element.193), channel_id=1, source_target_pairs={{0,32},{32,64},{64,96},{1,33},{33,65},{65,97},{2,34},{34,66},{66,9... | collective-permute-start | bytes 49160 | tf_op jit(solution)/shard_map/ppermute | solution.py:26
  222.5 11.9 %collective-permute-start.26 = (f32[1,16,256]{2,1,0:T(8,128)S(1)}, f32[1,16,256]{2,1,0:T(8,128)S(1)}, u32[]{:S(2)}, u32[]{:S(2)}) collective-permute-start(f32[1,16,256]{2,1,0:T(8,128)S(1)} %get-tuple-element.183), channel_id=1, source_target_pairs={{0,32},{32,64},{64,96},{1,33},{33,65},{65,97},{2,34},{34,66},{66,9... | collective-permute-start | bytes 49160 | tf_op jit(solution)/shard_map/ppermute | solution.py:26
  285.9 9.0 %collective-permute-start.30 = (f32[1,16,256]{2,1,0:T(8,128)S(1)}, f32[1,16,256]{2,1,0:T(8,128)S(1)}, u32[]{:S(2)}, u32[]{:S(2)}) collective-permute-start(f32[1,16,256]{2,1,0:T(8,128)S(1)} %get-tuple-element.177), channel_id=1, source_target_pairs={{0,32},{32,64},{64,96},{1,33},{33,65},{65,97},{2,34},{34,66},{66,9... | collective-permute-start | bytes 49160 | tf_op jit(solution)/shard_map/ppermute | solution.py:26
  345.0 9.7 %collective-permute-start.34 = (f32[1,16,256]{2,1,0:T(8,128)S(1)}, f32[1,16,256]{2,1,0:T(8,128)S(1)}, u32[]{:S(2)}, u32[]{:S(2)}) collective-permute-start(f32[1,16,256]{2,1,0:T(8,128)S(1)} %get-tuple-element.173), channel_id=1, source_target_pairs={{0,32},{32,64},{64,96},{1,33},{33,65},{65,97},{2,34},{34,66},{66,9... | collective-permute-start | bytes 49160 | tf_op jit(solution)/shard_map/ppermute | solution.py:26
  402.3 10.6 %collective-permute-start.37 = (f32[32,16,256]{2,1,0:T(8,128)S(1)}, f32[32,16,256]{2,1,0:T(8,128)S(1)}, u32[]{:S(2)}, u32[]{:S(2)}) collective-permute-start(f32[32,16,256]{2,1,0:T(8,128)S(1)} %multiply_add_fusion.1), channel_id=1, source_target_pairs={{0,128},{1,129},{2,130},{3,131},{4,132},{5,133},{6,134},{7,135},{8... | collective-permute-start | bytes 1572872 | tf_op jit(solution)/shard_map/ppermute | solution.py:45
  403.7 14.7 %collective-permute-start.43 = (f32[1,16,256]{2,1,0:T(8,128)S(1)}, f32[1,16,256]{2,1,0:T(8,128)S(1)}, u32[]{:S(2)}, u32[]{:S(2)}) collective-permute-start(f32[1,16,256]{2,1,0:T(8,128)S(1)} %get-tuple-element.167), channel_id=1, source_target_pairs={{0,32},{32,64},{64,96},{1,33},{33,65},{65,97},{2,34},{34,66},{66,9... | collective-permute-start | bytes 49160 | tf_op jit(solution)/shard_map/ppermute | solution.py:26
  405.3 14.3 %collective-permute-start.42 = (f32[1,16,256]{2,1,0:T(8,128)S(1)}, f32[1,16,256]{2,1,0:T(8,128)S(1)}, u32[]{:S(2)}, u32[]{:S(2)}) collective-permute-start(f32[1,16,256]{2,1,0:T(8,128)S(1)} %get-tuple-element.168), channel_id=1, source_target_pairs={{32,0},{64,32},{96,64},{33,1},{65,33},{97,65},{34,2},{66,34},{98,6... | collective-permute-start | bytes 49160 | tf_op jit(solution)/shard_map/ppermute | solution.py:27
  406.7 15.1 %collective-permute-start.44 = (f32[32,1,256]{2,1,0:T(1,128)S(1)}, f32[32,1,256]{2,1,0:T(1,128)S(1)}, u32[]{:S(2)}, u32[]{:S(2)}) collective-permute-start(f32[32,1,256]{2,1,0:T(1,128)S(1)} %get-tuple-element.165), channel_id=1, source_target_pairs={{1,0},{2,1},{3,2},{4,3},{5,4},{6,5},{7,6},{8,7},{9,8},{10,9},{11,1... | collective-permute-start | bytes 98312 | tf_op jit(solution)/shard_map/ppermute | solution.py:27
  408.9 17.0 %collective-permute-start.45 = (f32[32,1,256]{2,1,0:T(1,128)S(1)}, f32[32,1,256]{2,1,0:T(1,128)S(1)}, u32[]{:S(2)}, u32[]{:S(2)}) collective-permute-start(f32[32,1,256]{2,1,0:T(1,128)S(1)} %get-tuple-element.166), channel_id=1, source_target_pairs={{0,1},{1,2},{2,3},{3,4},{4,5},{5,6},{6,7},{7,8},{8,9},{9,10},{10,1... | collective-permute-start | bytes 98312 | tf_op jit(solution)/shard_map/ppermute | solution.py:26
  413.8 12.1 %collective-permute-start.39 = (f32[1,16,256]{2,1,0:T(8,128)S(1)}, f32[1,16,256]{2,1,0:T(8,128)S(1)}, u32[]{:S(2)}, u32[]{:S(2)}) collective-permute-start(f32[1,16,256]{2,1,0:T(8,128)S(1)} %get-tuple-element.163), channel_id=1, source_target_pairs={{0,32},{32,64},{64,96},{1,33},{33,65},{65,97},{2,34},{34,66},{66,9... | collective-permute-start | bytes 49160 | tf_op jit(solution)/shard_map/ppermute | solution.py:26
  428.7 11.9 %collective-permute-start.47 = (f32[1,16,256]{2,1,0:T(8,128)S(1)}, f32[1,16,256]{2,1,0:T(8,128)S(1)}, u32[]{:S(2)}, u32[]{:S(2)}) collective-permute-start(f32[1,16,256]{2,1,0:T(8,128)S(1)} %get-tuple-element.153), channel_id=1, source_target_pairs={{0,32},{32,64},{64,96},{1,33},{33,65},{65,97},{2,34},{34,66},{66,9... | collective-permute-start | bytes 49160 | tf_op jit(solution)/shard_map/ppermute | solution.py:26
  492.1 9.7 %collective-permute-start.51 = (f32[1,16,256]{2,1,0:T(8,128)S(1)}, f32[1,16,256]{2,1,0:T(8,128)S(1)}, u32[]{:S(2)}, u32[]{:S(2)}) collective-permute-start(f32[1,16,256]{2,1,0:T(8,128)S(1)} %get-tuple-element.147), channel_id=1, source_target_pairs={{0,32},{32,64},{64,96},{1,33},{33,65},{65,97},{2,34},{34,66},{66,9... | collective-permute-start | bytes 49160 | tf_op jit(solution)/shard_map/ppermute | solution.py:26
  551.8 9.1 %collective-permute-start.55 = (f32[1,16,256]{2,1,0:T(8,128)S(1)}, f32[1,16,256]{2,1,0:T(8,128)S(1)}, u32[]{:S(2)}, u32[]{:S(2)}) collective-permute-start(f32[1,16,256]{2,1,0:T(8,128)S(1)} %get-tuple-element.143), channel_id=1, source_target_pairs={{0,32},{32,64},{64,96},{1,33},{33,65},{65,97},{2,34},{34,66},{66,9... | collective-permute-start | bytes 49160 | tf_op jit(solution)/shard_map/ppermute | solution.py:26
  608.3 11.3 %collective-permute-start.58 = (f32[32,16,256]{2,1,0:T(8,128)S(1)}, f32[32,16,256]{2,1,0:T(8,128)S(1)}, u32[]{:S(2)}, u32[]{:S(2)}) collective-permute-start(f32[32,16,256]{2,1,0:T(8,128)S(1)} %multiply_add_fusion), channel_id=1, source_target_pairs={{0,128},{1,129},{2,130},{3,131},{4,132},{5,133},{6,134},{7,135},{8... | collective-permute-start | bytes 1572872 | tf_op jit(solution)/shard_map/ppermute | solution.py:45
  609.6 14.7 %collective-permute-start.64 = (f32[1,16,256]{2,1,0:T(8,128)S(1)}, f32[1,16,256]{2,1,0:T(8,128)S(1)}, u32[]{:S(2)}, u32[]{:S(2)}) collective-permute-start(f32[1,16,256]{2,1,0:T(8,128)S(1)} %get-tuple-element.137), channel_id=1, source_target_pairs={{0,32},{32,64},{64,96},{1,33},{33,65},{65,97},{2,34},{34,66},{66,9... | collective-permute-start | bytes 49160 | tf_op jit(solution)/shard_map/ppermute | solution.py:26
  612.0 13.6 %collective-permute-start.63 = (f32[1,16,256]{2,1,0:T(8,128)S(1)}, f32[1,16,256]{2,1,0:T(8,128)S(1)}, u32[]{:S(2)}, u32[]{:S(2)}) collective-permute-start(f32[1,16,256]{2,1,0:T(8,128)S(1)} %get-tuple-element.138), channel_id=1, source_target_pairs={{32,0},{64,32},{96,64},{33,1},{65,33},{97,65},{34,2},{66,34},{98,6... | collective-permute-start | bytes 49160 | tf_op jit(solution)/shard_map/ppermute | solution.py:27
  613.4 14.4 %collective-permute-start.65 = (f32[32,1,256]{2,1,0:T(1,128)S(1)}, f32[32,1,256]{2,1,0:T(1,128)S(1)}, u32[]{:S(2)}, u32[]{:S(2)}) collective-permute-start(f32[32,1,256]{2,1,0:T(1,128)S(1)} %get-tuple-element.135), channel_id=1, source_target_pairs={{1,0},{2,1},{3,2},{4,3},{5,4},{6,5},{7,6},{8,7},{9,8},{10,9},{11,1... | collective-permute-start | bytes 98312 | tf_op jit(solution)/shard_map/ppermute | solution.py:27
  615.6 16.3 %collective-permute-start.66 = (f32[32,1,256]{2,1,0:T(1,128)S(1)}, f32[32,1,256]{2,1,0:T(1,128)S(1)}, u32[]{:S(2)}, u32[]{:S(2)}) collective-permute-start(f32[32,1,256]{2,1,0:T(1,128)S(1)} %get-tuple-element.136), channel_id=1, source_target_pairs={{0,1},{1,2},{2,3},{3,4},{4,5},{5,6},{6,7},{7,8},{8,9},{9,10},{10,1... | collective-permute-start | bytes 98312 | tf_op jit(solution)/shard_map/ppermute | solution.py:26
  619.8 12.1 %collective-permute-start.60 = (f32[1,16,256]{2,1,0:T(8,128)S(1)}, f32[1,16,256]{2,1,0:T(8,128)S(1)}, u32[]{:S(2)}, u32[]{:S(2)}) collective-permute-start(f32[1,16,256]{2,1,0:T(8,128)S(1)} %get-tuple-element.133), channel_id=1, source_target_pairs={{0,32},{32,64},{64,96},{1,33},{33,65},{65,97},{2,34},{34,66},{66,9... | collective-permute-start | bytes 49160 | tf_op jit(solution)/shard_map/ppermute | solution.py:26
  634.6 11.9 %collective-permute-start.68 = (f32[1,16,256]{2,1,0:T(8,128)S(1)}, f32[1,16,256]{2,1,0:T(8,128)S(1)}, u32[]{:S(2)}, u32[]{:S(2)}) collective-permute-start(f32[1,16,256]{2,1,0:T(8,128)S(1)} %get-tuple-element.123), channel_id=1, source_target_pairs={{0,32},{32,64},{64,96},{1,33},{33,65},{65,97},{2,34},{34,66},{66,9... | collective-permute-start | bytes 49160 | tf_op jit(solution)/shard_map/ppermute | solution.py:26
  698.2 9.0 %collective-permute-start.72 = (f32[1,16,256]{2,1,0:T(8,128)S(1)}, f32[1,16,256]{2,1,0:T(8,128)S(1)}, u32[]{:S(2)}, u32[]{:S(2)}) collective-permute-start(f32[1,16,256]{2,1,0:T(8,128)S(1)} %get-tuple-element.117), channel_id=1, source_target_pairs={{0,32},{32,64},{64,96},{1,33},{33,65},{65,97},{2,34},{34,66},{66,9... | collective-permute-start | bytes 49160 | tf_op jit(solution)/shard_map/ppermute | solution.py:26
  757.5 9.7 %collective-permute-start.76 = (f32[1,16,256]{2,1,0:T(8,128)S(1)}, f32[1,16,256]{2,1,0:T(8,128)S(1)}, u32[]{:S(2)}, u32[]{:S(2)}) collective-permute-start(f32[1,16,256]{2,1,0:T(8,128)S(1)} %get-tuple-element.113), channel_id=1, source_target_pairs={{0,32},{32,64},{64,96},{1,33},{33,65},{65,97},{2,34},{34,66},{66,9... | collective-permute-start | bytes 49160 | tf_op jit(solution)/shard_map/ppermute | solution.py:26
  (57 other events, 340.2 us)
where the time goes:
time: 820 us; the launch traced here: 816 us
  blocking collectives  515 us (63%)
  starting transfers between devices  197 us (24%)
  between operations  38.5 us (5%)
  waiting for transfers between devices  30 us (4%)
  other arithmetic  26.8 us (3%)
  local copies, waits for them, and re-layouts  9.39 us (1%)
    psum x36, blocking collectives, one_axis_at_a_time(): return functools.reduce(lax.psum, axes, shard)  515 us
    ppermute x38, starting transfers between devices, padded_2(): lax.ppermute(last, axis, up)  126 us
    ppermute x38, starting transfers between devices, padded_2(): lax.ppermute(initial, axis, [(b, a) for a, b in up])  66.9 us
    ppermute x38, waiting for transfers between devices, padded_2(): lax.ppermute(last, axis, up)  29.9 us
    reduce_sum x12, other arithmetic, two_products(): jnp.sum(resid * image)  16.6 us
  transfers between devices with their start and end apart: 79, of which 16 were waited for; matrix products, arithmetic and copies ran while one was open for 1% of the time, Pallas kernels for 0%

commit v1 on v0

v1 whole, which is shorter than its diff:
```python
import math

import jax
import jax.numpy as jnp
import numpy as np
from jax import lax
from jax.experimental import pallas as pl
from jax.experimental.pallas import tpu as pltpu
from jax.sharding import PartitionSpec as P

STEPS = 3
ITERS = 3
DIFFUSION = 1.0
CENTRE, RADIUS = 8.0, 7.0
HALF = 6
TOP = 2 * HALF
MOMENTS = 2 * TOP
NODES = 128
WIDE = HALF + 1
ROWS = 8
NOISE_GAIN = 4.0
ERROR_BOUND = 4e-5

AXES = ("gx", "yz")
CHECK_AT, FIELD_AT = 32, 47
LOW_AT = 64


def chebyshev_tables():
    angle = np.pi * (np.arange(NODES) + 0.5) / NODES
    exact = np.cos(np.arange(32)[:, None] * angle[None])
    first = np.round(exact * 2048.0) / 2048.0
    second = np.round((exact - first) * 2.0**23) / 2.0**23
    parts = np.concatenate([first, second, exact - first - second, exact])
    return parts.astype(np.float32), (CENTRE + RADIUS * exact[1:2]).astype(np.float32)


def total(values):
    return jnp.sum(values, axis=1, keepdims=True)


def two_sum(a, b):
    s = a + b
    t = s - a
    return s, (a - (s - t)) + (b - t)


def plus(a, b):
    s, e = two_sum(a[0], b[0])
    return two_sum(s, e + (a[1] + b[1]))


def times(scale, a):
    return scale * a[0], scale * a[1]


def halves(values):
    wide = 4097.0 * values
    high = wide - (wide - values)
    return high, values - high


def split_sum(values, axis=None):
    count = values.size if axis is None else values.shape[axis]
    most = jnp.max(jnp.abs(values), axis=axis, keepdims=True)
    unit = (4.0 * count) * most
    high = (values + unit) - unit
    return jnp.sum(high, axis=axis, keepdims=True), jnp.sum(values - high, axis=axis, keepdims=True)


def spectral_solve(resid, weight, nodes, noise):
    direction = resid
    answer = jnp.zeros_like(resid)
    norm_now = total(weight * resid * resid)
    noise_now = noise * total(resid * resid)
    error = jnp.zeros_like(norm_now)
    for step in range(ITERS):
        image = nodes * direction
        product = total(weight * direction * image)
        length = total(weight * direction * direction)
        noise_product = noise * total(direction * image)
        alpha = norm_now / product
        error = error + alpha * (noise_now / norm_now + noise_product / product) * jnp.sqrt(length)
        answer = answer + alpha * direction
        resid = resid - alpha * image
        if step + 1 < ITERS:
            norm_next = total(weight * resid * resid)
            noise_now = noise * total(resid * resid)
            direction = resid + (norm_next / norm_now) * direction
            norm_now = norm_next
    return answer, error


def coefficients(high, low, tables, nodes):
    table = tables[96:128]
    place = lax.broadcasted_iota(jnp.int32, (32, 1), 0)
    raw = high[:32], low[:32]
    base = tuple(jnp.where(place % 2 == 0, r[0:1], r[1:2]) for r in raw)
    shifted = plus(times(2.0, raw), times(-1.0, base))
    used = place < MOMENTS
    moment = tuple(jnp.where(used, jnp.where(place < 2, r, m), 0.0) for r, m in zip(raw, shifted))
    factor = jnp.where(place == 0, 1.0 / NODES, 2.0 / NODES)
    big, small = halves(factor * moment[0])
    small = small + factor * moment[1]
    parts = big * tables[:32]
    rest = big * tables[32:64] + small * tables[:32] + (big * tables[64:96] + small * tables[32:64])
    pieces = (parts, rest)
    count = 32
    while count > 1:
        count //= 2
        pieces = plus(tuple(p[:count] for p in pieces), tuple(p[count : 2 * count] for p in pieces))
    weight = pieces[0] + pieces[1]
    worst = jnp.zeros((1, 1), jnp.float32)
    at = lambda pair, k: (pair[0][k : k + 1], pair[1][k : k + 1])
    for k in range(1, TOP):
        gap = plus(times(2.0, at((high, low), CHECK_AT + k)), times(-1.0, at(moment, 2)))
        gap = plus(gap, times(-1.0, at(moment, 2 * k)))
        worst = jnp.maximum(worst, jnp.abs(gap[0] + gap[1]))
    noise = (worst + 1e-10 * high[0:1]) * (NOISE_GAIN / NODES)
    dots = high
    above = nodes - 1.0
    one = jnp.ones_like(nodes)
    path = [jnp.zeros_like(nodes)]
    second = path[0]
    errors = [jnp.zeros((1, 1), jnp.float32), jnp.zeros((1, 1), jnp.float32)]
    for step in range(STEPS):
        change, error = spectral_solve(one - above * path[-1], weight, nodes, noise)
        path.append(path[-1] + change)
        errors[0] = errors[0] + error
    for step in range(STEPS):
        resid = one - above * second + 0.5 * above * (path[step + 1] - path[step])
        change, error = spectral_solve(resid, weight, nodes, noise)
        second = second + change
        errors[1] = errors[1] + error
    results = []
    for values, error in ((path[-1], errors[0]), (second, errors[0] + errors[1])):
        part = total(table[:16] * values) * (2.0 / NODES)
        row = lax.broadcasted_iota(jnp.int32, (16, 1), 0)
        part = jnp.where(row == 0, 0.5 * part, part)
        part = jnp.where(row < TOP, part, 0.0)
        cross = jnp.sum(part * dots[FIELD_AT + 1 : FIELD_AT + 17], axis=0, keepdims=True)
        square = dots[FIELD_AT : FIELD_AT + 1] + 2.0 * cross + total(weight * values * values)
        fine = (error * error <= ERROR_BOUND * ERROR_BOUND * square) & (error >= 0.0)
        results.append((part, fine))
    return results


def pack_rows_kernel(u, f, d, to_high, to_low):
    nx, ny, _ = u.shape
    for n, ref in enumerate((u, f, d)):
        to_high[n * nx : (n + 1) * nx] = ref[:, ny - ROWS :, :]
        to_low[n * nx : (n + 1) * nx] = ref[:, :ROWS, :]


def pack_planes_kernel(u, f, d, low, high, to_high, to_low):
    nx, ny, _ = u.shape
    at = 0
    for n, (ref, width) in enumerate(((u, WIDE), (f, HALF), (d, HALF))):
        for out, start in ((to_high, nx - width), (to_low, 0)):
            out[at : at + width, :ROWS] = low[n * nx + start : n * nx + start + width]
            out[at : at + width, ROWS : ROWS + ny] = ref[start : start + width]
            out[at : at + width, ROWS + ny :] = high[n * nx + start : n * nx + start + width]
        at += width


def pack_vector_kernel(v, low, high, to_high, to_low):
    nx, ny, _ = v.shape
    for out, start in ((to_high, nx - HALF), (to_low, 0)):
        out[:, :ROWS] = low[start : start + HALF]
        out[:, ROWS : ROWS + ny] = v[start : start + HALF]
        out[:, ROWS + ny :] = high[start : start + HALF]


def beside(ref, i):
    here = ref[i]
    lane = lax.broadcasted_iota(jnp.int32, here.shape, 1)
    last = here.shape[1] - 1
    right = jnp.where(lane == last, 0.0, pltpu.roll(here, last, 1))
    left = jnp.where(lane == 0, 0.0, pltpu.roll(here, 1, 1))
    rows = pltpu.roll(here, 1, 0) + pltpu.roll(here, here.shape[0] - 1, 0)
    return here, (ref[i + 1] + ref[i - 1]) + rows + (right + left)


def row_mask(shape, ny):
    row = lax.broadcasted_iota(jnp.int32, shape, 0)
    here, count = lax.axis_index("yz"), lax.axis_size("yz")
    low = jnp.where(here == 0, ROWS, 0)
    high = jnp.where(here == count - 1, ROWS + ny, 2 * ROWS + ny)
    return jnp.where((row >= low) & (row < high), 1.0, 0.0)


def plane_range(nx, halo):
    here, count = lax.axis_index("gx"), lax.axis_size("gx")
    return jnp.where(here == 0, WIDE, WIDE - halo), jnp.where(here == count - 1, WIDE + nx, WIDE + nx + halo)


def put(row, index, values):
    lane = lax.broadcasted_iota(jnp.int32, row.shape, 1)
    high, low = split_sum(values)
    return jnp.where(lane == index, high, jnp.where(lane == index + LOW_AT, low, row))


def own_dots(nx, loads, pairs):
    def body(i, sums):
        planes = loads(i)
        return tuple(s + planes[a] * planes[b] for s, (a, b) in zip(sums, pairs))

    shape = jax.eval_shape(loads, 0)[0].shape
    start = tuple(jnp.zeros(shape, jnp.float32) for _ in pairs)
    return lax.fori_loop(0, nx, body, start, unroll=2)


def first_kernel(u, f, d, ylow, yhigh, xlow, xhigh, basis, scale, to_high, to_low, dots, wide_u, va, vb):
    nx, ny, nz = u.shape
    high = ROWS + ny
    for n, (ref, width, dst) in enumerate(((u, WIDE, wide_u), (d, HALF, scale))):
        at = 0 if n == 0 else WIDE + HALF
        dst[WIDE - width : WIDE] = xlow[at : at + width]
        dst[WIDE + nx : WIDE + nx + width] = xhigh[at : at + width]
        src = 0 if n == 0 else 2 * nx
        dst[WIDE : WIDE + nx, :ROWS] = ylow[src : src + nx]
        dst[WIDE : WIDE + nx, ROWS:high] = ref[...]
        dst[WIDE : WIDE + nx, high:] = yhigh[src : src + nx]
    va[WIDE - HALF : WIDE] = xlow[WIDE : WIDE + HALF]
    va[WIDE + nx : WIDE + nx + HALF] = xhigh[WIDE : WIDE + HALF]
    va[WIDE : WIDE + nx, :ROWS] = ylow[nx : 2 * nx]
    va[WIDE : WIDE + nx, ROWS:high] = f[...]
    va[WIDE : WIDE + nx, high:] = yhigh[nx : 2 * nx]
    none = jnp.zeros((WIDE,) + va.shape[1:], jnp.float32)
    vb[:WIDE] = none
    vb[WIDE + nx :] = none
    va[0] = none[0]
    va[2 * WIDE + nx - 1] = none[0]
    scale[0] = none[0]
    scale[2 * WIDE + nx - 1] = none[0]
    keep = row_mask(va.shape[1:], ny)
    pull = keep * (2.0 / RADIUS * DIFFUSION)

    def start(i, _):
        here, around = beside(wide_u, i)
        damp = scale[i]
        va[i] = keep * (va[i] - (damp * here + DIFFUSION * (6.0 * here - around)))
        scale[i] = keep * ((2.0 / RADIUS) * (damp + (1.0 + 6.0 * DIFFUSION - CENTRE)))
        return 0

    lax.fori_loop(*plane_range(nx, HALF), start, 0)
    row = jnp.zeros((8, 128), jnp.float32)
    now, other = va, vb
    own = pl.ds(ROWS, ny)

    def save(k, ref):
        def body(i, _):
            basis[k, i] = ref[i + WIDE, own, :]
            return 0

        lax.fori_loop(0, nx, body, 0, unroll=4)

    save(0, va)
    s = own_dots(nx, lambda i: (u[i], va[i + WIDE, own, :]), ((0, 0), (0, 1), (1, 1)))
    for at, value in zip((FIELD_AT, FIELD_AT + 1, 0), s):
        row = put(row, at, value)
    for k in range(HALF):
        src, dst = (va, vb) if k % 2 == 0 else (vb, va)
        halo = HALF - 1 - k

        def step(i, _):
            here, around = beside(src, i)
            twice = scale[i] * here - pull * around
            dst[i] = 0.5 * twice if k == 0 else twice - dst[i]
            return 0

        lax.fori_loop(*plane_range(nx, halo), step, 0)
        save(k + 1, dst)
        loads = lambda i: (u[i], src[i + WIDE, own, :], dst[i + WIDE, own, :]) + ((basis[k - 1, i],) if k else ())
        pairs = ((0, 2), (1, 2), (2, 2)) + (((3, 2),) if k else ())
        s = own_dots(nx, loads, pairs)
        where = (FIELD_AT + 2 + k, 2 * k + 1, 2 * k + 2, CHECK_AT + k)
        for at, value in zip(where, s):
            row = put(row, at, value)
    to_high[...] = basis[HALF, :, ny - ROWS :, :]
    to_low[...] = basis[HALF, :, :ROWS, :]
    dots[...] = row


def second_kernel(u, first, scale, ylow, yhigh, xlow, xhigh, before, basis, dots, va, vb, prior):
    _, nx, ny, nz = first.shape
    high = ROWS + ny
    va[WIDE - HALF : WIDE] = xlow[...]
    va[WIDE + nx : WIDE + nx + HALF] = xhigh[...]
    va[WIDE : WIDE + nx, :ROWS] = ylow[...]
    va[WIDE : WIDE + nx, ROWS:high] = first[HALF]
    va[WIDE : WIDE + nx, high:] = yhigh[...]
    none = jnp.zeros((WIDE,) + va.shape[1:], jnp.float32)
    vb[:WIDE] = none
    vb[WIDE + nx :] = none
    keep = row_mask(va.shape[1:], ny)
    pull = keep * (2.0 / RADIUS * DIFFUSION)
    row = before[...]
    own = pl.ds(ROWS, ny)
    for j in range(HALF):
        src, dst = (va, vb) if j % 2 == 0 else (vb, va)

        def step(i, _):
            here, around = beside(src, i)
            twice = scale[i] * here - pull * around
            dst[i] = 0.5 * twice if j == 0 else twice - dst[i]
            return 0

        lax.fori_loop(*plane_range(nx, HALF - 1 - j), step, 0)
        get = lambda k, i: first[k, i] if k <= HALF else basis[k - HALF - 1, i]
        k = HALF + j

        def body(i, sums):
            new = 2.0 * dst[i + WIDE, own, :] - first[HALF - 1 - j, i]
            if j + 1 < HALF:
                basis[j, i] = new
            terms = [get(k, i) * new, get(k - 1, i) * new]
            if j + 1 < HALF:
                terms += [new * new, u[i] * new]
            return tuple(a + b for a, b in zip(sums, terms))

        count = 4 if j + 1 < HALF else 2
        sums = tuple(jnp.zeros((ny, nz), jnp.float32) for _ in range(count))
        sums = lax.fori_loop(0, nx, body, sums, unroll=2)
        where = (2 * k + 1, CHECK_AT + k, 2 * k + 2, FIELD_AT + 2 + k)
        for at, value in zip(where, sums):
            row = put(row, at, value)
    dots[...] = jnp.broadcast_to(row[0:1], dots.shape)


def finish_kernel(gathered, tables, nodes, u, first, second, out, flag):
    nx, ny, nz = u.shape
    turned = gathered[...].T
    high, low = split_sum(turned[:LOW_AT], 1)
    high, low = two_sum(high, low + total(turned[LOW_AT:]))
    (lower, fine_low), (upper, fine_up) = coefficients(high, low, tables[...], nodes[...])
    level = lax.axis_index("level")
    part = jnp.where(level == 0, lower, upper)
    flag[...] = jnp.broadcast_to(jnp.where(fine_low & fine_up, 1.0, 0.0), flag.shape)
    factors = [jnp.broadcast_to(part[k : k + 1], (8, 128)) for k in range(TOP)]

    def body(i, _):
        for r in range(0, ny, 8):
            for c in range(0, nz, 128):
                at = (i, pl.ds(r, 8), pl.ds(c, 128))
                value = u[at]
                for k in range(TOP):
                    ref, n = (first, k) if k <= HALF else (second, k - HALF - 1)
                    value = value + factors[k] * ref[(n,) + at]
                out[at] = value
        return 0

    lax.fori_loop(0, nx, body, 0)


def call(kernel, outs, args, scratch=(), limit=30 << 20):
    whole = pl.BlockSpec(memory_space=pltpu.VMEM)
    return pl.pallas_call(
        kernel,
        out_shape=[jax.ShapeDtypeStruct(s, jnp.float32) for s in outs],
        in_specs=[whole] * len(args),
        out_specs=[whole] * len(outs),
        scratch_shapes=[pltpu.VMEM(s, jnp.float32) for s in scratch],
        compiler_params=pltpu.CompilerParams(vmem_limit_bytes=limit),
        name=kernel.__name__,
    )(*args)


def both_ways(up, down, axis):
    size = lax.axis_size(axis)
    route = [(i, i + 1) for i in range(size - 1)]
    return lax.ppermute(up, axis, route), lax.ppermute(down, axis, [(b, a) for a, b in route])


def stencil(field, damping):
    low, high = both_ways(field[-1:], field[:1], "gx")
    left, right = both_ways(field[:, -1:], field[:, :1], "yz")
    tall = jnp.concatenate([low, field, high], axis=0)
    long = jnp.concatenate([left, field, right], axis=1)
    zero = jnp.zeros_like(field[:, :, :1])
    near = tall[2:] + tall[:-2] + long[:, 2:] + long[:, :-2]
    near = near + jnp.concatenate([field[:, :, 1:], zero], axis=2) + jnp.concatenate([zero, field[:, :, :-1]], axis=2)
    return damping * field + DIFFUSION * (6.0 * field - near)


def dot(a, b):
    value = jnp.sum(a * b)
    for axis in AXES:
        value = lax.psum(value, axis)
    return value


def solve(target, guess, damping):
    resid = target - (guess + stencil(guess, damping))

    def step(_, state):
        answer, resid, direction, norm_now = state
        image = direction + stencil(direction, damping)
        alpha = norm_now / dot(direction, image)
        answer = answer + alpha * direction
        resid = resid - alpha * image
        norm_next = dot(resid, resid)
        return answer, resid, resid + (norm_next / norm_now) * direction, norm_next

    return lax.fori_loop(0, ITERS, step, (guess, resid, resid, dot(resid, resid)))[0]


def step_by_step(init_field, source, damping):
    def body(_, carry):
        lower, upper = carry
        fresh = solve(lower + source, lower, damping)
        extra = 0.5 * stencil(fresh - lower, damping)
        return fresh, solve(upper + source + extra, upper, damping)

    lower, upper = lax.fori_loop(0, STEPS, body, (init_field, init_field))
    return jnp.where(lax.axis_index("level") == 1, upper, lower)


def per_device(u, f, d):
    nx, ny, nz = u.shape
    tall = 2 * ROWS + ny
    ups, downs = call(pack_rows_kernel, [(3 * nx, ROWS, nz)] * 2, (u, f, d))
    ylow, yhigh = both_ways(ups, downs, "yz")
    edge = (WIDE + 2 * HALF, tall, nz)
    ups, downs = call(pack_planes_kernel, [edge] * 2, (u, f, d, ylow, yhigh))
    xlow, xhigh = both_ways(ups, downs, "gx")
    padded = (nx + 2 * WIDE, tall, nz)
    first, scale, ups, downs, dots = call(
        first_kernel,
        [(HALF + 1, nx, ny, nz), padded, (nx, ROWS, nz), (nx, ROWS, nz), (8, 128)],
        (u, f, d, ylow, yhigh, xlow, xhigh),
        [padded] * 3,
    )
    ylow, yhigh = both_ways(ups, downs, "yz")
    ups, downs = call(pack_vector_kernel, [(HALF, tall, nz)] * 2, (first[HALF], ylow, yhigh))
    xlow, xhigh = both_ways(ups, downs, "gx")
    parts = lax.axis_size(AXES)
    second, dots = call(
        second_kernel,
        [(HALF - 1, nx, ny, nz), (parts, 128)],
        (u, first, scale, ylow, yhigh, xlow, xhigh, dots),
        [padded] * 2 + [(8, 128)],
    )
    gathered = lax.all_to_all(dots.reshape(parts, 1, 128), AXES, 0, 0).reshape(parts, 128)
    tables, nodes = chebyshev_tables()
    fast, flag = call(
        finish_kernel,
        [(nx, ny, nz), (8, 128)],
        (gathered, jnp.asarray(tables), jnp.asarray(nodes), u, first, second),
    )
    state = lax.cond(flag[0, 0] > 0.5, lambda: fast, lambda: step_by_step(u, f, d))
    return state[None]


def solution(mesh):
    placed = P("gx", "yz", None)
    return jax.shard_map(
        per_device,
        mesh=mesh,
        in_specs=(placed, placed, placed),
        out_specs=P("level", "gx", "yz", None),
        check_vma=False,
    )
```

time: 820 us -> 168 us (0.20)
  blocking collectives: 515 us -> 0 us
  starting transfers between devices: 197 us -> 40.2 us
  Pallas kernels: 0 us -> 63.4 us
  between operations: 38.5 us -> 0.93 us
  waiting for transfers between devices: 30 us -> 58 us
  other arithmetic: 26.8 us -> 0 us
    psum x36 -> x0, blocking collectives: 515 us -> none  [one_axis_at_a_time(): return functools.reduce(lax.psum, axes, shard)]
    ppermute x79 -> x8, starting transfers between devices: 197 us -> 23.1 us  [the longest x4 15.4 us: both_ways(): lax.ppermute(up, axis, route)]
    pallas_call x0 -> x6, Pallas kernels: none -> 63.4 us  [call(): pl.pallas_call(kernel, out_shape=[jax.ShapeDtypeStruct(s, jnp.float32) fo...]
    all_to_all x0 -> x1, starting transfers between devices: none -> 17.1 us  [per_device(): lax.all_to_all(dots.reshape(parts, 1, 128), AXES, 0, 0).reshape(parts, 128)]
    ppermute x79 -> x8, waiting for transfers between devices: 30 us -> 46.9 us  [the longest x4 30.3 us: both_ways(): lax.ppermute(up, axis, route)]
    reduce_sum x12 -> x0, other arithmetic: 16.6 us -> none  [two_products(): jnp.sum(resid * image)]
    all_to_all x0 -> x1, waiting for transfers between devices: none -> 11.1 us  [per_device(): lax.all_to_all(dots.reshape(parts, 1, 128), AXES, 0, 0).reshape(parts, 128)]
    sub x15 -> x0, other arithmetic: 8.33 us -> none  [the longest x8 5.18 us: solve(): resid = resid - alpha * along]
  transfers between devices with their start and end apart: 79 -> 9, of which waited for: 16 -> 9; matrix products, arithmetic and copies ran while one was open for 1% -> 0% of each run, Pallas kernels for 0% -> 0%
where the time goes in v1:
time: 168 us; the launch traced here: 167 us
  Pallas kernels  63.4 us (38%)
  waiting for transfers between devices  58 us (35%)
  starting transfers between devices  40.2 us (24%)
  local copies, waits for them, and re-layouts  4.57 us (3%)
    pallas_call x6, Pallas kernels, call(): pl.pallas_call(kernel, out_shape=[jax.ShapeDtypeStruct(s, jnp.float32) fo...  63.4 us
    ppermute x4, waiting for transfers between devices, both_ways(): lax.ppermute(up, axis, route)  30.3 us
    all_to_all x1, starting transfers between devices, per_device(): lax.all_to_all(dots.reshape(parts, 1, 128), AXES, 0, 0).reshape(parts, 128)  17.1 us
    ppermute x4, waiting for transfers between devices, both_ways(): lax.ppermute(down, axis, [(b, a) for a, b in route])  16.6 us
    ppermute x4, starting transfers between devices, both_ways(): lax.ppermute(up, axis, route)  15.4 us
    all_to_all x1, waiting for transfers between devices, per_device(): lax.all_to_all(dots.reshape(parts, 1, 128), AXES, 0, 0).reshape(parts, 128)  11.1 us
    ppermute x4, starting transfers between devices, both_ways(): lax.ppermute(down, axis, [(b, a) for a, b in route])  7.65 us
    unnamed x13, local copies, waits for them, and re-layouts  4.01 us
  transfers between devices with their start and end apart: 9, of which 9 were waited for; matrix products, arithmetic and copies ran while one was open for 0% of the time, Pallas kernels for 0%

profile of v1, /device:TPU:8, one launch (start us, length us, event | category | flops | bytes accessed | tf_op | source)
XLA Modules:
  0.0 167.3 jit_solution(5830290926945858114)
XLA Ops:
  0.0 1.9 %copy.53.u = f32[32,16,256]{2,1,0:T(8,128)} copy(f32[32,16,256]{2,1,0:T(8,128)} %param.13) | data formatting | bytes 1048576
  2.0 1.5 pack_rows_kernel.1
  3.4 3.5 %collective-permute-start.20 = (f32[96,8,256]{2,1,0:T(8,128)S(1)}, f32[96,8,256]{2,1,0:T(8,128)S(1)}, u32[]{:S(2)}, u32[]{:S(2)}) collective-permute-start(f32[96,8,256]{2,1,0:T(8,128)S(1)} %get-tuple-element.127), channel_id=1, source_target_pairs={{0,1},{1,2},{2,3},{3,4},{4,5},{5,6},{6,7},{7,8},{8,9},{9,10},{10,1... | collective-permute-start | bytes 2359304 | tf_op jit(solution)/shard_map/ppermute | solution.py:372
  6.9 2.4 %collective-permute-start.21 = (f32[96,8,256]{2,1,0:T(8,128)S(1)}, f32[96,8,256]{2,1,0:T(8,128)S(1)}, u32[]{:S(2)}, u32[]{:S(2)}) collective-permute-start(f32[96,8,256]{2,1,0:T(8,128)S(1)} %get-tuple-element.128), channel_id=1, source_target_pairs={{1,0},{2,1},{3,2},{4,3},{5,4},{6,5},{7,6},{8,7},{9,8},{10,9},{11,1... | collective-permute-start | bytes 2359304 | tf_op jit(solution)/shard_map/ppermute | solution.py:372
  9.3 15.3 %collective-permute-done.20.low.ylow = f32[96,8,256]{2,1,0:T(8,128)S(1)} collective-permute-done((f32[96,8,256]{2,1,0:T(8,128)S(1)}, f32[96,8,256]{2,1,0:T(8,128)S(1)}, u32[]{:S(2)}, u32[]{:S(2)}) %collective-permute-start.20) | collective-permute-done | bytes 786464 | tf_op jit(solution)/shard_map/ppermute | solution.py:372
  24.6 3.2 %collective-permute-done.21.high.yhigh = f32[96,8,256]{2,1,0:T(8,128)S(1)} collective-permute-done((f32[96,8,256]{2,1,0:T(8,128)S(1)}, f32[96,8,256]{2,1,0:T(8,128)S(1)}, u32[]{:S(2)}, u32[]{:S(2)}) %collective-permute-start.21) | collective-permute-done | bytes 786464 | tf_op jit(solution)/shard_map/ppermute | solution.py:372
  27.8 1.4 pack_planes_kernel.1
  29.2 3.4 %collective-permute-start.22 = (f32[19,32,256]{2,1,0:T(8,128)S(1)}, f32[19,32,256]{2,1,0:T(8,128)S(1)}, u32[]{:S(2)}, u32[]{:S(2)}) collective-permute-start(f32[19,32,256]{2,1,0:T(8,128)S(1)} %get-tuple-element.129), channel_id=1, source_target_pairs={{0,32},{32,64},{64,96},{1,33},{33,65},{65,97},{2,34},{34,66},{66,9... | collective-permute-start | bytes 1867784 | tf_op jit(solution)/shard_map/ppermute | solution.py:372
  32.7 1.3 collective-permute-start.23
  34.0 10.8 %collective-permute-done.22.xlow = f32[19,32,256]{2,1,0:T(8,128)S(1)} collective-permute-done((f32[19,32,256]{2,1,0:T(8,128)S(1)}, f32[19,32,256]{2,1,0:T(8,128)S(1)}, u32[]{:S(2)}, u32[]{:S(2)}) %collective-permute-start.22) | collective-permute-done | bytes 622624 | tf_op jit(solution)/shard_map/ppermute | solution.py:372
  44.8 4.2 %collective-permute-done.23.xhigh = f32[19,32,256]{2,1,0:T(8,128)S(1)} collective-permute-done((f32[19,32,256]{2,1,0:T(8,128)S(1)}, f32[19,32,256]{2,1,0:T(8,128)S(1)}, u32[]{:S(2)}, u32[]{:S(2)}) %collective-permute-start.23) | collective-permute-done | bytes 622624 | tf_op jit(solution)/shard_map/ppermute | solution.py:372
  48.9 0.0 copy-done.8
  48.9 0.0 copy-done.4
  48.9 30.0 %first_kernel.1 = (f32[7,32,16,256]{3,2,1,0:T(8,128)S(1)}, f32[46,32,256]{2,1,0:T(8,128)S(1)}, f32[32,8,256]{2,1,0:T(8,128)S(1)}, f32[32,8,256]{2,1,0:T(8,128)S(1)}, f32[8,128]{1,0:T(8,128)S(1)}) custom-call(f32[32,16,256]{2,1,0:T(8,128)} %copy.53.u, f32[32,16,256]{2,1,0:T(8,128)S(1)} %copy-done.8, f32[32,16,256]{2,1,0:T(8,128)S(1)} %copy-done.4, ...), custom_call_target="tpu_custom_call" | custom-call | tf_op jit(solution)/shard_map/first_kernel/pallas_call | solution.py:358
  78.9 3.2 %collective-permute-start.24 = (f32[32,8,256]{2,1,0:T(8,128)S(1)}, f32[32,8,256]{2,1,0:T(8,128)S(1)}, u32[]{:S(2)}, u32[]{:S(2)}) collective-permute-start(f32[32,8,256]{2,1,0:T(8,128)S(1)} %get-tuple-element.133), channel_id=1, source_target_pairs={{0,1},{1,2},{2,3},{3,4},{4,5},{5,6},{6,7},{7,8},{8,9},{9,10},{10,1... | collective-permute-start | bytes 786440 | tf_op jit(solution)/shard_map/ppermute | solution.py:372
  82.1 2.7 %collective-permute-start.25 = (f32[32,8,256]{2,1,0:T(8,128)S(1)}, f32[32,8,256]{2,1,0:T(8,128)S(1)}, u32[]{:S(2)}, u32[]{:S(2)}) collective-permute-start(f32[32,8,256]{2,1,0:T(8,128)S(1)} %get-tuple-element.134), channel_id=1, source_target_pairs={{1,0},{2,1},{3,2},{4,3},{5,4},{6,5},{7,6},{8,7},{9,8},{10,9},{11,1... | collective-permute-start | bytes 786440 | tf_op jit(solution)/shard_map/ppermute | solution.py:372
  84.8 0.0 copy-start.2
  84.9 0.0 copy-start.3
  84.9 2.3 %collective-permute-done.24.low.ylow = f32[32,8,256]{2,1,0:T(8,128)S(1)} collective-permute-done((f32[32,8,256]{2,1,0:T(8,128)S(1)}, f32[32,8,256]{2,1,0:T(8,128)S(1)}, u32[]{:S(2)}, u32[]{:S(2)}) %collective-permute-start.24) | collective-permute-done | bytes 262176 | tf_op jit(solution)/shard_map/ppermute | solution.py:372
  87.2 4.9 %collective-permute-done.25.high.yhigh = f32[32,8,256]{2,1,0:T(8,128)S(1)} collective-permute-done((f32[32,8,256]{2,1,0:T(8,128)S(1)}, f32[32,8,256]{2,1,0:T(8,128)S(1)}, u32[]{:S(2)}, u32[]{:S(2)}) %collective-permute-start.25) | collective-permute-done | bytes 262176 | tf_op jit(solution)/shard_map/ppermute | solution.py:372
  92.1 5.3 %collective-permute-start.26 = (f32[6,32,256]{2,1,0:T(8,128)S(1)}, f32[6,32,256]{2,1,0:T(8,128)S(1)}, u32[]{:S(2)}, u32[]{:S(2)}) collective-permute-start(f32[6,32,256]{2,1,0:T(8,128)S(1)} %get-tuple-element.135), channel_id=1, source_target_pairs={{0,32},{32,64},{64,96},{1,33},{33,65},{65,97},{2,34},{34,66},{66,9... | collective-permute-start | bytes 589832 | tf_op jit(solution)/shard_map/ppermute | solution.py:372
  97.4 1.3 collective-permute-start.27
  98.7 1.9 %collective-permute-done.26.xlow = f32[6,32,256]{2,1,0:T(8,128)S(1)} collective-permute-done((f32[6,32,256]{2,1,0:T(8,128)S(1)}, f32[6,32,256]{2,1,0:T(8,128)S(1)}, u32[]{:S(2)}, u32[]{:S(2)}) %collective-permute-start.26) | collective-permute-done | bytes 196640 | tf_op jit(solution)/shard_map/ppermute | solution.py:372
  100.6 4.4 %collective-permute-done.27.xhigh = f32[6,32,256]{2,1,0:T(8,128)S(1)} collective-permute-done((f32[6,32,256]{2,1,0:T(8,128)S(1)}, f32[6,32,256]{2,1,0:T(8,128)S(1)}, u32[]{:S(2)}, u32[]{:S(2)}) %collective-permute-start.27) | collective-permute-done | bytes 196640 | tf_op jit(solution)/shard_map/ppermute | solution.py:372
  105.0 25.9 %second_kernel.1 = (f32[5,32,16,256]{3,2,1,0:T(8,128)S(1)}, f32[128,128]{1,0:T(8,128)}) custom-call(f32[32,16,256]{2,1,0:T(8,128)} %copy.53.u, f32[7,32,16,256]{3,2,1,0:T(8,128)S(1)} %get-tuple-element.131.first, f32[46,32,256]{2,1,0:T(8,128)S(1)} %get-tuple-element.132.scale, f32[32,8,256]{2,1,0:T(8,128)S(1)} %collective-permute-done.24.low.ylow, ...), custom_call_target="tpu_custom_call" | custom-call | tf_op jit(solution)/shard_map/second_kernel/pallas_call | solution.py:358
  130.9 17.1 %all-to-all-start = ((f32[128,1,128]{2,1,0:T(1,128)}), f32[128,1,128]{2,1,0:T(1,128)S(1)}, u32[]{:S(2)}, u32[]{:S(2)}) async-start(f32[128,1,128]{2,1,0:T(1,128)} %bitcast.4), calls=%async_computation | async-start | bytes 131072 | tf_op jit(solution)/shard_map/all_to_all | solution.py:444
  148.0 11.1 %all-to-all-done = f32[128,1,128]{2,1,0:T(1,128)S(1)} async-done(((f32[128,1,128]{2,1,0:T(1,128)}), f32[128,1,128]{2,1,0:T(1,128)S(1)}, u32[]{:S(2)}, u32[]{:S(2)}) %all-to-all-start) | async-done | bytes 65568 | tf_op jit(solution)/shard_map/all_to_all | solution.py:444
  159.1 0.0 copy-done.2
  159.2 2.0 %copy-done.1 = f32[7,32,16,256]{3,2,1,0:T(8,128)S(1)} copy-done((f32[7,32,16,256]{3,2,1,0:T(8,128)S(1)}, f32[7,32,16,256]{3,2,1,0:T(8,128)}, u32[]{:S(2)}) %copy-start.1) | copy-done | bytes 3670040
  161.2 4.6 %finish_kernel.1 = (f32[32,16,256]{2,1,0:T(8,128)}, f32[8,128]{1,0:T(8,128)S(1)}) custom-call(f32[128,128]{1,0:T(8,128)S(1)} %bitcast.10, f32[128,128]{1,0:T(8,128)S(1)} %copy-done.2, f32[1,128]{1,0:T(1,128)S(1)} %copy-done.3, f32[32,16,256]{2,1,0:T(8,128)} %copy.53.u, f32[7,32,16,256]{3,2,1,0:T(8,128)S(1)} %copy-done.1, ...), custom_call_target="tpu_custom_call" | custom-call | tf_op jit(solution)/shard_map/finish_kernel/pallas_call | solution.py:358
  165.8 0.5 slice.177
  166.9 0.2 conditional.1
  (8 shorter events, 0.1 us)
Async XLA Ops:
  0.0 48.9 %copy-start.8 = (f32[32,16,256]{2,1,0:T(8,128)S(1)}, f32[32,16,256]{2,1,0:T(8,128)}, u32[]{:S(2)}) copy-start(f32[32,16,256]{2,1,0:T(8,128)} %f.5) | copy-start | bytes 1572868
  0.0 48.9 %copy-start.4 = (f32[32,16,256]{2,1,0:T(8,128)S(1)}, f32[32,16,256]{2,1,0:T(8,128)}, u32[]{:S(2)}) copy-start(f32[32,16,256]{2,1,0:T(8,128)} %d.5) | copy-start | bytes 1572868
  3.4 21.2 %collective-permute-start.20 = (f32[96,8,256]{2,1,0:T(8,128)S(1)}, f32[96,8,256]{2,1,0:T(8,128)S(1)}, u32[]{:S(2)}, u32[]{:S(2)}) collective-permute-start(f32[96,8,256]{2,1,0:T(8,128)S(1)} %get-tuple-element.127), channel_id=1, source_target_pairs={{0,1},{1,2},{2,3},{3,4},{4,5},{5,6},{6,7},{7,8},{8,9},{9,10},{10,1... | collective-permute-start | bytes 2359304 | tf_op jit(solution)/shard_map/ppermute | solution.py:372
  6.9 20.9 %collective-permute-start.21 = (f32[96,8,256]{2,1,0:T(8,128)S(1)}, f32[96,8,256]{2,1,0:T(8,128)S(1)}, u32[]{:S(2)}, u32[]{:S(2)}) collective-permute-start(f32[96,8,256]{2,1,0:T(8,128)S(1)} %get-tuple-element.128), channel_id=1, source_target_pairs={{1,0},{2,1},{3,2},{4,3},{5,4},{6,5},{7,6},{8,7},{9,8},{10,9},{11,1... | collective-permute-start | bytes 2359304 | tf_op jit(solution)/shard_map/ppermute | solution.py:372
  29.2 15.5 %collective-permute-start.22 = (f32[19,32,256]{2,1,0:T(8,128)S(1)}, f32[19,32,256]{2,1,0:T(8,128)S(1)}, u32[]{:S(2)}, u32[]{:S(2)}) collective-permute-start(f32[19,32,256]{2,1,0:T(8,128)S(1)} %get-tuple-element.129), channel_id=1, source_target_pairs={{0,32},{32,64},{64,96},{1,33},{33,65},{65,97},{2,34},{34,66},{66,9... | collective-permute-start | bytes 1867784 | tf_op jit(solution)/shard_map/ppermute | solution.py:372
  32.7 16.2 %collective-permute-start.23 = (f32[19,32,256]{2,1,0:T(8,128)S(1)}, f32[19,32,256]{2,1,0:T(8,128)S(1)}, u32[]{:S(2)}, u32[]{:S(2)}) collective-permute-start(f32[19,32,256]{2,1,0:T(8,128)S(1)} %get-tuple-element.130), channel_id=1, source_target_pairs={{32,0},{64,32},{96,64},{33,1},{65,33},{97,65},{34,2},{66,34},{98,6... | collective-permute-start | bytes 1867784 | tf_op jit(solution)/shard_map/ppermute | solution.py:372
  78.9 52.0 %copy-start = (f32[7,32,16,256]{3,2,1,0:T(8,128)}, f32[7,32,16,256]{3,2,1,0:T(8,128)S(1)}, u32[]{:S(2)}) copy-start(f32[7,32,16,256]{3,2,1,0:T(8,128)S(1)} %get-tuple-element.131.first) | copy-start | bytes 11010052
  78.9 8.3 %collective-permute-start.24 = (f32[32,8,256]{2,1,0:T(8,128)S(1)}, f32[32,8,256]{2,1,0:T(8,128)S(1)}, u32[]{:S(2)}, u32[]{:S(2)}) collective-permute-start(f32[32,8,256]{2,1,0:T(8,128)S(1)} %get-tuple-element.133), channel_id=1, source_target_pairs={{0,1},{1,2},{2,3},{3,4},{4,5},{5,6},{6,7},{7,8},{8,9},{9,10},{10,1... | collective-permute-start | bytes 786440 | tf_op jit(solution)/shard_map/ppermute | solution.py:372
  82.1 9.9 %collective-permute-start.25 = (f32[32,8,256]{2,1,0:T(8,128)S(1)}, f32[32,8,256]{2,1,0:T(8,128)S(1)}, u32[]{:S(2)}, u32[]{:S(2)}) collective-permute-start(f32[32,8,256]{2,1,0:T(8,128)S(1)} %get-tuple-element.134), channel_id=1, source_target_pairs={{1,0},{2,1},{3,2},{4,3},{5,4},{6,5},{7,6},{8,7},{9,8},{10,9},{11,1... | collective-permute-start | bytes 786440 | tf_op jit(solution)/shard_map/ppermute | solution.py:372
  84.8 74.3 %copy-start.2 = (f32[128,128]{1,0:T(8,128)S(1)}, f32[128,128]{1,0:T(8,128)}, u32[]{:S(2)}) copy-start(f32[128,128]{1,0:T(8,128)} %constant.48.clone.tables) | copy-start | bytes 196612
  84.9 74.3 %copy-start.3 = (f32[1,128]{1,0:T(1,128)S(1)}, f32[1,128]{1,0:T(1,128)}, u32[]{:S(2)}) copy-start(f32[1,128]{1,0:T(1,128)} %constant.49.clone.nodes) | copy-start | bytes 1540
  92.1 8.5 %collective-permute-start.26 = (f32[6,32,256]{2,1,0:T(8,128)S(1)}, f32[6,32,256]{2,1,0:T(8,128)S(1)}, u32[]{:S(2)}, u32[]{:S(2)}) collective-permute-start(f32[6,32,256]{2,1,0:T(8,128)S(1)} %get-tuple-element.135), channel_id=1, source_target_pairs={{0,32},{32,64},{64,96},{1,33},{33,65},{65,97},{2,34},{34,66},{66,9... | collective-permute-start | bytes 589832 | tf_op jit(solution)/shard_map/ppermute | solution.py:372
  97.4 7.6 %collective-permute-start.27 = (f32[6,32,256]{2,1,0:T(8,128)S(1)}, f32[6,32,256]{2,1,0:T(8,128)S(1)}, u32[]{:S(2)}, u32[]{:S(2)}) collective-permute-start(f32[6,32,256]{2,1,0:T(8,128)S(1)} %get-tuple-element.136), channel_id=1, source_target_pairs={{32,0},{64,32},{96,64},{33,1},{65,33},{97,65},{34,2},{66,34},{98,6... | collective-permute-start | bytes 589832 | tf_op jit(solution)/shard_map/ppermute | solution.py:372
  130.9 28.2 %all-to-all-start = ((f32[128,1,128]{2,1,0:T(1,128)}), f32[128,1,128]{2,1,0:T(1,128)S(1)}, u32[]{:S(2)}, u32[]{:S(2)}) async-start(f32[128,1,128]{2,1,0:T(1,128)} %bitcast.4), calls=%async_computation | async-start | bytes 131072 | tf_op jit(solution)/shard_map/all_to_all | solution.py:444
  159.2 2.0 %copy-start.1 = (f32[7,32,16,256]{3,2,1,0:T(8,128)S(1)}, f32[7,32,16,256]{3,2,1,0:T(8,128)}, u32[]{:S(2)}) copy-start(f32[7,32,16,256]{3,2,1,0:T(8,128)} %copy-done) | copy-start | bytes 11010052

commit v2 on v1

--- a/solution.py
+++ b/solution.py
@@ -145,11 +145,20 @@
     return results
 
 
+PAD = 8
+OWN = PAD + ROWS
+
+
+def half_of(ref, rows):
+    level = lax.axis_index("level")
+    return jnp.where(level == 0, ref[:, rows, :128], ref[:, rows, 128:])
+
+
 def pack_rows_kernel(u, f, d, to_high, to_low):
     nx, ny, _ = u.shape
     for n, ref in enumerate((u, f, d)):
-        to_high[n * nx : (n + 1) * nx] = ref[:, ny - ROWS :, :]
-        to_low[n * nx : (n + 1) * nx] = ref[:, :ROWS, :]
+        to_high[n * nx : (n + 1) * nx] = half_of(ref, slice(ny - ROWS, ny))
+        to_low[n * nx : (n + 1) * nx] = half_of(ref, slice(0, ROWS))
 
 
 def pack_planes_kernel(u, f, d, low, high, to_high, to_low):
@@ -158,40 +167,59 @@
     for n, (ref, width) in enumerate(((u, WIDE), (f, HALF), (d, HALF))):
         for out, start in ((to_high, nx - width), (to_low, 0)):
             out[at : at + width, :ROWS] = low[n * nx + start : n * nx + start + width]
-            out[at : at + width, ROWS : ROWS + ny] = ref[start : start + width]
+            out[at : at + width, ROWS : ROWS + ny] = half_of(ref.at[start : start + width], slice(0, ny))
             out[at : at + width, ROWS + ny :] = high[n * nx + start : n * nx + start + width]
         at += width
 
 
 def pack_vector_kernel(v, low, high, to_high, to_low):
-    nx, ny, _ = v.shape
+    nx, _, ny, _ = v.shape
     for out, start in ((to_high, nx - HALF), (to_low, 0)):
-        out[:, :ROWS] = low[start : start + HALF]
-        out[:, ROWS : ROWS + ny] = v[start : start + HALF]
-        out[:, ROWS + ny :] = high[start : start + HALF]
-
-
-def beside(ref, i):
-    here = ref[i]
-    lane = lax.broadcasted_iota(jnp.int32, here.shape, 1)
-    last = here.shape[1] - 1
-    right = jnp.where(lane == last, 0.0, pltpu.roll(here, last, 1))
-    left = jnp.where(lane == 0, 0.0, pltpu.roll(here, 1, 1))
-    rows = pltpu.roll(here, 1, 0) + pltpu.roll(here, here.shape[0] - 1, 0)
-    return here, (ref[i + 1] + ref[i - 1]) + rows + (right + left)
-
-
-def row_mask(shape, ny):
-    row = lax.broadcasted_iota(jnp.int32, shape, 0)
+        out[:, :, :ROWS] = low[start : start + HALF]
+        out[:, :, ROWS : ROWS + ny] = v[start : start + HALF]
+        out[:, :, ROWS + ny :] = high[start : start + HALF]
+
+
+def beside(ref, i, start, count):
+    here = [ref[i, c, start : start + count] for c in range(2)]
+    lane = lax.broadcasted_iota(jnp.int32, (count, 128), 1)
+    left = [pltpu.roll(v, 1, 1) for v in here]
+    right = [pltpu.roll(v, 127, 1) for v in here]
+    along = (
+        jnp.where(lane == 0, 0.0, left[0]) + jnp.where(lane == 127, right[1], right[0]),
+        jnp.where(lane == 0, left[0], left[1]) + jnp.where(lane == 127, 0.0, right[1]),
+    )
+    around = []
+    for c in range(2):
+        planes = ref[i + 1, c, start : start + count] + ref[i - 1, c, start : start + count]
+        rows = ref[i, c, start - 1 : start - 1 + count] + ref[i, c, start + 1 : start + 1 + count]
+        around.append((planes + rows) + along[c])
+    return here, around
+
+
+def row_mask(ny):
+    row = lax.broadcasted_iota(jnp.int32, (ny + 2 * ROWS, 128), 0)
     here, count = lax.axis_index("yz"), lax.axis_size("yz")
     low = jnp.where(here == 0, ROWS, 0)
     high = jnp.where(here == count - 1, ROWS + ny, 2 * ROWS + ny)
     return jnp.where((row >= low) & (row < high), 1.0, 0.0)
 
 
-def plane_range(nx, halo):
+def over_planes(nx, halo, body, own_body=None):
     here, count = lax.axis_index("gx"), lax.axis_size("gx")
-    return jnp.where(here == 0, WIDE, WIDE - halo), jnp.where(here == count - 1, WIDE + nx, WIDE + nx + halo)
+    below = jnp.where(here == 0, 0.0, 1.0)
+    above = jnp.where(here == count - 1, 0.0, 1.0)
+    for j in range(halo):
+        body(WIDE - halo + j, below)
+    for j in range(halo):
+        body(WIDE + nx + j, above)
+
+    def inner(i, _):
+        body(i + WIDE, None)
+        return 0
+
+    if own_body is None:
+        lax.fori_loop(0, nx, inner, 0, unroll=4)
 
 
 def put(row, index, values):
@@ -200,131 +228,172 @@
     return jnp.where(lane == index, high, jnp.where(lane == index + LOW_AT, low, row))
 
 
-def own_dots(nx, loads, pairs):
-    def body(i, sums):
-        planes = loads(i)
-        return tuple(s + planes[a] * planes[b] for s, (a, b) in zip(sums, pairs))
-
-    shape = jax.eval_shape(loads, 0)[0].shape
-    start = tuple(jnp.zeros(shape, jnp.float32) for _ in pairs)
-    return lax.fori_loop(0, nx, body, start, unroll=2)
-
-
-def first_kernel(u, f, d, ylow, yhigh, xlow, xhigh, basis, scale, to_high, to_low, dots, wide_u, va, vb):
-    nx, ny, nz = u.shape
-    high = ROWS + ny
-    for n, (ref, width, dst) in enumerate(((u, WIDE, wide_u), (d, HALF, scale))):
-        at = 0 if n == 0 else WIDE + HALF
-        dst[WIDE - width : WIDE] = xlow[at : at + width]
-        dst[WIDE + nx : WIDE + nx + width] = xhigh[at : at + width]
-        src = 0 if n == 0 else 2 * nx
-        dst[WIDE : WIDE + nx, :ROWS] = ylow[src : src + nx]
-        dst[WIDE : WIDE + nx, ROWS:high] = ref[...]
-        dst[WIDE : WIDE + nx, high:] = yhigh[src : src + nx]
-    va[WIDE - HALF : WIDE] = xlow[WIDE : WIDE + HALF]
-    va[WIDE + nx : WIDE + nx + HALF] = xhigh[WIDE : WIDE + HALF]
-    va[WIDE : WIDE + nx, :ROWS] = ylow[nx : 2 * nx]
-    va[WIDE : WIDE + nx, ROWS:high] = f[...]
-    va[WIDE : WIDE + nx, high:] = yhigh[nx : 2 * nx]
-    none = jnp.zeros((WIDE,) + va.shape[1:], jnp.float32)
-    vb[:WIDE] = none
-    vb[WIDE + nx :] = none
-    va[0] = none[0]
-    va[2 * WIDE + nx - 1] = none[0]
-    scale[0] = none[0]
-    scale[2 * WIDE + nx - 1] = none[0]
-    keep = row_mask(va.shape[1:], ny)
+def fill_edges(dst, low, high, nx):
+    width = low.shape[0]
+    dst[WIDE - width : WIDE, :, PAD:-PAD] = low
+    dst[WIDE + nx : WIDE + nx + width, :, PAD:-PAD] = high
+
+
+def clear(ref, nx, width):
+    tall = ref.shape[2]
+    side = jnp.zeros((2, PAD, 128), jnp.float32)
+    whole = jnp.zeros((2, tall, 128), jnp.float32)
+
+    def margins(i, _):
+        ref[i, :, :PAD] = side
+        ref[i, :, tall - PAD :] = side
+        return 0
+
+    lax.fori_loop(0, nx + 2 * WIDE, margins, 0)
+    for j in range(width):
+        ref[j] = whole
+        ref[WIDE + nx + (WIDE - width) + j] = whole
+
+
+def recur(src, dst, scale, pull, first_step, rows):
+    start, count = rows
+    offset = start - PAD
+    factor = pull[offset : offset + count]
+
+    def body(i, mask):
+        here, around = beside(src, i, start, count)
+        weight = factor if mask is None else factor * mask
+        made = []
+        for c in range(2):
+            at = (i, c, slice(start, start + count))
+            twice = scale[at] * here[c] - weight * around[c]
+            new = 0.5 * twice if first_step else twice - dst[at]
+            dst[at] = new
+            made.append(new)
+        return made
+
+    return body
+
+
+def first_kernel(u, f, d, *refs):
+    mine, theirs = refs[:4], refs[4:8]
+    basis, scale, to_high, to_low, wide_u, va, vb = refs[8:]
+    nx, ny, _ = u.shape
+    level = lax.axis_index("level")
+    for ref in (wide_u, va, vb):
+        clear(ref, nx, WIDE if ref is vb else 0)
+    va[0, :, PAD:-PAD] = jnp.zeros((2, ny + 2 * ROWS, 128), jnp.float32)
+    va[2 * WIDE + nx - 1, :, PAD:-PAD] = jnp.zeros((2, ny + 2 * ROWS, 128), jnp.float32)
+    at = 0
+    for n, (ref, width, dst) in enumerate(((u, WIDE, wide_u), (f, HALF, va), (d, HALF, scale))):
+        for (ylow, yhigh, xlow, xhigh), c in ((mine, level), (theirs, 1 - level)):
+            dst[WIDE - width : WIDE, c, PAD:-PAD] = xlow[at : at + width]
+            dst[WIDE + nx : WIDE + nx + width, c, PAD:-PAD] = xhigh[at : at + width]
+            dst[WIDE : WIDE + nx, c, PAD:OWN] = ylow[n * nx : (n + 1) * nx]
+            dst[WIDE : WIDE + nx, c, OWN + ny : OWN + ny + ROWS] = yhigh[n * nx : (n + 1) * nx]
+        for c in range(2):
+            dst[WIDE : WIDE + nx, c, OWN : OWN + ny] = ref[:, :, c * 128 : (c + 1) * 128]
+        at += width
+    keep = row_mask(ny)
     pull = keep * (2.0 / RADIUS * DIFFUSION)
-
-    def start(i, _):
-        here, around = beside(wide_u, i)
-        damp = scale[i]
-        va[i] = keep * (va[i] - (damp * here + DIFFUSION * (6.0 * here - around)))
-        scale[i] = keep * ((2.0 / RADIUS) * (damp + (1.0 + 6.0 * DIFFUSION - CENTRE)))
+    rows = (PAD, ny + 2 * ROWS)
+
+    def start(i, mask):
+        here, around = beside(wide_u, i, *rows)
+        inside = keep if mask is None else keep * mask
+        for c in range(2):
+            at = (i, c, slice(PAD, PAD + rows[1]))
+            damp = scale[at]
+            va[at] = inside * (va[at] - (damp * here[c] + DIFFUSION * (6.0 * here[c] - around[c])))
+            scale[at] = inside * ((2.0 / RADIUS) * (damp + (1.0 + 6.0 * DIFFUSION - CENTRE)))
+
+    over_planes(nx, HALF, start)
+
+    def save(i, _):
+        basis[0, i] = va[i + WIDE, :, OWN : OWN + ny]
         return 0
 
-    lax.fori_loop(*plane_range(nx, HALF), start, 0)
-    row = jnp.zeros((8, 128), jnp.float32)
-    now, other = va, vb
-    own = pl.ds(ROWS, ny)
-
-    def save(k, ref):
-        def body(i, _):
-            basis[k, i] = ref[i + WIDE, own, :]
-            return 0
-
-        lax.fori_loop(0, nx, body, 0, unroll=4)
-
-    save(0, va)
-    s = own_dots(nx, lambda i: (u[i], va[i + WIDE, own, :]), ((0, 0), (0, 1), (1, 1)))
-    for at, value in zip((FIELD_AT, FIELD_AT + 1, 0), s):
-        row = put(row, at, value)
+    lax.fori_loop(0, nx, save, 0, unroll=4)
     for k in range(HALF):
         src, dst = (va, vb) if k % 2 == 0 else (vb, va)
-        halo = HALF - 1 - k
-
-        def step(i, _):
-            here, around = beside(src, i)
-            twice = scale[i] * here - pull * around
-            dst[i] = 0.5 * twice if k == 0 else twice - dst[i]
-            return 0
-
-        lax.fori_loop(*plane_range(nx, halo), step, 0)
-        save(k + 1, dst)
-        loads = lambda i: (u[i], src[i + WIDE, own, :], dst[i + WIDE, own, :]) + ((basis[k - 1, i],) if k else ())
-        pairs = ((0, 2), (1, 2), (2, 2)) + (((3, 2),) if k else ())
-        s = own_dots(nx, loads, pairs)
-        where = (FIELD_AT + 2 + k, 2 * k + 1, 2 * k + 2, CHECK_AT + k)
-        for at, value in zip(where, s):
-            row = put(row, at, value)
-    to_high[...] = basis[HALF, :, ny - ROWS :, :]
-    to_low[...] = basis[HALF, :, :ROWS, :]
+        last = k == HALF - 1
+        step = recur(src, dst, scale, pull, k == 0, (OWN, ny) if last else rows)
+
+        def body(i, mask, step=step, k=k, last=last):
+            made = step(i, mask)
+            if mask is None:
+                for c in range(2):
+                    basis[k + 1, i - WIDE, c] = made[c] if last else made[c][ROWS : ROWS + ny]
+
+        over_planes(nx, HALF - 1 - k, body)
+    to_high[...] = basis[HALF, :, :, ny - ROWS :, :]
+    to_low[...] = basis[HALF, :, :, :ROWS, :]
+
+
+def first_dots_kernel(u, basis, dots):
+    count, nx, _, ny, _ = basis.shape
+    row = jnp.zeros((8, 128), jnp.float32)
+    for k in range(count):
+
+        def body(i, sums, k=k):
+            terms = [[] for _ in sums]
+            for c in range(2):
+                own = u[i, :, c * 128 : (c + 1) * 128]
+                new = basis[k, i, c]
+                parts = [own * new, new * new]
+                if k == 0:
+                    parts.append(own * own)
+                else:
+                    parts.append(basis[k - 1, i, c] * new)
+                if k > 1:
+                    parts.append(basis[k - 2, i, c] * new)
+                for t, p in zip(terms, parts):
+                    t.append(p)
+            return tuple((s[0] + t[0], s[1] + t[1]) for s, t in zip(sums, terms))
+
+        zero = jnp.zeros((ny, 128), jnp.float32)
+        sums = lax.fori_loop(0, nx, body, ((zero, zero),) * (4 if k > 1 else 3), unroll=4)
+        where = (FIELD_AT + 1 + k, 2 * k, FIELD_AT if k == 0 else 2 * k - 1, CHECK_AT + k - 1)
+        for at, (a, b) in zip(where, sums):
+            row = put(row, at, jnp.concatenate([a, b], axis=0))
     dots[...] = row
 
 
-def second_kernel(u, first, scale, ylow, yhigh, xlow, xhigh, before, basis, dots, va, vb, prior):
-    _, nx, ny, nz = first.shape
-    high = ROWS + ny
-    va[WIDE - HALF : WIDE] = xlow[...]
-    va[WIDE + nx : WIDE + nx + HALF] = xhigh[...]
-    va[WIDE : WIDE + nx, :ROWS] = ylow[...]
-    va[WIDE : WIDE + nx, ROWS:high] = first[HALF]
-    va[WIDE : WIDE + nx, high:] = yhigh[...]
-    none = jnp.zeros((WIDE,) + va.shape[1:], jnp.float32)
-    vb[:WIDE] = none
-    vb[WIDE + nx :] = none
-    keep = row_mask(va.shape[1:], ny)
-    pull = keep * (2.0 / RADIUS * DIFFUSION)
+def second_kernel(u, first, scale, ylow, yhigh, xlow, xhigh, before, basis, dots, va, vb):
+    _, nx, _, ny, _ = first.shape
+    clear(va, nx, 0)
+    clear(vb, nx, WIDE)
+    fill_edges(va, xlow[...], xhigh[...], nx)
+    va[0, :, PAD:-PAD] = jnp.zeros((2, ny + 2 * ROWS, 128), jnp.float32)
+    va[2 * WIDE + nx - 1, :, PAD:-PAD] = jnp.zeros((2, ny + 2 * ROWS, 128), jnp.float32)
+    va[WIDE : WIDE + nx, :, PAD:OWN] = ylow[...]
+    va[WIDE : WIDE + nx, :, OWN : OWN + ny] = first[HALF]
+    va[WIDE : WIDE + nx, :, OWN + ny : OWN + ny + ROWS] = yhigh[...]
+    pull = row_mask(ny) * (2.0 / RADIUS * DIFFUSION)
+    rows = (PAD, ny + 2 * ROWS)
     row = before[...]
-    own = pl.ds(ROWS, ny)
+    get = lambda k, i, c: first[k, i, c] if k <= HALF else basis[k - HALF - 1, i, c]
     for j in range(HALF):
         src, dst = (va, vb) if j % 2 == 0 else (vb, va)
-
-        def step(i, _):
-            here, around = beside(src, i)
-            twice = scale[i] * here - pull * around
-            dst[i] = 0.5 * twice if j == 0 else twice - dst[i]
-            return 0
-
-        lax.fori_loop(*plane_range(nx, HALF - 1 - j), step, 0)
-        get = lambda k, i: first[k, i] if k <= HALF else basis[k - HALF - 1, i]
+        last = j == HALF - 1
+        step = recur(src, dst, scale, pull, j == 0, (OWN, ny) if last else rows)
+        over_planes(nx, HALF - 1 - j, step, own_body=step)
         k = HALF + j
 
-        def body(i, sums):
-            new = 2.0 * dst[i + WIDE, own, :] - first[HALF - 1 - j, i]
-            if j + 1 < HALF:
-                basis[j, i] = new
-            terms = [get(k, i) * new, get(k - 1, i) * new]
-            if j + 1 < HALF:
-                terms += [new * new, u[i] * new]
-            return tuple(a + b for a, b in zip(sums, terms))
-
-        count = 4 if j + 1 < HALF else 2
-        sums = tuple(jnp.zeros((ny, nz), jnp.float32) for _ in range(count))
-        sums = lax.fori_loop(0, nx, body, sums, unroll=2)
+        def body(i, sums, step=step, j=j, k=k, last=last):
+            made = step(i + WIDE, None)
+            result = [list(s) for s in sums]
+            for c in range(2):
+                mid = made[c] if last else made[c][ROWS : ROWS + ny]
+                new = 2.0 * mid - first[HALF - 1 - j, i, c]
+                parts = [get(k, i, c) * new, get(k - 1, i, c) * new]
+                if not last:
+                    basis[j, i, c] = new
+                    parts += [new * new, u[i, :, c * 128 : (c + 1) * 128] * new]
+                for r, p in zip(result, parts):
+                    r[c] = r[c] + p
+            return tuple(tuple(r) for r in result)
+
+        zero = jnp.zeros((ny, 128), jnp.float32)
+        sums = lax.fori_loop(0, nx, body, ((zero, zero),) * (2 if last else 4), unroll=4)
         where = (2 * k + 1, CHECK_AT + k, 2 * k + 2, FIELD_AT + 2 + k)
-        for at, value in zip(where, sums):
-            row = put(row, at, value)
+        for at, (a, b) in zip(where, sums):
+            row = put(row, at, jnp.concatenate([a, b], axis=0))
     dots[...] = jnp.broadcast_to(row[0:1], dots.shape)
 
 
@@ -341,16 +410,15 @@
 
     def body(i, _):
         for r in range(0, ny, 8):
-            for c in range(0, nz, 128):
-                at = (i, pl.ds(r, 8), pl.ds(c, 128))
-                value = u[at]
+            for c in range(2):
+                value = u[i, r : r + 8, c * 128 : (c + 1) * 128]
                 for k in range(TOP):
                     ref, n = (first, k) if k <= HALF else (second, k - HALF - 1)
-                    value = value + factors[k] * ref[(n,) + at]
-                out[at] = value
+                    value = value + factors[k] * ref[n, i, c, r : r + 8]
+                out[i, r : r + 8, c * 128 : (c + 1) * 128] = value
         return 0
 
-    lax.fori_loop(0, nx, body, 0)
+    lax.fori_loop(0, nx, body, 0, unroll=2)
 
 
 def call(kernel, outs, args, scratch=(), limit=30 << 20):
@@ -419,27 +487,29 @@
 def per_device(u, f, d):
     nx, ny, nz = u.shape
     tall = 2 * ROWS + ny
-    ups, downs = call(pack_rows_kernel, [(3 * nx, ROWS, nz)] * 2, (u, f, d))
+    ups, downs = call(pack_rows_kernel, [(3 * nx, ROWS, 128)] * 2, (u, f, d))
     ylow, yhigh = both_ways(ups, downs, "yz")
-    edge = (WIDE + 2 * HALF, tall, nz)
+    edge = (WIDE + 2 * HALF, tall, 128)
     ups, downs = call(pack_planes_kernel, [edge] * 2, (u, f, d, ylow, yhigh))
-    xlow, xhigh = both_ways(ups, downs, "gx")
-    padded = (nx + 2 * WIDE, tall, nz)
-    first, scale, ups, downs, dots = call(
+    mine = (ylow, yhigh) + both_ways(ups, downs, "gx")
+    theirs = tuple(lax.ppermute(half, "level", [(0, 1), (1, 0)]) for half in mine)
+    padded = (nx + 2 * WIDE, 2, tall + 2 * PAD, 128)
+    first, scale, ups, downs = call(
         first_kernel,
-        [(HALF + 1, nx, ny, nz), padded, (nx, ROWS, nz), (nx, ROWS, nz), (8, 128)],
-        (u, f, d, ylow, yhigh, xlow, xhigh),
+        [(HALF + 1, nx, 2, ny, 128), padded, (nx, 2, ROWS, 128), (nx, 2, ROWS, 128)],
+        (u, f, d) + mine + theirs,
         [padded] * 3,
     )
     ylow, yhigh = both_ways(ups, downs, "yz")
-    ups, downs = call(pack_vector_kernel, [(HALF, tall, nz)] * 2, (first[HALF], ylow, yhigh))
+    (dots,) = call(first_dots_kernel, [(8, 128)], (u, first))
+    ups, downs = call(pack_vector_kernel, [(HALF, 2, tall, 128)] * 2, (first[HALF], ylow, yhigh))
     xlow, xhigh = both_ways(ups, downs, "gx")
     parts = lax.axis_size(AXES)
     second, dots = call(
         second_kernel,
-        [(HALF - 1, nx, ny, nz), (parts, 128)],
+        [(HALF - 1, nx, 2, ny, 128), (parts, 128)],
         (u, first, scale, ylow, yhigh, xlow, xhigh, dots),
-        [padded] * 2 + [(8, 128)],
+        [padded] * 2,
     )
     gathered = lax.all_to_all(dots.reshape(parts, 1, 128), AXES, 0, 0).reshape(parts, 128)
     tables, nodes = chebyshev_tables()

time: 168 us -> 120 us (0.71)
  Pallas kernels: 63.4 us -> 34.5 us
  waiting for transfers between devices: 58 us -> 40.8 us
    pallas_call x6 -> x7, Pallas kernels: 63.4 us -> 34.5 us  [call(): pl.pallas_call(kernel, out_shape=[jax.ShapeDtypeStruct(s, jnp.float32) fo...]
    ppermute x4, waiting for transfers between devices: 30.3 us -> 14.7 us  [both_ways(): lax.ppermute(up, axis, route)]
    ppermute x4, waiting for transfers between devices: 16.6 us -> 13.3 us  [both_ways(): lax.ppermute(down, axis, [(b, a) for a, b in route])]
    ppermute x4, starting transfers between devices: 15.4 us -> 13.5 us  [both_ways(): lax.ppermute(up, axis, route)]
    unnamed x13 -> x17, local copies, waits for them, and re-layouts: 4.01 us -> 3.2 us
  transfers between devices with their start and end apart: 9 -> 13, of which waited for: 9 -> 9; matrix products, arithmetic and copies ran while one was open for 0% -> 0% of each run, Pallas kernels for 0% -> 4%
where the time goes in v2:
time: 120 us; the launch traced here: 119 us
  waiting for transfers between devices  40.8 us (34%)
  starting transfers between devices  39 us (32%)
  Pallas kernels  34.5 us (29%)
  local copies, waits for them, and re-layouts  3.76 us (3%)
    pallas_call x7, Pallas kernels, call(): pl.pallas_call(kernel, out_shape=[jax.ShapeDtypeStruct(s, jnp.float32) fo...  34.5 us
    all_to_all x1, starting transfers between devices, per_device(): lax.all_to_all(dots.reshape(parts, 1, 128), AXES, 0, 0).reshape(parts, 128)  17.3 us
    ppermute x4, waiting for transfers between devices, both_ways(): lax.ppermute(up, axis, route)  14.7 us
    ppermute x4, starting transfers between devices, both_ways(): lax.ppermute(up, axis, route)  13.5 us
    ppermute x4, waiting for transfers between devices, both_ways(): lax.ppermute(down, axis, [(b, a) for a, b in route])  13.3 us
    all_to_all x1, waiting for transfers between devices, per_device(): lax.all_to_all(dots.reshape(parts, 1, 128), AXES, 0, 0).reshape(parts, 128)  11.1 us
    ppermute x4, starting transfers between devices, both_ways(): lax.ppermute(down, axis, [(b, a) for a, b in route])  7.63 us
    unnamed x17, local copies, waits for them, and re-layouts  3.2 us
  transfers between devices with their start and end apart: 13, of which 9 were waited for; matrix products, arithmetic and copies ran while one was open for 0% of the time, Pallas kernels for 4%

profile of v2, /device:TPU:8, one launch (start us, length us, event | category | flops | bytes accessed | tf_op | source)
XLA Modules:
  0.0 119.2 jit_solution(5629306456725303162)
XLA Ops:
  0.0 1.1 copy.53.u
  1.1 1.5 %pack_rows_kernel.1 = (f32[96,8,128]{2,1,0:T(8,128)S(1)}, f32[96,8,128]{2,1,0:T(8,128)S(1)}) custom-call(f32[32,16,256]{2,1,0:T(8,128)S(1)} %copy.53.u, f32[32,16,256]{2,1,0:T(8,128)} %f.5, f32[32,16,256]{2,1,0:T(8,128)} %d.5), custom_call_target="tpu_custom_call" | custom-call | tf_op jit(solution)/shard_map/pack_rows_kernel/pallas_call | solution.py:426
  2.6 3.5 %collective-permute-start.20 = (f32[96,8,128]{2,1,0:T(8,128)S(1)}, f32[96,8,128]{2,1,0:T(8,128)S(1)}, u32[]{:S(2)}, u32[]{:S(2)}) collective-permute-start(f32[96,8,128]{2,1,0:T(8,128)S(1)} %get-tuple-element.126), channel_id=1, source_target_pairs={{0,1},{1,2},{2,3},{3,4},{4,5},{5,6},{6,7},{7,8},{8,9},{9,10},{10,1... | collective-permute-start | bytes 1179656 | tf_op jit(solution)/shard_map/ppermute | solution.py:440
  6.1 2.4 %collective-permute-start.21 = (f32[96,8,128]{2,1,0:T(8,128)S(1)}, f32[96,8,128]{2,1,0:T(8,128)S(1)}, u32[]{:S(2)}, u32[]{:S(2)}) collective-permute-start(f32[96,8,128]{2,1,0:T(8,128)S(1)} %get-tuple-element.127), channel_id=1, source_target_pairs={{1,0},{2,1},{3,2},{4,3},{5,4},{6,5},{7,6},{8,7},{9,8},{10,9},{11,1... | collective-permute-start | bytes 1179656 | tf_op jit(solution)/shard_map/ppermute | solution.py:440
  8.5 6.9 %collective-permute-done.20.low.refs_0_ = f32[96,8,128]{2,1,0:T(8,128)S(1)} collective-permute-done((f32[96,8,128]{2,1,0:T(8,128)S(1)}, f32[96,8,128]{2,1,0:T(8,128)S(1)}, u32[]{:S(2)}, u32[]{:S(2)}) %collective-permute-start.20) | collective-permute-done | bytes 393248 | tf_op jit(solution)/shard_map/ppermute | solution.py:440
  15.4 3.2 %collective-permute-done.21.high.refs_1_ = f32[96,8,128]{2,1,0:T(8,128)S(1)} collective-permute-done((f32[96,8,128]{2,1,0:T(8,128)S(1)}, f32[96,8,128]{2,1,0:T(8,128)S(1)}, u32[]{:S(2)}, u32[]{:S(2)}) %collective-permute-start.21) | collective-permute-done | bytes 393248 | tf_op jit(solution)/shard_map/ppermute | solution.py:440
  18.6 1.3 %pack_planes_kernel.1 = (f32[19,32,128]{2,1,0:T(8,128)S(1)}, f32[19,32,128]{2,1,0:T(8,128)S(1)}) custom-call(f32[32,16,256]{2,1,0:T(8,128)S(1)} %copy.53.u, f32[32,16,256]{2,1,0:T(8,128)} %f.5, f32[32,16,256]{2,1,0:T(8,128)} %d.5, f32[96,8,128]{2,1,0:T(8,128)S(1)} %collective-permute-done.20.low.refs_0_, f32[96,8,128]{2,1,0:T(8,128)S(1)} %collective-permute-done.21.high.refs_1_), custom_call_target="tpu_custom_call" | custom-call | tf_op jit(solution)/shard_map/pack_planes_kernel/pallas_call | solution.py:426
  19.8 3.4 %collective-permute-start.22 = (f32[19,32,128]{2,1,0:T(8,128)S(1)}, f32[19,32,128]{2,1,0:T(8,128)S(1)}, u32[]{:S(2)}, u32[]{:S(2)}) collective-permute-start(f32[19,32,128]{2,1,0:T(8,128)S(1)} %get-tuple-element.128), channel_id=1, source_target_pairs={{0,32},{32,64},{64,96},{1,33},{33,65},{65,97},{2,34},{34,66},{66,9... | collective-permute-start | bytes 933896 | tf_op jit(solution)/shard_map/ppermute | solution.py:440
  23.3 1.3 %collective-permute-start.23 = (f32[19,32,128]{2,1,0:T(8,128)S(1)}, f32[19,32,128]{2,1,0:T(8,128)S(1)}, u32[]{:S(2)}, u32[]{:S(2)}) collective-permute-start(f32[19,32,128]{2,1,0:T(8,128)S(1)} %get-tuple-element.129), channel_id=1, source_target_pairs={{32,0},{64,32},{96,64},{33,1},{65,33},{97,65},{34,2},{66,34},{98,6... | collective-permute-start | bytes 933896 | tf_op jit(solution)/shard_map/ppermute | solution.py:440
  24.6 0.1 collective-permute-start.24
  24.7 0.5 collective-permute-start.25
  25.2 3.5 %collective-permute-done.22.refs_2_ = f32[19,32,128]{2,1,0:T(8,128)S(1)} collective-permute-done((f32[19,32,128]{2,1,0:T(8,128)S(1)}, f32[19,32,128]{2,1,0:T(8,128)S(1)}, u32[]{:S(2)}, u32[]{:S(2)}) %collective-permute-start.22) | collective-permute-done | bytes 311328 | tf_op jit(solution)/shard_map/ppermute | solution.py:440
  28.7 0.0 collective-permute-start.26
  28.7 4.1 %collective-permute-done.23.refs_3_ = f32[19,32,128]{2,1,0:T(8,128)S(1)} collective-permute-done((f32[19,32,128]{2,1,0:T(8,128)S(1)}, f32[19,32,128]{2,1,0:T(8,128)S(1)}, u32[]{:S(2)}, u32[]{:S(2)}) %collective-permute-start.23) | collective-permute-done | bytes 311328 | tf_op jit(solution)/shard_map/ppermute | solution.py:440
  32.8 0.0 collective-permute-start.27
  32.9 1.6 %collective-permute-done.27.refs_7_ = f32[19,32,128]{2,1,0:T(8,128)S(1)} collective-permute-done((f32[19,32,128]{2,1,0:T(8,128)S(1)}, f32[19,32,128]{2,1,0:T(8,128)S(1)}, u32[]{:S(2)}, u32[]{:S(2)}) %collective-permute-start.27) | collective-permute-done | bytes 311328 | tf_op jit(solution)/shard_map/ppermute | solution.py:495
  34.4 10.2 %first_kernel.1 = (f32[7,32,2,16,128]{4,3,2,1,0:T(8,128)S(1)}, f32[46,2,48,128]{3,2,1,0:T(8,128)S(1)}, f32[32,2,8,128]{3,2,1,0:T(8,128)S(1)}, f32[32,2,8,128]{3,2,1,0:T(8,128)S(1)}) custom-call(f32[32,16,256]{2,1,0:T(8,128)S(1)} %copy.53.u, f32[32,16,256]{2,1,0:T(8,128)S(1)} %copy-done.12, f32[32,16,256]{2,1,0:T(8,128)S(1)} %copy-done.4, ...), custom_call_target="tpu_custom_call" | custom-call | tf_op jit(solution)/shard_map/first_kernel/pallas_call | solution.py:426
  44.7 3.2 %collective-permute-start.28 = (f32[32,2,8,128]{3,2,1,0:T(8,128)S(1)}, f32[32,2,8,128]{3,2,1,0:T(8,128)S(1)}, u32[]{:S(2)}, u32[]{:S(2)}) collective-permute-start(f32[32,2,8,128]{3,2,1,0:T(8,128)S(1)} %get-tuple-element.132), channel_id=1, source_target_pairs={{0,1},{1,2},{2,3},{3,4},{4,5},{5,6},{6,7},{7,8},{8,9},{9,10},{10,1... | collective-permute-start | bytes 786440 | tf_op jit(solution)/shard_map/ppermute | solution.py:440
  47.9 2.7 %collective-permute-start.29 = (f32[32,2,8,128]{3,2,1,0:T(8,128)S(1)}, f32[32,2,8,128]{3,2,1,0:T(8,128)S(1)}, u32[]{:S(2)}, u32[]{:S(2)}) collective-permute-start(f32[32,2,8,128]{3,2,1,0:T(8,128)S(1)} %get-tuple-element.133), channel_id=1, source_target_pairs={{1,0},{2,1},{3,2},{4,3},{5,4},{6,5},{7,6},{8,7},{9,8},{10,9},{11,1... | collective-permute-start | bytes 786440 | tf_op jit(solution)/shard_map/ppermute | solution.py:440
  50.6 4.3 %collective-permute-done.28.low.ylow = f32[32,2,8,128]{3,2,1,0:T(8,128)S(1)} collective-permute-done((f32[32,2,8,128]{3,2,1,0:T(8,128)S(1)}, f32[32,2,8,128]{3,2,1,0:T(8,128)S(1)}, u32[]{:S(2)}, u32[]{:S(2)}) %collective-permute-start.28) | collective-permute-done | bytes 262176 | tf_op jit(solution)/shard_map/ppermute | solution.py:440
  54.9 4.9 %collective-permute-done.29.high.yhigh = f32[32,2,8,128]{3,2,1,0:T(8,128)S(1)} collective-permute-done((f32[32,2,8,128]{3,2,1,0:T(8,128)S(1)}, f32[32,2,8,128]{3,2,1,0:T(8,128)S(1)}, u32[]{:S(2)}, u32[]{:S(2)}) %collective-permute-start.29) | collective-permute-done | bytes 262176 | tf_op jit(solution)/shard_map/ppermute | solution.py:440
  59.8 3.4 %collective-permute-start.30 = (f32[6,2,32,128]{3,2,1,0:T(8,128)S(1)}, f32[6,2,32,128]{3,2,1,0:T(8,128)S(1)}, u32[]{:S(2)}, u32[]{:S(2)}) collective-permute-start(f32[6,2,32,128]{3,2,1,0:T(8,128)S(1)} %get-tuple-element.134), channel_id=1, source_target_pairs={{0,32},{32,64},{64,96},{1,33},{33,65},{65,97},{2,34},{34,66},{66,9... | collective-permute-start | bytes 589832 | tf_op jit(solution)/shard_map/ppermute | solution.py:440
  63.2 1.3 %collective-permute-start.31 = (f32[6,2,32,128]{3,2,1,0:T(8,128)S(1)}, f32[6,2,32,128]{3,2,1,0:T(8,128)S(1)}, u32[]{:S(2)}, u32[]{:S(2)}) collective-permute-start(f32[6,2,32,128]{3,2,1,0:T(8,128)S(1)} %get-tuple-element.135), channel_id=1, source_target_pairs={{32,0},{64,32},{96,64},{33,1},{65,33},{97,65},{34,2},{66,34},{98,6... | collective-permute-start | bytes 589832 | tf_op jit(solution)/shard_map/ppermute | solution.py:440
  64.5 5.3 %first_dots_kernel.1.before = f32[8,128]{1,0:T(8,128)S(1)} custom-call(f32[32,16,256]{2,1,0:T(8,128)S(1)} %copy.53.u, f32[7,32,2,16,128]{4,3,2,1,0:T(8,128)S(1)} %get-tuple-element.130.basis.first), custom_call_target="tpu_custom_call" | custom-call | tf_op jit(solution)/shard_map/first_dots_kernel/pallas_call | solution.py:426
  69.8 1.1 collective-permute-done.31.xhigh
  70.9 11.6 %second_kernel.1 = (f32[5,32,2,16,128]{4,3,2,1,0:T(8,128)S(1)}, f32[128,128]{1,0:T(8,128)}) custom-call(f32[32,16,256]{2,1,0:T(8,128)S(1)} %copy.53.u, f32[7,32,2,16,128]{4,3,2,1,0:T(8,128)S(1)} %get-tuple-element.130.basis.first, f32[46,2,48,128]{3,2,1,0:T(8,128)S(1)} %get-tuple-element.131.scale, f32[32,2,8,128]{3,2,1,0:T(8,128)S(1)} %collective-permute-done.28.low.ylow, ...), custom_call_target="tpu_custom_call" | custom-call | tf_op jit(solution)/shard_map/second_kernel/pallas_call | solution.py:426
  82.5 17.3 %all-to-all-start = ((f32[128,1,128]{2,1,0:T(1,128)}), f32[128,1,128]{2,1,0:T(1,128)S(1)}, u32[]{:S(2)}, u32[]{:S(2)}) async-start(f32[128,1,128]{2,1,0:T(1,128)} %bitcast.4), calls=%async_computation | async-start | bytes 131072 | tf_op jit(solution)/shard_map/all_to_all | solution.py:514
  99.8 11.1 %all-to-all-done = f32[128,1,128]{2,1,0:T(1,128)S(1)} async-done(((f32[128,1,128]{2,1,0:T(1,128)}), f32[128,1,128]{2,1,0:T(1,128)S(1)}, u32[]{:S(2)}, u32[]{:S(2)}) %all-to-all-start) | async-done | bytes 65568 | tf_op jit(solution)/shard_map/all_to_all | solution.py:514
  110.9 2.0 %copy-done.1 = f32[7,32,2,16,128]{4,3,2,1,0:T(8,128)S(1)} copy-done((f32[7,32,2,16,128]{4,3,2,1,0:T(8,128)S(1)}, f32[7,32,2,16,128]{4,3,2,1,0:T(8,128)}, u32[]{:S(2)}) %copy-start.1) | copy-done | bytes 3670040
  112.9 4.7 %finish_kernel.1 = (f32[32,16,256]{2,1,0:T(8,128)}, f32[8,128]{1,0:T(8,128)S(1)}) custom-call(f32[128,128]{1,0:T(8,128)S(1)} %bitcast.10, f32[128,128]{1,0:T(8,128)S(1)} %copy-done.2, f32[1,128]{1,0:T(1,128)S(1)} %copy-done.3, f32[32,16,256]{2,1,0:T(8,128)} %copy-done.8, f32[7,32,2,16,128]{4,3,2,1,0:T(8,128)S(1)} %copy-done.1, ...), custom_call_target="tpu_custom_call" | custom-call | tf_op jit(solution)/shard_map/finish_kernel/pallas_call | solution.py:426
  117.6 0.5 slice.177
  118.8 0.2 conditional.1
  (21 shorter events, 0.1 us)
Async XLA Ops:
  0.0 34.4 %copy-start.12 = (f32[32,16,256]{2,1,0:T(8,128)S(1)}, f32[32,16,256]{2,1,0:T(8,128)}, u32[]{:S(2)}) copy-start(f32[32,16,256]{2,1,0:T(8,128)} %f.5) | copy-start | bytes 1572868
  0.0 34.4 %copy-start.4 = (f32[32,16,256]{2,1,0:T(8,128)S(1)}, f32[32,16,256]{2,1,0:T(8,128)}, u32[]{:S(2)}) copy-start(f32[32,16,256]{2,1,0:T(8,128)} %d.5) | copy-start | bytes 1572868
  1.1 81.4 %copy-start.8 = (f32[32,16,256]{2,1,0:T(8,128)}, f32[32,16,256]{2,1,0:T(8,128)S(1)}, u32[]{:S(2)}) copy-start(f32[32,16,256]{2,1,0:T(8,128)S(1)} %copy.53.u) | copy-start | bytes 1572868
  2.6 12.7 %collective-permute-start.20 = (f32[96,8,128]{2,1,0:T(8,128)S(1)}, f32[96,8,128]{2,1,0:T(8,128)S(1)}, u32[]{:S(2)}, u32[]{:S(2)}) collective-permute-start(f32[96,8,128]{2,1,0:T(8,128)S(1)} %get-tuple-element.126), channel_id=1, source_target_pairs={{0,1},{1,2},{2,3},{3,4},{4,5},{5,6},{6,7},{7,8},{8,9},{9,10},{10,1... | collective-permute-start | bytes 1179656 | tf_op jit(solution)/shard_map/ppermute | solution.py:440
  6.1 12.5 %collective-permute-start.21 = (f32[96,8,128]{2,1,0:T(8,128)S(1)}, f32[96,8,128]{2,1,0:T(8,128)S(1)}, u32[]{:S(2)}, u32[]{:S(2)}) collective-permute-start(f32[96,8,128]{2,1,0:T(8,128)S(1)} %get-tuple-element.127), channel_id=1, source_target_pairs={{1,0},{2,1},{3,2},{4,3},{5,4},{6,5},{7,6},{8,7},{9,8},{10,9},{11,1... | collective-permute-start | bytes 1179656 | tf_op jit(solution)/shard_map/ppermute | solution.py:440
  19.8 8.9 %collective-permute-start.22 = (f32[19,32,128]{2,1,0:T(8,128)S(1)}, f32[19,32,128]{2,1,0:T(8,128)S(1)}, u32[]{:S(2)}, u32[]{:S(2)}) collective-permute-start(f32[19,32,128]{2,1,0:T(8,128)S(1)} %get-tuple-element.128), channel_id=1, source_target_pairs={{0,32},{32,64},{64,96},{1,33},{33,65},{65,97},{2,34},{34,66},{66,9... | collective-permute-start | bytes 933896 | tf_op jit(solution)/shard_map/ppermute | solution.py:440
  23.3 9.6 %collective-permute-start.23 = (f32[19,32,128]{2,1,0:T(8,128)S(1)}, f32[19,32,128]{2,1,0:T(8,128)S(1)}, u32[]{:S(2)}, u32[]{:S(2)}) collective-permute-start(f32[19,32,128]{2,1,0:T(8,128)S(1)} %get-tuple-element.129), channel_id=1, source_target_pairs={{32,0},{64,32},{96,64},{33,1},{65,33},{97,65},{34,2},{66,34},{98,6... | collective-permute-start | bytes 933896 | tf_op jit(solution)/shard_map/ppermute | solution.py:440
  24.6 8.3 %collective-permute-start.24 = (f32[96,8,128]{2,1,0:T(8,128)S(1)}, f32[96,8,128]{2,1,0:T(8,128)S(1)}, u32[]{:S(2)}, u32[]{:S(2)}) collective-permute-start(f32[96,8,128]{2,1,0:T(8,128)S(1)} %collective-permute-done.20.low.refs_0_), channel_id=1, source_target_pairs={{0,128},{128,0},{1,129},{129,1},{2,130},{130,2},{3,131},{131,3},{4... | collective-permute-start | bytes 1179656 | tf_op jit(solution)/shard_map/ppermute | solution.py:495
  24.7 8.2 %collective-permute-start.25 = (f32[96,8,128]{2,1,0:T(8,128)S(1)}, f32[96,8,128]{2,1,0:T(8,128)S(1)}, u32[]{:S(2)}, u32[]{:S(2)}) collective-permute-start(f32[96,8,128]{2,1,0:T(8,128)S(1)} %collective-permute-done.21.high.refs_1_), channel_id=1, source_target_pairs={{0,128},{128,0},{1,129},{129,1},{2,130},{130,2},{3,131},{131,3},{4... | collective-permute-start | bytes 1179656 | tf_op jit(solution)/shard_map/ppermute | solution.py:495
  28.7 4.1 %collective-permute-start.26 = (f32[19,32,128]{2,1,0:T(8,128)S(1)}, f32[19,32,128]{2,1,0:T(8,128)S(1)}, u32[]{:S(2)}, u32[]{:S(2)}) collective-permute-start(f32[19,32,128]{2,1,0:T(8,128)S(1)} %collective-permute-done.22.refs_2_), channel_id=1, source_target_pairs={{0,128},{128,0},{1,129},{129,1},{2,130},{130,2},{3,131},{131,3},{4... | collective-permute-start | bytes 933896 | tf_op jit(solution)/shard_map/ppermute | solution.py:495
  32.8 1.6 %collective-permute-start.27 = (f32[19,32,128]{2,1,0:T(8,128)S(1)}, f32[19,32,128]{2,1,0:T(8,128)S(1)}, u32[]{:S(2)}, u32[]{:S(2)}) collective-permute-start(f32[19,32,128]{2,1,0:T(8,128)S(1)} %collective-permute-done.23.refs_3_), channel_id=1, source_target_pairs={{0,128},{128,0},{1,129},{129,1},{2,130},{130,2},{3,131},{131,3},{4... | collective-permute-start | bytes 933896 | tf_op jit(solution)/shard_map/ppermute | solution.py:495
  44.6 37.9 %copy-start = (f32[7,32,2,16,128]{4,3,2,1,0:T(8,128)}, f32[7,32,2,16,128]{4,3,2,1,0:T(8,128)S(1)}, u32[]{:S(2)}) copy-start(f32[7,32,2,16,128]{4,3,2,1,0:T(8,128)S(1)} %get-tuple-element.130.basis.first) | copy-start | bytes 11010052
  44.7 10.2 %collective-permute-start.28 = (f32[32,2,8,128]{3,2,1,0:T(8,128)S(1)}, f32[32,2,8,128]{3,2,1,0:T(8,128)S(1)}, u32[]{:S(2)}, u32[]{:S(2)}) collective-permute-start(f32[32,2,8,128]{3,2,1,0:T(8,128)S(1)} %get-tuple-element.132), channel_id=1, source_target_pairs={{0,1},{1,2},{2,3},{3,4},{4,5},{5,6},{6,7},{7,8},{8,9},{9,10},{10,1... | collective-permute-start | bytes 786440 | tf_op jit(solution)/shard_map/ppermute | solution.py:440
  47.9 11.9 %collective-permute-start.29 = (f32[32,2,8,128]{3,2,1,0:T(8,128)S(1)}, f32[32,2,8,128]{3,2,1,0:T(8,128)S(1)}, u32[]{:S(2)}, u32[]{:S(2)}) collective-permute-start(f32[32,2,8,128]{3,2,1,0:T(8,128)S(1)} %get-tuple-element.133), channel_id=1, source_target_pairs={{1,0},{2,1},{3,2},{4,3},{5,4},{6,5},{7,6},{8,7},{9,8},{10,9},{11,1... | collective-permute-start | bytes 786440 | tf_op jit(solution)/shard_map/ppermute | solution.py:440
  59.8 10.0 %collective-permute-start.30 = (f32[6,2,32,128]{3,2,1,0:T(8,128)S(1)}, f32[6,2,32,128]{3,2,1,0:T(8,128)S(1)}, u32[]{:S(2)}, u32[]{:S(2)}) collective-permute-start(f32[6,2,32,128]{3,2,1,0:T(8,128)S(1)} %get-tuple-element.134), channel_id=1, source_target_pairs={{0,32},{32,64},{64,96},{1,33},{33,65},{65,97},{2,34},{34,66},{66,9... | collective-permute-start | bytes 589832 | tf_op jit(solution)/shard_map/ppermute | solution.py:440
  63.2 7.7 %collective-permute-start.31 = (f32[6,2,32,128]{3,2,1,0:T(8,128)S(1)}, f32[6,2,32,128]{3,2,1,0:T(8,128)S(1)}, u32[]{:S(2)}, u32[]{:S(2)}) collective-permute-start(f32[6,2,32,128]{3,2,1,0:T(8,128)S(1)} %get-tuple-element.135), channel_id=1, source_target_pairs={{32,0},{64,32},{96,64},{33,1},{65,33},{97,65},{34,2},{66,34},{98,6... | collective-permute-start | bytes 589832 | tf_op jit(solution)/shard_map/ppermute | solution.py:440
  70.9 40.0 %copy-start.2 = (f32[128,128]{1,0:T(8,128)S(1)}, f32[128,128]{1,0:T(8,128)}, u32[]{:S(2)}) copy-start(f32[128,128]{1,0:T(8,128)} %constant.48.clone.tables) | copy-start | bytes 196612
  70.9 40.0 %copy-start.3 = (f32[1,128]{1,0:T(1,128)S(1)}, f32[1,128]{1,0:T(1,128)}, u32[]{:S(2)}) copy-start(f32[1,128]{1,0:T(1,128)} %constant.49.clone.nodes) | copy-start | bytes 1540
  82.5 28.4 %all-to-all-start = ((f32[128,1,128]{2,1,0:T(1,128)}), f32[128,1,128]{2,1,0:T(1,128)S(1)}, u32[]{:S(2)}, u32[]{:S(2)}) async-start(f32[128,1,128]{2,1,0:T(1,128)} %bitcast.4), calls=%async_computation | async-start | bytes 131072 | tf_op jit(solution)/shard_map/all_to_all | solution.py:514
  110.9 2.0 %copy-start.1 = (f32[7,32,2,16,128]{4,3,2,1,0:T(8,128)S(1)}, f32[7,32,2,16,128]{4,3,2,1,0:T(8,128)}, u32[]{:S(2)}) copy-start(f32[7,32,2,16,128]{4,3,2,1,0:T(8,128)} %copy-done) | copy-start | bytes 11010052
  112.9 5.9 %copy-start.9 = (f32[32,16,256]{2,1,0:T(8,128)S(1)}, f32[32,16,256]{2,1,0:T(8,128)}, u32[]{:S(2)}) copy-start(f32[32,16,256]{2,1,0:T(8,128)} %copy-done.8) | copy-start | bytes 1572868

commit v3 on v2

--- a/solution.py
+++ b/solution.py
@@ -123,15 +123,19 @@
     path = [jnp.zeros_like(nodes)]
     second = path[0]
     errors = [jnp.zeros((1, 1), jnp.float32), jnp.zeros((1, 1), jnp.float32)]
-    for step in range(STEPS):
-        change, error = spectral_solve(one - above * path[-1], weight, nodes, noise)
-        path.append(path[-1] + change)
-        errors[0] = errors[0] + error
-    for step in range(STEPS):
-        resid = one - above * second + 0.5 * above * (path[step + 1] - path[step])
-        change, error = spectral_solve(resid, weight, nodes, noise)
-        second = second + change
-        errors[1] = errors[1] + error
+    for rounds in range(STEPS + 1):
+        lower = upper = one
+        if rounds < STEPS:
+            lower = one - above * path[-1]
+        if rounds > 0:
+            upper = one - above * second + 0.5 * above * (path[rounds] - path[rounds - 1])
+        change, error = spectral_solve(jnp.concatenate([lower, upper], axis=0), weight, nodes, noise)
+        if rounds > 0:
+            second = second + change[1:2]
+            errors[1] = errors[1] + error[1:2]
+        if rounds < STEPS:
+            path.append(path[-1] + change[0:1])
+            errors[0] = errors[0] + error[0:1]
     results = []
     for values, error in ((path[-1], errors[0]), (second, errors[0] + errors[1])):
         part = total(table[:16] * values) * (2.0 / NODES)
@@ -149,35 +153,43 @@
 OWN = PAD + ROWS
 
 
-def half_of(ref, rows):
-    level = lax.axis_index("level")
-    return jnp.where(level == 0, ref[:, rows, :128], ref[:, rows, 128:])
-
-
-def pack_rows_kernel(u, f, d, to_high, to_low):
+def by_level(lower, upper):
+    return jnp.where(lax.axis_index("level") == 0, lower, upper)
+
+
+def pack_rows_kernel(u, f, d, out):
     nx, ny, _ = u.shape
     for n, ref in enumerate((u, f, d)):
-        to_high[n * nx : (n + 1) * nx] = half_of(ref, slice(ny - ROWS, ny))
-        to_low[n * nx : (n + 1) * nx] = half_of(ref, slice(0, ROWS))
-
-
-def pack_planes_kernel(u, f, d, low, high, to_high, to_low):
+        for c in range(2):
+            lanes = slice(c * 128, (c + 1) * 128)
+            out[n * nx : (n + 1) * nx, c] = by_level(ref[:, ny - ROWS :, lanes], ref[:, :ROWS, lanes])
+
+
+def pack_planes_kernel(u, f, d, halo, to_high, to_low):
     nx, ny, _ = u.shape
     at = 0
     for n, (ref, width) in enumerate(((u, WIDE), (f, HALF), (d, HALF))):
         for out, start in ((to_high, nx - width), (to_low, 0)):
-            out[at : at + width, :ROWS] = low[n * nx + start : n * nx + start + width]
-            out[at : at + width, ROWS : ROWS + ny] = half_of(ref.at[start : start + width], slice(0, ny))
-            out[at : at + width, ROWS + ny :] = high[n * nx + start : n * nx + start + width]
+            for c in range(2):
+                lanes = slice(c * 128, (c + 1) * 128)
+                outer = halo[n * nx + start : n * nx + start + width, c]
+                out[at : at + width, c, :ROWS] = by_level(outer, ref[start : start + width, ny - ROWS :, lanes])
+                out[at : at + width, c, ROWS:] = by_level(ref[start : start + width, :ROWS, lanes], outer)
         at += width
 
 
-def pack_vector_kernel(v, low, high, to_high, to_low):
+def pack_vector_kernel(v, halo, to_high, to_low):
     nx, _, ny, _ = v.shape
     for out, start in ((to_high, nx - HALF), (to_low, 0)):
-        out[:, :, :ROWS] = low[start : start + HALF]
-        out[:, :, ROWS : ROWS + ny] = v[start : start + HALF]
-        out[:, :, ROWS + ny :] = high[start : start + HALF]
+        outer = halo[start : start + HALF]
+        out[:, :, :ROWS] = by_level(outer, v[start : start + HALF, :, ny - ROWS :])
+        out[:, :, ROWS:] = by_level(v[start : start + HALF, :, :ROWS], outer)
+
+
+def row_spans(level, ny):
+    halo = pl.multiple_of(PAD + level * (ROWS + ny), 8)
+    half = pl.multiple_of(PAD + level * (2 * ROWS), 8)
+    return pl.ds(halo, ROWS), pl.ds(half, 2 * ROWS)
 
 
 def beside(ref, i, start, count):
@@ -228,12 +240,6 @@
     return jnp.where(lane == index, high, jnp.where(lane == index + LOW_AT, low, row))
 
 
-def fill_edges(dst, low, high, nx):
-    width = low.shape[0]
-    dst[WIDE - width : WIDE, :, PAD:-PAD] = low
-    dst[WIDE + nx : WIDE + nx + width, :, PAD:-PAD] = high
-
-
 def clear(ref, nx, width):
     tall = ref.shape[2]
     side = jnp.zeros((2, PAD, 128), jnp.float32)
@@ -271,8 +277,8 @@
 
 
 def first_kernel(u, f, d, *refs):
-    mine, theirs = refs[:4], refs[4:8]
-    basis, scale, to_high, to_low, wide_u, va, vb = refs[8:]
+    mine, theirs = refs[:3], refs[3:6]
+    basis, scale, edge, wide_u, va, vb = refs[6:]
     nx, ny, _ = u.shape
     level = lax.axis_index("level")
     for ref in (wide_u, va, vb):
@@ -281,11 +287,11 @@
     va[2 * WIDE + nx - 1, :, PAD:-PAD] = jnp.zeros((2, ny + 2 * ROWS, 128), jnp.float32)
     at = 0
     for n, (ref, width, dst) in enumerate(((u, WIDE, wide_u), (f, HALF, va), (d, HALF, scale))):
-        for (ylow, yhigh, xlow, xhigh), c in ((mine, level), (theirs, 1 - level)):
-            dst[WIDE - width : WIDE, c, PAD:-PAD] = xlow[at : at + width]
-            dst[WIDE + nx : WIDE + nx + width, c, PAD:-PAD] = xhigh[at : at + width]
-            dst[WIDE : WIDE + nx, c, PAD:OWN] = ylow[n * nx : (n + 1) * nx]
-            dst[WIDE : WIDE + nx, c, OWN + ny : OWN + ny + ROWS] = yhigh[n * nx : (n + 1) * nx]
+        for (halo, xlow, xhigh), place in ((mine, level), (theirs, 1 - level)):
+            outer, part = row_spans(place, ny)
+            dst[WIDE - width : WIDE, :, part] = xlow[at : at + width]
+            dst[WIDE + nx : WIDE + nx + width, :, part] = xhigh[at : at + width]
+            dst[WIDE : WIDE + nx, :, outer] = halo[n * nx : (n + 1) * nx]
         for c in range(2):
             dst[WIDE : WIDE + nx, c, OWN : OWN + ny] = ref[:, :, c * 128 : (c + 1) * 128]
         at += width
@@ -321,8 +327,7 @@
                     basis[k + 1, i - WIDE, c] = made[c] if last else made[c][ROWS : ROWS + ny]
 
         over_planes(nx, HALF - 1 - k, body)
-    to_high[...] = basis[HALF, :, :, ny - ROWS :, :]
-    to_low[...] = basis[HALF, :, :, :ROWS, :]
+    edge[...] = by_level(basis[HALF, :, :, ny - ROWS :, :], basis[HALF, :, :, :ROWS, :])
 
 
 def first_dots_kernel(u, basis, dots):
@@ -354,16 +359,21 @@
     dots[...] = row
 
 
-def second_kernel(u, first, scale, ylow, yhigh, xlow, xhigh, before, basis, dots, va, vb):
+def second_kernel(u, first, scale, before, *refs):
+    mine, theirs = refs[:3], refs[3:6]
+    basis, dots, va, vb = refs[6:]
     _, nx, _, ny, _ = first.shape
     clear(va, nx, 0)
     clear(vb, nx, WIDE)
-    fill_edges(va, xlow[...], xhigh[...], nx)
     va[0, :, PAD:-PAD] = jnp.zeros((2, ny + 2 * ROWS, 128), jnp.float32)
     va[2 * WIDE + nx - 1, :, PAD:-PAD] = jnp.zeros((2, ny + 2 * ROWS, 128), jnp.float32)
-    va[WIDE : WIDE + nx, :, PAD:OWN] = ylow[...]
+    level = lax.axis_index("level")
+    for (halo, xlow, xhigh), place in ((mine, level), (theirs, 1 - level)):
+        outer, part = row_spans(place, ny)
+        va[WIDE - HALF : WIDE, :, part] = xlow[...]
+        va[WIDE + nx : WIDE + nx + HALF, :, part] = xhigh[...]
+        va[WIDE : WIDE + nx, :, outer] = halo[...]
     va[WIDE : WIDE + nx, :, OWN : OWN + ny] = first[HALF]
-    va[WIDE : WIDE + nx, :, OWN + ny : OWN + ny + ROWS] = yhigh[...]
     pull = row_mask(ny) * (2.0 / RADIUS * DIFFUSION)
     rows = (PAD, ny + 2 * ROWS)
     row = before[...]
@@ -405,7 +415,7 @@
     (lower, fine_low), (upper, fine_up) = coefficients(high, low, tables[...], nodes[...])
     level = lax.axis_index("level")
     part = jnp.where(level == 0, lower, upper)
-    flag[...] = jnp.broadcast_to(jnp.where(fine_low & fine_up, 1.0, 0.0), flag.shape)
+    flag[0, 0] = jnp.where(jnp.min(jnp.where(fine_low & fine_up, 1.0, 0.0)) > 0.5, 1, 0)
     factors = [jnp.broadcast_to(part[k : k + 1], (8, 128)) for k in range(TOP)]
 
     def body(i, _):
@@ -421,13 +431,14 @@
     lax.fori_loop(0, nx, body, 0, unroll=2)
 
 
-def call(kernel, outs, args, scratch=(), limit=30 << 20):
+def call(kernel, outs, args, scratch=(), limit=16 << 20, flags=()):
     whole = pl.BlockSpec(memory_space=pltpu.VMEM)
+    shapes = [jax.ShapeDtypeStruct(s, jnp.float32) for s in outs]
     return pl.pallas_call(
         kernel,
-        out_shape=[jax.ShapeDtypeStruct(s, jnp.float32) for s in outs],
+        out_shape=shapes + [jax.ShapeDtypeStruct(s, jnp.int32) for s in flags],
         in_specs=[whole] * len(args),
-        out_specs=[whole] * len(outs),
+        out_specs=[whole] * len(outs) + [pl.BlockSpec(memory_space=pltpu.SMEM)] * len(flags),
         scratch_shapes=[pltpu.VMEM(s, jnp.float32) for s in scratch],
         compiler_params=pltpu.CompilerParams(vmem_limit_bytes=limit),
         name=kernel.__name__,
@@ -484,41 +495,53 @@
     return jnp.where(lax.axis_index("level") == 1, upper, lower)
 
 
+def along_rows(block):
+    size = lax.axis_size("yz")
+    route = [(i, i + 1) for i in range(size - 1)] + [(size + i + 1, size + i) for i in range(size - 1)]
+    return lax.ppermute(block, ("level", "yz"), route)
+
+
+def swapped(block):
+    return lax.ppermute(block, "level", [(0, 1), (1, 0)])
+
+
 def per_device(u, f, d):
     nx, ny, nz = u.shape
     tall = 2 * ROWS + ny
-    ups, downs = call(pack_rows_kernel, [(3 * nx, ROWS, 128)] * 2, (u, f, d))
-    ylow, yhigh = both_ways(ups, downs, "yz")
-    edge = (WIDE + 2 * HALF, tall, 128)
-    ups, downs = call(pack_planes_kernel, [edge] * 2, (u, f, d, ylow, yhigh))
-    mine = (ylow, yhigh) + both_ways(ups, downs, "gx")
-    theirs = tuple(lax.ppermute(half, "level", [(0, 1), (1, 0)]) for half in mine)
+    (edge,) = call(pack_rows_kernel, [(3 * nx, 2, ROWS, 128)], (u, f, d))
+    halo = along_rows(edge)
+    planes = (WIDE + 2 * HALF, 2, 2 * ROWS, 128)
+    ups, downs = call(pack_planes_kernel, [planes] * 2, (u, f, d, halo))
+    mine = (halo,) + both_ways(ups, downs, "gx")
+    theirs = tuple(swapped(part) for part in mine)
     padded = (nx + 2 * WIDE, 2, tall + 2 * PAD, 128)
-    first, scale, ups, downs = call(
+    first, scale, edge = call(
         first_kernel,
-        [(HALF + 1, nx, 2, ny, 128), padded, (nx, 2, ROWS, 128), (nx, 2, ROWS, 128)],
+        [(HALF + 1, nx, 2, ny, 128), padded, (nx, 2, ROWS, 128)],
         (u, f, d) + mine + theirs,
         [padded] * 3,
     )
-    ylow, yhigh = both_ways(ups, downs, "yz")
+    halo = along_rows(edge)
     (dots,) = call(first_dots_kernel, [(8, 128)], (u, first))
-    ups, downs = call(pack_vector_kernel, [(HALF, 2, tall, 128)] * 2, (first[HALF], ylow, yhigh))
-    xlow, xhigh = both_ways(ups, downs, "gx")
+    ups, downs = call(pack_vector_kernel, [(HALF, 2, 2 * ROWS, 128)] * 2, (first[HALF], halo))
+    mine = (halo,) + both_ways(ups, downs, "gx")
+    theirs = tuple(swapped(part) for part in mine)
     parts = lax.axis_size(AXES)
     second, dots = call(
         second_kernel,
         [(HALF - 1, nx, 2, ny, 128), (parts, 128)],
-        (u, first, scale, ylow, yhigh, xlow, xhigh, dots),
+        (u, first, scale, dots) + mine + theirs,
         [padded] * 2,
     )
     gathered = lax.all_to_all(dots.reshape(parts, 1, 128), AXES, 0, 0).reshape(parts, 128)
     tables, nodes = chebyshev_tables()
     fast, flag = call(
         finish_kernel,
-        [(nx, ny, nz), (8, 128)],
+        [(nx, ny, nz)],
         (gathered, jnp.asarray(tables), jnp.asarray(nodes), u, first, second),
+        flags=[(1, 1)],
     )
-    state = lax.cond(flag[0, 0] > 0.5, lambda: fast, lambda: step_by_step(u, f, d))
+    state = lax.cond(flag.reshape(()), lambda: fast, lambda: step_by_step(u, f, d))
     return state[None]
 
 

time: 120 us -> 117 us (0.975)
  starting transfers between devices: 39 us -> 34.2 us
  waiting for transfers between devices: 40.8 us -> 43.5 us
  Pallas kernels: 34.5 us -> 33.3 us
    ppermute x4 -> x8, waiting for transfers between devices: 1.59 us -> 16.8 us  [the longest x2 15.2 us: along_rows(): return lax.ppermute(block, ('level', 'yz'), route)]
    ppermute x4 -> x2, waiting for transfers between devices: 14.7 us -> 7.35 us  [both_ways(): lax.ppermute(up, axis, route)]
    ppermute x4 -> x2, starting transfers between devices: 13.5 us -> 6.8 us  [both_ways(): lax.ppermute(up, axis, route)]
    ppermute x4 -> x8, starting transfers between devices: 0.59 us -> 6.99 us  [the longest x2 6.97 us: along_rows(): return lax.ppermute(block, ('level', 'yz'), route)]
    ppermute x4 -> x2, waiting for transfers between devices: 13.3 us -> 8.24 us  [both_ways(): lax.ppermute(down, axis, [(b, a) for a, b in route])]
    ppermute x4 -> x2, starting transfers between devices: 7.63 us -> 2.58 us  [both_ways(): lax.ppermute(down, axis, [(b, a) for a, b in route])]
    pallas_call x7, Pallas kernels: 34.5 us -> 33.3 us  [call(): pl.pallas_call(kernel, out_shape=shapes + [jax.ShapeDtypeStruct(s, jnp.in...]
  transfers between devices with their start and end apart: 13 -> 13, of which waited for: 9 -> 8; matrix products, arithmetic and copies ran while one was open for 0% -> 0% of each run, Pallas kernels for 4% -> 5%
where the time goes in v3:
time: 117 us; the launch traced here: 115 us
  waiting for transfers between devices  43.5 us (37%)
  starting transfers between devices  34.2 us (29%)
  Pallas kernels  33.3 us (28%)
  local copies, waits for them, and re-layouts  3.24 us (3%)
    pallas_call x7, Pallas kernels, call(): pl.pallas_call(kernel, out_shape=shapes + [jax.ShapeDtypeStruct(s, jnp.in...  33.3 us
    all_to_all x1, starting transfers between devices, per_device(): lax.all_to_all(dots.reshape(parts, 1, 128), AXES, 0, 0).reshape(parts, 128)  17.9 us
    ppermute x2, waiting for transfers between devices, along_rows(): return lax.ppermute(block, ('level', 'yz'), route)  15.2 us
    all_to_all x1, waiting for transfers between devices, per_device(): lax.all_to_all(dots.reshape(parts, 1, 128), AXES, 0, 0).reshape(parts, 128)  11.1 us
    ppermute x2, waiting for transfers between devices, both_ways(): lax.ppermute(down, axis, [(b, a) for a, b in route])  8.24 us
    ppermute x2, waiting for transfers between devices, both_ways(): lax.ppermute(up, axis, route)  7.35 us
    ppermute x2, starting transfers between devices, along_rows(): return lax.ppermute(block, ('level', 'yz'), route)  6.97 us
    ppermute x2, starting transfers between devices, both_ways(): lax.ppermute(up, axis, route)  6.8 us
  transfers between devices with their start and end apart: 13, of which 8 were waited for; matrix products, arithmetic and copies ran while one was open for 0% of the time, Pallas kernels for 5%

profile of v3, /device:TPU:8, one launch (start us, length us, event | category | flops | bytes accessed | tf_op | source)
XLA Modules:
  0.0 115.4 jit_solution(13547233882436491161)
XLA Ops:
  0.0 1.1 copy.53.u
  1.1 1.5 %pack_rows_kernel.1 = f32[96,2,8,128]{3,2,1,0:T(8,128)S(1)} custom-call(f32[32,16,256]{2,1,0:T(8,128)S(1)} %copy.53.u, f32[32,16,256]{2,1,0:T(8,128)} %f.5, f32[32,16,256]{2,1,0:T(8,128)} %d.5), custom_call_target="tpu_custom_call" | custom-call | tf_op jit(solution)/shard_map/pack_rows_kernel/pallas_call | solution.py:437
  2.6 3.5 %collective-permute-start.20 = (f32[96,2,8,128]{3,2,1,0:T(8,128)S(1)}, f32[96,2,8,128]{3,2,1,0:T(8,128)S(1)}, u32[]{:S(2)}, u32[]{:S(2)}) collective-permute-start(f32[96,2,8,128]{3,2,1,0:T(8,128)S(1)} %pack_rows_kernel.1), channel_id=1, source_target_pairs={{0,1},{1,2},{2,3},{3,4},{4,5},{5,6},{6,7},{7,8},{8,9},{9,10},{10,1... | collective-permute-start | bytes 2359304 | tf_op jit(solution)/shard_map/ppermute | solution.py:501
  6.1 10.4 %collective-permute-done.20.halo.refs_0_ = f32[96,2,8,128]{3,2,1,0:T(8,128)S(1)} collective-permute-done((f32[96,2,8,128]{3,2,1,0:T(8,128)S(1)}, f32[96,2,8,128]{3,2,1,0:T(8,128)S(1)}, u32[]{:S(2)}, u32[]{:S(2)}) %collective-permute-start.20) | collective-permute-done | bytes 786464 | tf_op jit(solution)/shard_map/ppermute | solution.py:501
  16.5 0.1 pack_planes_kernel.1
  16.6 3.4 %collective-permute-start.21 = (f32[19,2,16,128]{3,2,1,0:T(8,128)S(1)}, f32[19,2,16,128]{3,2,1,0:T(8,128)S(1)}, u32[]{:S(2)}, u32[]{:S(2)}) collective-permute-start(f32[19,2,16,128]{3,2,1,0:T(8,128)S(1)} %get-tuple-element.123), channel_id=1, source_target_pairs={{0,32},{32,64},{64,96},{1,33},{33,65},{65,97},{2,34},{34,66},{66,9... | collective-permute-start | bytes 933896 | tf_op jit(solution)/shard_map/ppermute | solution.py:451
  20.0 1.3 %collective-permute-start.22 = (f32[19,2,16,128]{3,2,1,0:T(8,128)S(1)}, f32[19,2,16,128]{3,2,1,0:T(8,128)S(1)}, u32[]{:S(2)}, u32[]{:S(2)}) collective-permute-start(f32[19,2,16,128]{3,2,1,0:T(8,128)S(1)} %get-tuple-element.124), channel_id=1, source_target_pairs={{32,0},{64,32},{96,64},{33,1},{65,33},{97,65},{34,2},{66,34},{98,6... | collective-permute-start | bytes 933896 | tf_op jit(solution)/shard_map/ppermute | solution.py:451
  21.3 5.9 %collective-permute-done.21.refs_1_ = f32[19,2,16,128]{3,2,1,0:T(8,128)S(1)} collective-permute-done((f32[19,2,16,128]{3,2,1,0:T(8,128)S(1)}, f32[19,2,16,128]{3,2,1,0:T(8,128)S(1)}, u32[]{:S(2)}, u32[]{:S(2)}) %collective-permute-start.21) | collective-permute-done | bytes 311328 | tf_op jit(solution)/shard_map/ppermute | solution.py:451
  27.2 0.0 collective-permute-start.24
  27.2 4.1 %collective-permute-done.22.refs_2_ = f32[19,2,16,128]{3,2,1,0:T(8,128)S(1)} collective-permute-done((f32[19,2,16,128]{3,2,1,0:T(8,128)S(1)}, f32[19,2,16,128]{3,2,1,0:T(8,128)S(1)}, u32[]{:S(2)}, u32[]{:S(2)}) %collective-permute-start.22) | collective-permute-done | bytes 311328 | tf_op jit(solution)/shard_map/ppermute | solution.py:451
  31.4 0.0 collective-permute-start.25
  31.4 0.0 collective-permute-done.24.refs_4_
  31.4 1.6 %collective-permute-done.25.refs_5_ = f32[19,2,16,128]{3,2,1,0:T(8,128)S(1)} collective-permute-done((f32[19,2,16,128]{3,2,1,0:T(8,128)S(1)}, f32[19,2,16,128]{3,2,1,0:T(8,128)S(1)}, u32[]{:S(2)}, u32[]{:S(2)}) %collective-permute-start.25) | collective-permute-done | bytes 311328 | tf_op jit(solution)/shard_map/ppermute | solution.py:505
  33.0 0.0 collective-permute-done.23.refs_3_
  33.0 10.1 %first_kernel.1 = (f32[7,32,2,16,128]{4,3,2,1,0:T(8,128)S(1)}, f32[46,2,48,128]{3,2,1,0:T(8,128)S(1)}, f32[32,2,8,128]{3,2,1,0:T(8,128)S(1)}) custom-call(f32[32,16,256]{2,1,0:T(8,128)S(1)} %copy.53.u, f32[32,16,256]{2,1,0:T(8,128)S(1)} %copy-done.12, f32[32,16,256]{2,1,0:T(8,128)S(1)} %copy-done.4, ...), custom_call_target="tpu_custom_call" | custom-call | tf_op jit(solution)/shard_map/first_kernel/pallas_call | solution.py:437
  43.2 3.5 %collective-permute-start.26 = (f32[32,2,8,128]{3,2,1,0:T(8,128)S(1)}, f32[32,2,8,128]{3,2,1,0:T(8,128)S(1)}, u32[]{:S(2)}, u32[]{:S(2)}) collective-permute-start(f32[32,2,8,128]{3,2,1,0:T(8,128)S(1)} %get-tuple-element.127), channel_id=1, source_target_pairs={{0,1},{1,2},{2,3},{3,4},{4,5},{5,6},{6,7},{7,8},{8,9},{9,10},{10,1... | collective-permute-start | bytes 786440 | tf_op jit(solution)/shard_map/ppermute | solution.py:501
  46.6 4.8 %collective-permute-done.26.halo.refs_0_ = f32[32,2,8,128]{3,2,1,0:T(8,128)S(1)} collective-permute-done((f32[32,2,8,128]{3,2,1,0:T(8,128)S(1)}, f32[32,2,8,128]{3,2,1,0:T(8,128)S(1)}, u32[]{:S(2)}, u32[]{:S(2)}) %collective-permute-start.26) | collective-permute-done | bytes 262176 | tf_op jit(solution)/shard_map/ppermute | solution.py:501
  51.4 0.0 collective-permute-start.29
  51.5 3.4 %collective-permute-start.27 = (f32[6,2,16,128]{3,2,1,0:T(8,128)S(1)}, f32[6,2,16,128]{3,2,1,0:T(8,128)S(1)}, u32[]{:S(2)}, u32[]{:S(2)}) collective-permute-start(f32[6,2,16,128]{3,2,1,0:T(8,128)S(1)} %get-tuple-element.128), channel_id=1, source_target_pairs={{0,32},{32,64},{64,96},{1,33},{33,65},{65,97},{2,34},{34,66},{66,9... | collective-permute-start | bytes 294920 | tf_op jit(solution)/shard_map/ppermute | solution.py:451
  54.9 1.3 %collective-permute-start.28 = (f32[6,2,16,128]{3,2,1,0:T(8,128)S(1)}, f32[6,2,16,128]{3,2,1,0:T(8,128)S(1)}, u32[]{:S(2)}, u32[]{:S(2)}) collective-permute-start(f32[6,2,16,128]{3,2,1,0:T(8,128)S(1)} %get-tuple-element.129), channel_id=1, source_target_pairs={{32,0},{64,32},{96,64},{33,1},{65,33},{97,65},{34,2},{66,34},{98,6... | collective-permute-start | bytes 294920 | tf_op jit(solution)/shard_map/ppermute | solution.py:451
  56.2 1.4 %collective-permute-done.27.refs_1_ = f32[6,2,16,128]{3,2,1,0:T(8,128)S(1)} collective-permute-done((f32[6,2,16,128]{3,2,1,0:T(8,128)S(1)}, f32[6,2,16,128]{3,2,1,0:T(8,128)S(1)}, u32[]{:S(2)}, u32[]{:S(2)}) %collective-permute-start.27) | collective-permute-done | bytes 98336 | tf_op jit(solution)/shard_map/ppermute | solution.py:451
  57.6 4.1 %collective-permute-done.28.refs_2_ = f32[6,2,16,128]{3,2,1,0:T(8,128)S(1)} collective-permute-done((f32[6,2,16,128]{3,2,1,0:T(8,128)S(1)}, f32[6,2,16,128]{3,2,1,0:T(8,128)S(1)}, u32[]{:S(2)}, u32[]{:S(2)}) %collective-permute-start.28) | collective-permute-done | bytes 98336 | tf_op jit(solution)/shard_map/ppermute | solution.py:451
  61.7 5.2 %first_dots_kernel.1.before = f32[8,128]{1,0:T(8,128)S(1)} custom-call(f32[32,16,256]{2,1,0:T(8,128)S(1)} %copy.53.u, f32[7,32,2,16,128]{4,3,2,1,0:T(8,128)S(1)} %get-tuple-element.125.basis.first), custom_call_target="tpu_custom_call" | custom-call | tf_op jit(solution)/shard_map/first_dots_kernel/pallas_call | solution.py:437
  67.0 0.0 collective-permute-done.29.refs_3_
  67.0 0.0 copy-start.2
  67.0 0.0 copy-start.3
  67.0 11.7 %second_kernel.1 = (f32[5,32,2,16,128]{4,3,2,1,0:T(8,128)S(1)}, f32[128,128]{1,0:T(8,128)}) custom-call(f32[32,16,256]{2,1,0:T(8,128)S(1)} %copy.53.u, f32[7,32,2,16,128]{4,3,2,1,0:T(8,128)S(1)} %get-tuple-element.125.basis.first, f32[46,2,48,128]{3,2,1,0:T(8,128)S(1)} %get-tuple-element.126.scale, f32[8,128]{1,0:T(8,128)S(1)} %first_dots_kernel.1.before, ...), custom_call_target="tpu_custom_call" | custom-call | tf_op jit(solution)/shard_map/second_kernel/pallas_call | solution.py:437
  78.7 17.9 %all-to-all-start = ((f32[128,1,128]{2,1,0:T(1,128)}), f32[128,1,128]{2,1,0:T(1,128)S(1)}, u32[]{:S(2)}, u32[]{:S(2)}) async-start(f32[128,1,128]{2,1,0:T(1,128)} %bitcast.4), calls=%async_computation | async-start | bytes 131072 | tf_op jit(solution)/shard_map/all_to_all | solution.py:536
  96.6 11.1 %all-to-all-done = f32[128,1,128]{2,1,0:T(1,128)S(1)} async-done(((f32[128,1,128]{2,1,0:T(1,128)}), f32[128,1,128]{2,1,0:T(1,128)S(1)}, u32[]{:S(2)}, u32[]{:S(2)}) %all-to-all-start) | async-done | bytes 65568 | tf_op jit(solution)/shard_map/all_to_all | solution.py:536
  107.7 2.0 %copy-done.1 = f32[7,32,2,16,128]{4,3,2,1,0:T(8,128)S(1)} copy-done((f32[7,32,2,16,128]{4,3,2,1,0:T(8,128)S(1)}, f32[7,32,2,16,128]{4,3,2,1,0:T(8,128)}, u32[]{:S(2)}) %copy-start.1) | copy-done | bytes 3670040
  109.7 4.6 %finish_kernel.1 = (f32[32,16,256]{2,1,0:T(8,128)}, s32[1,1]{1,0:T(1,128)}) custom-call(f32[128,128]{1,0:T(8,128)S(1)} %bitcast.10, f32[128,128]{1,0:T(8,128)S(1)} %copy-done.2, f32[1,128]{1,0:T(1,128)S(1)} %copy-done.3, f32[32,16,256]{2,1,0:T(8,128)} %copy-done.8, f32[7,32,2,16,128]{4,3,2,1,0:T(8,128)S(1)} %copy-done.1, ...), custom_call_target="tpu_custom_call" | custom-call | tf_op jit(solution)/shard_map/finish_kernel/pallas_call | solution.py:437
  115.1 0.2 conditional.1
  (20 shorter events, 0.1 us)
Async XLA Ops:
  0.0 16.5 %copy-start.12 = (f32[32,16,256]{2,1,0:T(8,128)S(1)}, f32[32,16,256]{2,1,0:T(8,128)}, u32[]{:S(2)}) copy-start(f32[32,16,256]{2,1,0:T(8,128)} %f.5) | copy-start | bytes 1572868
  0.0 16.5 %copy-start.4 = (f32[32,16,256]{2,1,0:T(8,128)S(1)}, f32[32,16,256]{2,1,0:T(8,128)}, u32[]{:S(2)}) copy-start(f32[32,16,256]{2,1,0:T(8,128)} %d.5) | copy-start | bytes 1572868
  1.1 77.6 %copy-start.8 = (f32[32,16,256]{2,1,0:T(8,128)}, f32[32,16,256]{2,1,0:T(8,128)S(1)}, u32[]{:S(2)}) copy-start(f32[32,16,256]{2,1,0:T(8,128)S(1)} %copy.53.u) | copy-start | bytes 1572868
  2.6 13.9 %collective-permute-start.20 = (f32[96,2,8,128]{3,2,1,0:T(8,128)S(1)}, f32[96,2,8,128]{3,2,1,0:T(8,128)S(1)}, u32[]{:S(2)}, u32[]{:S(2)}) collective-permute-start(f32[96,2,8,128]{3,2,1,0:T(8,128)S(1)} %pack_rows_kernel.1), channel_id=1, source_target_pairs={{0,1},{1,2},{2,3},{3,4},{4,5},{5,6},{6,7},{7,8},{8,9},{9,10},{10,1... | collective-permute-start | bytes 2359304 | tf_op jit(solution)/shard_map/ppermute | solution.py:501
  16.5 16.5 %collective-permute-start.23 = (f32[96,2,8,128]{3,2,1,0:T(8,128)S(1)}, f32[96,2,8,128]{3,2,1,0:T(8,128)S(1)}, u32[]{:S(2)}, u32[]{:S(2)}) collective-permute-start(f32[96,2,8,128]{3,2,1,0:T(8,128)S(1)} %collective-permute-done.20.halo.refs_0_), channel_id=1, source_target_pairs={{0,128},{128,0},{1,129},{129,1},{2,130},{130,2},{3,131},{131,3},{4... | collective-permute-start | bytes 2359304 | tf_op jit(solution)/shard_map/ppermute | solution.py:505
  16.6 10.7 %collective-permute-start.21 = (f32[19,2,16,128]{3,2,1,0:T(8,128)S(1)}, f32[19,2,16,128]{3,2,1,0:T(8,128)S(1)}, u32[]{:S(2)}, u32[]{:S(2)}) collective-permute-start(f32[19,2,16,128]{3,2,1,0:T(8,128)S(1)} %get-tuple-element.123), channel_id=1, source_target_pairs={{0,32},{32,64},{64,96},{1,33},{33,65},{65,97},{2,34},{34,66},{66,9... | collective-permute-start | bytes 933896 | tf_op jit(solution)/shard_map/ppermute | solution.py:451
  20.0 11.4 %collective-permute-start.22 = (f32[19,2,16,128]{3,2,1,0:T(8,128)S(1)}, f32[19,2,16,128]{3,2,1,0:T(8,128)S(1)}, u32[]{:S(2)}, u32[]{:S(2)}) collective-permute-start(f32[19,2,16,128]{3,2,1,0:T(8,128)S(1)} %get-tuple-element.124), channel_id=1, source_target_pairs={{32,0},{64,32},{96,64},{33,1},{65,33},{97,65},{34,2},{66,34},{98,6... | collective-permute-start | bytes 933896 | tf_op jit(solution)/shard_map/ppermute | solution.py:451
  27.2 4.1 %collective-permute-start.24 = (f32[19,2,16,128]{3,2,1,0:T(8,128)S(1)}, f32[19,2,16,128]{3,2,1,0:T(8,128)S(1)}, u32[]{:S(2)}, u32[]{:S(2)}) collective-permute-start(f32[19,2,16,128]{3,2,1,0:T(8,128)S(1)} %collective-permute-done.21.refs_1_), channel_id=1, source_target_pairs={{0,128},{128,0},{1,129},{129,1},{2,130},{130,2},{3,131},{131,3},{4... | collective-permute-start | bytes 933896 | tf_op jit(solution)/shard_map/ppermute | solution.py:505
  31.4 1.6 %collective-permute-start.25 = (f32[19,2,16,128]{3,2,1,0:T(8,128)S(1)}, f32[19,2,16,128]{3,2,1,0:T(8,128)S(1)}, u32[]{:S(2)}, u32[]{:S(2)}) collective-permute-start(f32[19,2,16,128]{3,2,1,0:T(8,128)S(1)} %collective-permute-done.22.refs_2_), channel_id=1, source_target_pairs={{0,128},{128,0},{1,129},{129,1},{2,130},{130,2},{3,131},{131,3},{4... | collective-permute-start | bytes 933896 | tf_op jit(solution)/shard_map/ppermute | solution.py:505
  43.1 35.6 %copy-start = (f32[7,32,2,16,128]{4,3,2,1,0:T(8,128)}, f32[7,32,2,16,128]{4,3,2,1,0:T(8,128)S(1)}, u32[]{:S(2)}) copy-start(f32[7,32,2,16,128]{4,3,2,1,0:T(8,128)S(1)} %get-tuple-element.125.basis.first) | copy-start | bytes 11010052
  43.2 8.3 %collective-permute-start.26 = (f32[32,2,8,128]{3,2,1,0:T(8,128)S(1)}, f32[32,2,8,128]{3,2,1,0:T(8,128)S(1)}, u32[]{:S(2)}, u32[]{:S(2)}) collective-permute-start(f32[32,2,8,128]{3,2,1,0:T(8,128)S(1)} %get-tuple-element.127), channel_id=1, source_target_pairs={{0,1},{1,2},{2,3},{3,4},{4,5},{5,6},{6,7},{7,8},{8,9},{9,10},{10,1... | collective-permute-start | bytes 786440 | tf_op jit(solution)/shard_map/ppermute | solution.py:501
  51.4 15.6 %collective-permute-start.29 = (f32[32,2,8,128]{3,2,1,0:T(8,128)S(1)}, f32[32,2,8,128]{3,2,1,0:T(8,128)S(1)}, u32[]{:S(2)}, u32[]{:S(2)}) collective-permute-start(f32[32,2,8,128]{3,2,1,0:T(8,128)S(1)} %collective-permute-done.26.halo.refs_0_), channel_id=1, source_target_pairs={{0,128},{128,0},{1,129},{129,1},{2,130},{130,2},{3,131},{131,3},{4... | collective-permute-start | bytes 786440 | tf_op jit(solution)/shard_map/ppermute | solution.py:505
  51.5 6.1 %collective-permute-start.27 = (f32[6,2,16,128]{3,2,1,0:T(8,128)S(1)}, f32[6,2,16,128]{3,2,1,0:T(8,128)S(1)}, u32[]{:S(2)}, u32[]{:S(2)}) collective-permute-start(f32[6,2,16,128]{3,2,1,0:T(8,128)S(1)} %get-tuple-element.128), channel_id=1, source_target_pairs={{0,32},{32,64},{64,96},{1,33},{33,65},{65,97},{2,34},{34,66},{66,9... | collective-permute-start | bytes 294920 | tf_op jit(solution)/shard_map/ppermute | solution.py:451
  54.9 6.8 %collective-permute-start.28 = (f32[6,2,16,128]{3,2,1,0:T(8,128)S(1)}, f32[6,2,16,128]{3,2,1,0:T(8,128)S(1)}, u32[]{:S(2)}, u32[]{:S(2)}) collective-permute-start(f32[6,2,16,128]{3,2,1,0:T(8,128)S(1)} %get-tuple-element.129), channel_id=1, source_target_pairs={{32,0},{64,32},{96,64},{33,1},{65,33},{97,65},{34,2},{66,34},{98,6... | collective-permute-start | bytes 294920 | tf_op jit(solution)/shard_map/ppermute | solution.py:451
  57.6 9.4 %collective-permute-start.30 = (f32[6,2,16,128]{3,2,1,0:T(8,128)S(1)}, f32[6,2,16,128]{3,2,1,0:T(8,128)S(1)}, u32[]{:S(2)}, u32[]{:S(2)}) collective-permute-start(f32[6,2,16,128]{3,2,1,0:T(8,128)S(1)} %collective-permute-done.27.refs_1_), channel_id=1, source_target_pairs={{0,128},{128,0},{1,129},{129,1},{2,130},{130,2},{3,131},{131,3},{4... | collective-permute-start | bytes 294920 | tf_op jit(solution)/shard_map/ppermute | solution.py:505
  61.7 5.3 %collective-permute-start.31 = (f32[6,2,16,128]{3,2,1,0:T(8,128)S(1)}, f32[6,2,16,128]{3,2,1,0:T(8,128)S(1)}, u32[]{:S(2)}, u32[]{:S(2)}) collective-permute-start(f32[6,2,16,128]{3,2,1,0:T(8,128)S(1)} %collective-permute-done.28.refs_2_), channel_id=1, source_target_pairs={{0,128},{128,0},{1,129},{129,1},{2,130},{130,2},{3,131},{131,3},{4... | collective-permute-start | bytes 294920 | tf_op jit(solution)/shard_map/ppermute | solution.py:505
  67.0 40.7 %copy-start.2 = (f32[128,128]{1,0:T(8,128)S(1)}, f32[128,128]{1,0:T(8,128)}, u32[]{:S(2)}) copy-start(f32[128,128]{1,0:T(8,128)} %constant.48.clone.tables) | copy-start | bytes 196612
  67.0 40.7 %copy-start.3 = (f32[1,128]{1,0:T(1,128)S(1)}, f32[1,128]{1,0:T(1,128)}, u32[]{:S(2)}) copy-start(f32[1,128]{1,0:T(1,128)} %constant.49.clone.nodes) | copy-start | bytes 1540
  78.7 29.0 %all-to-all-start = ((f32[128,1,128]{2,1,0:T(1,128)}), f32[128,1,128]{2,1,0:T(1,128)S(1)}, u32[]{:S(2)}, u32[]{:S(2)}) async-start(f32[128,1,128]{2,1,0:T(1,128)} %bitcast.4), calls=%async_computation | async-start | bytes 131072 | tf_op jit(solution)/shard_map/all_to_all | solution.py:536
  107.7 2.0 %copy-start.1 = (f32[7,32,2,16,128]{4,3,2,1,0:T(8,128)S(1)}, f32[7,32,2,16,128]{4,3,2,1,0:T(8,128)}, u32[]{:S(2)}) copy-start(f32[7,32,2,16,128]{4,3,2,1,0:T(8,128)} %copy-done) | copy-start | bytes 11010052
  109.7 5.3 %copy-start.9 = (f32[32,16,256]{2,1,0:T(8,128)S(1)}, f32[32,16,256]{2,1,0:T(8,128)}, u32[]{:S(2)}) copy-start(f32[32,16,256]{2,1,0:T(8,128)} %copy-done.8) | copy-start | bytes 1572868

commit v4 on v3

--- a/solution.py
+++ b/solution.py
@@ -1,5 +1,3 @@
-import math
-
 import jax
 import jax.numpy as jnp
 import numpy as np
@@ -157,12 +155,19 @@
     return jnp.where(lax.axis_index("level") == 0, lower, upper)
 
 
-def pack_rows_kernel(u, f, d, out):
+def pack_rows_kernel(u, f, d, out, rows, arrived):
     nx, ny, _ = u.shape
-    for n, ref in enumerate((u, f, d)):
+    start = pl.multiple_of((ny - ROWS) * (1 - lax.axis_index("level")), ROWS)
+    copies = [
+        pltpu.make_async_copy(ref.at[:, pl.ds(start, ROWS), :], rows.at[n], arrived.at[n])
+        for n, ref in enumerate((u, f, d))
+    ]
+    for copy in copies:
+        copy.start()
+    for n, copy in enumerate(copies):
+        copy.wait()
         for c in range(2):
-            lanes = slice(c * 128, (c + 1) * 128)
-            out[n * nx : (n + 1) * nx, c] = by_level(ref[:, ny - ROWS :, lanes], ref[:, :ROWS, lanes])
+            out[n * nx : (n + 1) * nx, c] = rows[n, :, :, c * 128 : (c + 1) * 128]
 
 
 def pack_planes_kernel(u, f, d, halo, to_high, to_low):
@@ -178,12 +183,13 @@
         at += width
 
 
-def pack_vector_kernel(v, halo, to_high, to_low):
-    nx, _, ny, _ = v.shape
+def pack_vector_kernel(basis, halo, dots, to_high, to_low):
+    _, nx, _, ny, _ = basis.shape
     for out, start in ((to_high, nx - HALF), (to_low, 0)):
         outer = halo[start : start + HALF]
-        out[:, :, :ROWS] = by_level(outer, v[start : start + HALF, :, ny - ROWS :])
-        out[:, :, ROWS:] = by_level(v[start : start + HALF, :, :ROWS], outer)
+        own = slice(start, start + HALF)
+        out[:, :, :ROWS] = by_level(outer, basis[HALF, own, :, ny - ROWS :])
+        out[:, :, ROWS:] = by_level(basis[HALF, own, :, :ROWS], outer)
 
 
 def row_spans(level, ny):
@@ -217,21 +223,21 @@
     return jnp.where((row >= low) & (row < high), 1.0, 0.0)
 
 
-def over_planes(nx, halo, body, own_body=None):
+def over_inner(nx, skip, body):
+    def inner(i, _):
+        body(i, None)
+        return 0
+
+    lax.fori_loop(WIDE + skip, WIDE + nx - skip, inner, 0, unroll=4 if (nx - 2 * skip) % 4 == 0 else 2)
+
+
+def over_wedges(nx, halo, skip, body):
     here, count = lax.axis_index("gx"), lax.axis_size("gx")
     below = jnp.where(here == 0, 0.0, 1.0)
     above = jnp.where(here == count - 1, 0.0, 1.0)
-    for j in range(halo):
-        body(WIDE - halo + j, below)
-    for j in range(halo):
-        body(WIDE + nx + j, above)
-
-    def inner(i, _):
-        body(i + WIDE, None)
-        return 0
-
-    if own_body is None:
-        lax.fori_loop(0, nx, inner, 0, unroll=4)
+    for j in range(-halo, skip):
+        body(WIDE + j, below if j < 0 else None)
+        body(WIDE + nx - 1 - j, above if j < 0 else None)
 
 
 def put(row, index, values):
@@ -240,20 +246,17 @@
     return jnp.where(lane == index, high, jnp.where(lane == index + LOW_AT, low, row))
 
 
-def clear(ref, nx, width):
-    tall = ref.shape[2]
+def clear_margins(refs):
+    count, _, tall, _ = refs[0].shape
     side = jnp.zeros((2, PAD, 128), jnp.float32)
-    whole = jnp.zeros((2, tall, 128), jnp.float32)
 
     def margins(i, _):
-        ref[i, :, :PAD] = side
-        ref[i, :, tall - PAD :] = side
+        for ref in refs:
+            ref[i, :, :PAD] = side
+            ref[i, :, tall - PAD :] = side
         return 0
 
-    lax.fori_loop(0, nx + 2 * WIDE, margins, 0)
-    for j in range(width):
-        ref[j] = whole
-        ref[WIDE + nx + (WIDE - width) + j] = whole
+    lax.fori_loop(0, count, margins, 0, unroll=2)
 
 
 def recur(src, dst, scale, pull, first_step, rows):
@@ -276,30 +279,11 @@
     return body
 
 
-def first_kernel(u, f, d, *refs):
-    mine, theirs = refs[:3], refs[3:6]
-    basis, scale, edge, wide_u, va, vb = refs[6:]
-    nx, ny, _ = u.shape
-    level = lax.axis_index("level")
-    for ref in (wide_u, va, vb):
-        clear(ref, nx, WIDE if ref is vb else 0)
-    va[0, :, PAD:-PAD] = jnp.zeros((2, ny + 2 * ROWS, 128), jnp.float32)
-    va[2 * WIDE + nx - 1, :, PAD:-PAD] = jnp.zeros((2, ny + 2 * ROWS, 128), jnp.float32)
-    at = 0
-    for n, (ref, width, dst) in enumerate(((u, WIDE, wide_u), (f, HALF, va), (d, HALF, scale))):
-        for (halo, xlow, xhigh), place in ((mine, level), (theirs, 1 - level)):
-            outer, part = row_spans(place, ny)
-            dst[WIDE - width : WIDE, :, part] = xlow[at : at + width]
-            dst[WIDE + nx : WIDE + nx + width, :, part] = xhigh[at : at + width]
-            dst[WIDE : WIDE + nx, :, outer] = halo[n * nx : (n + 1) * nx]
-        for c in range(2):
-            dst[WIDE : WIDE + nx, c, OWN : OWN + ny] = ref[:, :, c * 128 : (c + 1) * 128]
-        at += width
+def first_start(wide_u, va, scale, ny):
     keep = row_mask(ny)
-    pull = keep * (2.0 / RADIUS * DIFFUSION)
     rows = (PAD, ny + 2 * ROWS)
 
-    def start(i, mask):
+    def body(i, mask):
         here, around = beside(wide_u, i, *rows)
         inside = keep if mask is None else keep * mask
         for c in range(2):
@@ -308,13 +292,20 @@
             va[at] = inside * (va[at] - (damp * here[c] + DIFFUSION * (6.0 * here[c] - around[c])))
             scale[at] = inside * ((2.0 / RADIUS) * (damp + (1.0 + 6.0 * DIFFUSION - CENTRE)))
 
-    over_planes(nx, HALF, start)
-
-    def save(i, _):
-        basis[0, i] = va[i + WIDE, :, OWN : OWN + ny]
-        return 0
-
-    lax.fori_loop(0, nx, save, 0, unroll=4)
+    return body
+
+
+def first_steps(ny, wide_u, va, vb, scale, basis, over):
+    pull = row_mask(ny) * (2.0 / RADIUS * DIFFUSION)
+    rows = (PAD, ny + 2 * ROWS)
+    begin = first_start(wide_u, va, scale, ny)
+
+    def start(i, mask):
+        begin(i, mask)
+        if mask is None:
+            basis[0, i - WIDE] = va[i, :, OWN : OWN + ny]
+
+    over(HALF, 1, start)
     for k in range(HALF):
         src, dst = (va, vb) if k % 2 == 0 else (vb, va)
         last = k == HALF - 1
@@ -326,7 +317,36 @@
                 for c in range(2):
                     basis[k + 1, i - WIDE, c] = made[c] if last else made[c][ROWS : ROWS + ny]
 
-        over_planes(nx, HALF - 1 - k, body)
+        over(HALF - 1 - k, k + 2, body)
+
+
+def first_inner_kernel(u, f, d, mine, theirs, wide_u, va, vb, scale, basis):
+    nx, ny, _ = u.shape
+    level = lax.axis_index("level")
+    clear_margins((wide_u, va, vb))
+    for n, (ref, dst) in enumerate(((u, wide_u), (f, va), (d, scale))):
+        for halo, place in ((mine, level), (theirs, 1 - level)):
+            outer, _ = row_spans(place, ny)
+            dst[WIDE : WIDE + nx, :, outer] = halo[n * nx : (n + 1) * nx]
+        for c in range(2):
+            dst[WIDE : WIDE + nx, c, OWN : OWN + ny] = ref[:, :, c * 128 : (c + 1) * 128]
+    first_steps(ny, wide_u, va, vb, scale, basis, lambda halo, skip, body: over_inner(nx, skip, body))
+
+
+def first_outer_kernel(*refs):
+    mine, theirs = refs[:2], refs[2:4]
+    wide_u, va, vb, scale, basis, edge = refs[9:]
+    _, nx, _, ny, _ = basis.shape
+    level = lax.axis_index("level")
+    at = 0
+    for width, dst in ((WIDE, wide_u), (HALF, va), (HALF, scale)):
+        for (xlow, xhigh), place in ((mine, level), (theirs, 1 - level)):
+            _, part = row_spans(place, ny)
+            dst[WIDE - width : WIDE, :, part] = xlow[at : at + width]
+            dst[WIDE + nx : WIDE + nx + width, :, part] = xhigh[at : at + width]
+        at += width
+    over = lambda halo, skip, body: over_wedges(nx, halo, skip, body)
+    first_steps(ny, wide_u, va, vb, scale, basis, over)
     edge[...] = by_level(basis[HALF, :, :, ny - ROWS :, :], basis[HALF, :, :, :ROWS, :])
 
 
@@ -359,56 +379,89 @@
     dots[...] = row
 
 
-def second_kernel(u, first, scale, before, *refs):
-    mine, theirs = refs[:3], refs[3:6]
-    basis, dots, va, vb = refs[6:]
-    _, nx, _, ny, _ = first.shape
-    clear(va, nx, 0)
-    clear(vb, nx, WIDE)
-    va[0, :, PAD:-PAD] = jnp.zeros((2, ny + 2 * ROWS, 128), jnp.float32)
-    va[2 * WIDE + nx - 1, :, PAD:-PAD] = jnp.zeros((2, ny + 2 * ROWS, 128), jnp.float32)
+def second_step(j, ny, va, vb, scale, pull, u, first, basis):
+    src, dst = (va, vb) if j % 2 == 0 else (vb, va)
+    last = j == HALF - 1
+    step = recur(src, dst, scale, pull, j == 0, (OWN, ny) if last else (PAD, ny + 2 * ROWS))
+    k = HALF + j
+    get = lambda n, i, c: first[n, i, c] if n <= HALF else basis[n - HALF - 1, i, c]
+
+    def body(i, mask, sums):
+        made = step(i, mask)
+        if mask is not None:
+            return sums
+        at = i - WIDE
+        result = [list(s) for s in sums]
+        for c in range(2):
+            mid = made[c] if last else made[c][ROWS : ROWS + ny]
+            new = 2.0 * mid - first[HALF - 1 - j, at, c]
+            parts = [get(k, at, c) * new, get(k - 1, at, c) * new]
+            if not last:
+                basis[j, at, c] = new
+                parts += [new * new, u[at, :, c * 128 : (c + 1) * 128] * new]
+            for r, p in zip(result, parts):
+                r[c] = r[c] + p
+        return tuple(tuple(r) for r in result)
+
+    return body, 2 if last else 4
+
+
+def second_inner_kernel(mine, theirs, scale, u, first, basis, va, vb, sums):
+    _, nx, _, ny, _ = basis.shape
     level = lax.axis_index("level")
-    for (halo, xlow, xhigh), place in ((mine, level), (theirs, 1 - level)):
-        outer, part = row_spans(place, ny)
-        va[WIDE - HALF : WIDE, :, part] = xlow[...]
-        va[WIDE + nx : WIDE + nx + HALF, :, part] = xhigh[...]
+    clear_margins((va, vb))
+    for halo, place in ((mine, level), (theirs, 1 - level)):
+        outer, _ = row_spans(place, ny)
         va[WIDE : WIDE + nx, :, outer] = halo[...]
     va[WIDE : WIDE + nx, :, OWN : OWN + ny] = first[HALF]
     pull = row_mask(ny) * (2.0 / RADIUS * DIFFUSION)
-    rows = (PAD, ny + 2 * ROWS)
+    for j in range(HALF):
+        body, count = second_step(j, ny, va, vb, scale, pull, u, first, basis)
+        zero = jnp.zeros((ny, 128), jnp.float32)
+        low, high = WIDE + j + 1, WIDE + nx - j - 1
+        run = lambda i, made, body=body: body(i, None, made)
+        unroll = 4 if (high - low) % 4 == 0 else 2
+        made = lax.fori_loop(low, high, run, ((zero, zero),) * count, unroll=unroll)
+        for n in range(count):
+            for c in range(2):
+                sums[j, n, c] = made[n][c]
+
+
+def second_outer_kernel(*refs):
+    mine, theirs = refs[:2], refs[2:4]
+    scale, u, first, before, sums = refs[4:9]
+    basis, va, vb, dots = refs[12:]
+    _, nx, _, ny, _ = basis.shape
+    level = lax.axis_index("level")
+    for (xlow, xhigh), place in ((mine, level), (theirs, 1 - level)):
+        _, part = row_spans(place, ny)
+        va[WIDE - HALF : WIDE, :, part] = xlow[...]
+        va[WIDE + nx : WIDE + nx + HALF, :, part] = xhigh[...]
+    pull = row_mask(ny) * (2.0 / RADIUS * DIFFUSION)
     row = before[...]
-    get = lambda k, i, c: first[k, i, c] if k <= HALF else basis[k - HALF - 1, i, c]
     for j in range(HALF):
-        src, dst = (va, vb) if j % 2 == 0 else (vb, va)
-        last = j == HALF - 1
-        step = recur(src, dst, scale, pull, j == 0, (OWN, ny) if last else rows)
-        over_planes(nx, HALF - 1 - j, step, own_body=step)
+        body, count = second_step(j, ny, va, vb, scale, pull, u, first, basis)
+        made = [tuple(tuple(sums[j, n, c] for c in range(2)) for n in range(count))]
+
+        def run(i, mask, body=body, made=made):
+            made[0] = body(i, mask, made[0])
+
+        over_wedges(nx, HALF - 1 - j, j + 1, run)
         k = HALF + j
-
-        def body(i, sums, step=step, j=j, k=k, last=last):
-            made = step(i + WIDE, None)
-            result = [list(s) for s in sums]
-            for c in range(2):
-                mid = made[c] if last else made[c][ROWS : ROWS + ny]
-                new = 2.0 * mid - first[HALF - 1 - j, i, c]
-                parts = [get(k, i, c) * new, get(k - 1, i, c) * new]
-                if not last:
-                    basis[j, i, c] = new
-                    parts += [new * new, u[i, :, c * 128 : (c + 1) * 128] * new]
-                for r, p in zip(result, parts):
-                    r[c] = r[c] + p
-            return tuple(tuple(r) for r in result)
-
-        zero = jnp.zeros((ny, 128), jnp.float32)
-        sums = lax.fori_loop(0, nx, body, ((zero, zero),) * (2 if last else 4), unroll=4)
         where = (2 * k + 1, CHECK_AT + k, 2 * k + 2, FIELD_AT + 2 + k)
-        for at, (a, b) in zip(where, sums):
+        for at, (a, b) in zip(where, made[0]):
             row = put(row, at, jnp.concatenate([a, b], axis=0))
     dots[...] = jnp.broadcast_to(row[0:1], dots.shape)
 
 
-def finish_kernel(gathered, tables, nodes, u, first, second, out, flag):
-    nx, ny, nz = u.shape
+def finish_kernel(gathered, tables, nodes, second, far_u, far_first, out, flag, u, first, arrived):
+    nx, ny, _ = out.shape
+    copies = [
+        pltpu.make_async_copy(far_u, u, arrived.at[0]),
+        pltpu.make_async_copy(far_first, first, arrived.at[1]),
+    ]
+    for copy in copies:
+        copy.start()
     turned = gathered[...].T
     high, low = split_sum(turned[:LOW_AT], 1)
     high, low = two_sum(high, low + total(turned[LOW_AT:]))
@@ -416,6 +469,8 @@
     level = lax.axis_index("level")
     part = jnp.where(level == 0, lower, upper)
     flag[0, 0] = jnp.where(jnp.min(jnp.where(fine_low & fine_up, 1.0, 0.0)) > 0.5, 1, 0)
+    for copy in copies:
+        copy.wait()
     factors = [jnp.broadcast_to(part[k : k + 1], (8, 128)) for k in range(TOP)]
 
     def body(i, _):
@@ -431,24 +486,26 @@
     lax.fori_loop(0, nx, body, 0, unroll=2)
 
 
-def call(kernel, outs, args, scratch=(), limit=16 << 20, flags=()):
+def call(kernel, outs, args, limit=16 << 20, flags=(), alias=None, far=0, scratch=()):
     whole = pl.BlockSpec(memory_space=pltpu.VMEM)
     shapes = [jax.ShapeDtypeStruct(s, jnp.float32) for s in outs]
     return pl.pallas_call(
         kernel,
         out_shape=shapes + [jax.ShapeDtypeStruct(s, jnp.int32) for s in flags],
-        in_specs=[whole] * len(args),
+        in_specs=[whole] * (len(args) - far) + [pl.BlockSpec(memory_space=pltpu.HBM)] * far,
+        scratch_shapes=scratch,
         out_specs=[whole] * len(outs) + [pl.BlockSpec(memory_space=pltpu.SMEM)] * len(flags),
-        scratch_shapes=[pltpu.VMEM(s, jnp.float32) for s in scratch],
+        input_output_aliases=alias or {},
         compiler_params=pltpu.CompilerParams(vmem_limit_bytes=limit),
-        name=kernel.__name__,
     )(*args)
 
 
 def both_ways(up, down, axis):
     size = lax.axis_size(axis)
     route = [(i, i + 1) for i in range(size - 1)]
-    return lax.ppermute(up, axis, route), lax.ppermute(down, axis, [(b, a) for a, b in route])
+    high = lax.ppermute(up, axis, route)
+    low = lax.ppermute(down, axis, [(b, a) for a, b in route])
+    return high, low
 
 
 def stencil(field, damping):
@@ -508,38 +565,57 @@
 def per_device(u, f, d):
     nx, ny, nz = u.shape
     tall = 2 * ROWS + ny
-    (edge,) = call(pack_rows_kernel, [(3 * nx, 2, ROWS, 128)], (u, f, d))
+    (edge,) = call(
+        pack_rows_kernel,
+        [(3 * nx, 2, ROWS, 128)],
+        (u, f, d),
+        far=3,
+        scratch=[pltpu.VMEM((3, nx, ROWS, nz), jnp.float32), pltpu.SemaphoreType.DMA((3,))],
+    )
     halo = along_rows(edge)
     planes = (WIDE + 2 * HALF, 2, 2 * ROWS, 128)
     ups, downs = call(pack_planes_kernel, [planes] * 2, (u, f, d, halo))
-    mine = (halo,) + both_ways(ups, downs, "gx")
-    theirs = tuple(swapped(part) for part in mine)
-    padded = (nx + 2 * WIDE, 2, tall + 2 * PAD, 128)
-    first, scale, edge = call(
-        first_kernel,
-        [(HALF + 1, nx, 2, ny, 128), padded, (nx, 2, ROWS, 128)],
-        (u, f, d) + mine + theirs,
-        [padded] * 3,
+    theirs = swapped(halo)
+    wide = (nx + 2 * WIDE, 2, tall + 2 * PAD, 128)
+    block = (nx, 2, ny, 128)
+    mine = both_ways(ups, downs, "gx")
+    buffers = call(first_inner_kernel, [wide] * 4 + [(HALF + 1,) + block], (u, f, d, halo, theirs))
+    *_, scale, first, edge = call(
+        first_outer_kernel,
+        [wide] * 4 + [(HALF + 1,) + block, (nx, 2, ROWS, 128)],
+        mine + tuple(swapped(part) for part in mine) + tuple(buffers),
+        alias={4 + n: n for n in range(5)},
     )
     halo = along_rows(edge)
+    theirs = swapped(halo)
     (dots,) = call(first_dots_kernel, [(8, 128)], (u, first))
-    ups, downs = call(pack_vector_kernel, [(HALF, 2, 2 * ROWS, 128)] * 2, (first[HALF], halo))
-    mine = (halo,) + both_ways(ups, downs, "gx")
-    theirs = tuple(swapped(part) for part in mine)
+    ups, downs = call(pack_vector_kernel, [(HALF, 2, 2 * ROWS, 128)] * 2, (first, halo, dots))
+    mine = both_ways(ups, downs, "gx")
+    second, va, vb, sums = call(
+        second_inner_kernel,
+        [(HALF - 1,) + block, wide, wide, (HALF, 4, 2, ny, 128)],
+        (halo, theirs, scale, u, first),
+    )
     parts = lax.axis_size(AXES)
-    second, dots = call(
-        second_kernel,
-        [(HALF - 1, nx, 2, ny, 128), (parts, 128)],
-        (u, first, scale, dots) + mine + theirs,
-        [padded] * 2,
+    second, _, _, dots = call(
+        second_outer_kernel,
+        [(HALF - 1,) + block, wide, wide, (parts, 128)],
+        mine + tuple(swapped(part) for part in mine) + (scale, u, first, dots, sums, second, va, vb),
+        alias={9: 0, 10: 1, 11: 2},
     )
     gathered = lax.all_to_all(dots.reshape(parts, 1, 128), AXES, 0, 0).reshape(parts, 128)
     tables, nodes = chebyshev_tables()
     fast, flag = call(
         finish_kernel,
         [(nx, ny, nz)],
-        (gathered, jnp.asarray(tables), jnp.asarray(nodes), u, first, second),
+        (gathered, jnp.asarray(tables), jnp.asarray(nodes), second, u, first),
         flags=[(1, 1)],
+        far=2,
+        scratch=[
+            pltpu.VMEM((nx, ny, nz), jnp.float32),
+            pltpu.VMEM((HALF + 1,) + block, jnp.float32),
+            pltpu.SemaphoreType.DMA((2,)),
+        ],
     )
     state = lax.cond(flag.reshape(()), lambda: fast, lambda: step_by_step(u, f, d))
     return state[None]

time: 117 us -> 113 us (0.966)
  Pallas kernels: 33.3 us -> 31.6 us
  waiting for transfers between devices: 43.5 us -> 41.9 us
    pallas_call x7 -> x9, Pallas kernels: 33.3 us -> 31.6 us  [call(): pl.pallas_call(kernel, out_shape=shapes + [jax.ShapeDtypeStruct(s, jnp.in...]
    ppermute x6, waiting for transfers between devices: 1.61 us -> 0.02 us  [swapped(): return lax.ppermute(block, 'level', [(0, 1), (1, 0)])]
  transfers between devices with their start and end apart: 13 -> 13, of which waited for: 8 -> 7; matrix products, arithmetic and copies ran while one was open for 0% -> 0% of each run, Pallas kernels for 5% -> 18%
where the time goes in v4:
time: 113 us; the launch traced here: 112 us
  waiting for transfers between devices  41.9 us (37%)
  starting transfers between devices  34.2 us (30%)
  Pallas kernels  31.6 us (28%)
  local copies, waits for them, and re-layouts  3.2 us (3%)
    pallas_call x9, Pallas kernels, call(): pl.pallas_call(kernel, out_shape=shapes + [jax.ShapeDtypeStruct(s, jnp.in...  31.6 us
    all_to_all x1, starting transfers between devices, per_device(): lax.all_to_all(dots.reshape(parts, 1, 128), AXES, 0, 0).reshape(parts, 128)  17.9 us
    ppermute x2, waiting for transfers between devices, along_rows(): return lax.ppermute(block, ('level', 'yz'), route)  15.2 us
    all_to_all x1, waiting for transfers between devices, per_device(): lax.all_to_all(dots.reshape(parts, 1, 128), AXES, 0, 0).reshape(parts, 128)  11.1 us
    ppermute x2, waiting for transfers between devices, both_ways(): low = lax.ppermute(down, axis, [(b, a) for a, b in route])  8.24 us
    ppermute x2, waiting for transfers between devices, both_ways(): high = lax.ppermute(up, axis, route)  7.35 us
    ppermute x2, starting transfers between devices, along_rows(): return lax.ppermute(block, ('level', 'yz'), route)  6.97 us
    ppermute x2, starting transfers between devices, both_ways(): high = lax.ppermute(up, axis, route)  6.8 us
  transfers between devices with their start and end apart: 13, of which 7 were waited for; matrix products, arithmetic and copies ran while one was open for 0% of the time, Pallas kernels for 18%

profile of v4, /device:TPU:8, one launch (start us, length us, event | category | flops | bytes accessed | tf_op | source)
XLA Modules:
  0.0 112.0 jit_solution(6563531410847833002)
XLA Ops:
  0.0 1.1 %copy.69.u.refs_5_.far_u = f32[32,16,256]{2,1,0:T(8,128)S(1)} copy(f32[32,16,256]{2,1,0:T(8,128)} %param.13) | data formatting | bytes 1048576
  1.1 1.3 %shard_map.57 = f32[96,2,8,128]{3,2,1,0:T(8,128)S(1)} custom-call(f32[32,16,256]{2,1,0:T(8,128)S(1)} %copy.69.u.refs_5_.far_u, f32[32,16,256]{2,1,0:T(8,128)} %f.5, f32[32,16,256]{2,1,0:T(8,128)} %d.5), custom_call_target="tpu_custom_call" | custom-call | tf_op jit(solution)/shard_map/pallas_call | solution.py:492
  2.4 3.5 %collective-permute-start.20 = (f32[96,2,8,128]{3,2,1,0:T(8,128)S(1)}, f32[96,2,8,128]{3,2,1,0:T(8,128)S(1)}, u32[]{:S(2)}, u32[]{:S(2)}) collective-permute-start(f32[96,2,8,128]{3,2,1,0:T(8,128)S(1)} %shard_map.57), channel_id=1, source_target_pairs={{0,1},{1,2},{2,3},{3,4},{4,5},{5,6},{6,7},{7,8},{8,9},{9,10},{10,1... | collective-permute-start | bytes 2359304 | tf_op jit(solution)/shard_map/ppermute | solution.py:558
  5.9 10.4 %collective-permute-done.20.halo.mine = f32[96,2,8,128]{3,2,1,0:T(8,128)S(1)} collective-permute-done((f32[96,2,8,128]{3,2,1,0:T(8,128)S(1)}, f32[96,2,8,128]{3,2,1,0:T(8,128)S(1)}, u32[]{:S(2)}, u32[]{:S(2)}) %collective-permute-start.20) | collective-permute-done | bytes 786464 | tf_op jit(solution)/shard_map/ppermute | solution.py:558
  16.3 0.0 collective-permute-start.25
  16.3 0.1 shard_map.58
  16.4 3.4 %collective-permute-start.21 = (f32[19,2,16,128]{3,2,1,0:T(8,128)S(1)}, f32[19,2,16,128]{3,2,1,0:T(8,128)S(1)}, u32[]{:S(2)}, u32[]{:S(2)}) collective-permute-start(f32[19,2,16,128]{3,2,1,0:T(8,128)S(1)} %get-tuple-element.132), channel_id=1, source_target_pairs={{0,32},{32,64},{64,96},{1,33},{33,65},{65,97},{2,34},{34,66},{66,9... | collective-permute-start | bytes 933896 | tf_op jit(solution)/shard_map/ppermute | solution.py:506
  19.8 1.3 %collective-permute-start.22 = (f32[19,2,16,128]{3,2,1,0:T(8,128)S(1)}, f32[19,2,16,128]{3,2,1,0:T(8,128)S(1)}, u32[]{:S(2)}, u32[]{:S(2)}) collective-permute-start(f32[19,2,16,128]{3,2,1,0:T(8,128)S(1)} %get-tuple-element.133), channel_id=1, source_target_pairs={{32,0},{64,32},{96,64},{33,1},{65,33},{97,65},{34,2},{66,34},{98,6... | collective-permute-start | bytes 933896 | tf_op jit(solution)/shard_map/ppermute | solution.py:507
  21.1 5.9 %collective-permute-done.21.refs_0_ = f32[19,2,16,128]{3,2,1,0:T(8,128)S(1)} collective-permute-done((f32[19,2,16,128]{3,2,1,0:T(8,128)S(1)}, f32[19,2,16,128]{3,2,1,0:T(8,128)S(1)}, u32[]{:S(2)}, u32[]{:S(2)}) %collective-permute-start.21) | collective-permute-done | bytes 311328 | tf_op jit(solution)/shard_map/ppermute | solution.py:506
  27.1 0.0 collective-permute-start.23
  27.1 4.1 %collective-permute-done.22.refs_1_ = f32[19,2,16,128]{3,2,1,0:T(8,128)S(1)} collective-permute-done((f32[19,2,16,128]{3,2,1,0:T(8,128)S(1)}, f32[19,2,16,128]{3,2,1,0:T(8,128)S(1)}, u32[]{:S(2)}, u32[]{:S(2)}) %collective-permute-start.22) | collective-permute-done | bytes 311328 | tf_op jit(solution)/shard_map/ppermute | solution.py:507
  31.2 0.0 collective-permute-start.24
  31.2 0.0 collective-permute-done.25.theirs
  31.2 8.0 %shard_map.59 = (f32[46,2,48,128]{3,2,1,0:T(8,128)S(1)}, f32[46,2,48,128]{3,2,1,0:T(8,128)S(1)}, f32[46,2,48,128]{3,2,1,0:T(8,128)S(1)}, f32[46,2,48,128]{3,2,1,0:T(8,128)S(1)}, f32[7,32,2,16,128]{4,3,2,1,0:T(8,128)S(1)}) custom-call(f32[32,16,256]{2,1,0:T(8,128)S(1)} %copy.69.u.refs_5_.far_u, f32[32,16,256]{2,1,0:T(8,128)S(1)} %copy-done.13, ...), custom_call_target="tpu_custom_call" | custom-call | tf_op jit(solution)/shard_map/pallas_call | solution.py:492
  39.2 0.0 collective-permute-done.24.refs_3_
  39.2 1.8 %shard_map.60 = (f32[46,2,48,128]{3,2,1,0:T(8,128)S(1)}, f32[46,2,48,128]{3,2,1,0:T(8,128)S(1)}, f32[46,2,48,128]{3,2,1,0:T(8,128)S(1)}, f32[46,2,48,128]{3,2,1,...) custom-call(f32[19,2,16,128]{3,2,1,0:T(8,128)S(1)} %collective-permu, ...), custom_call_target="tpu_custom_call", output_to_operand_aliasing={{0}: (4, {}), {1}: (5, {}), {2}: (6, {}), {3}: (7, {}), {4}... | custom-call | tf_op jit(solution)/shard_map/pallas_call | solution.py:492
  41.1 3.5 %collective-permute-start.26 = (f32[32,2,8,128]{3,2,1,0:T(8,128)S(1)}, f32[32,2,8,128]{3,2,1,0:T(8,128)S(1)}, u32[]{:S(2)}, u32[]{:S(2)}) collective-permute-start(f32[32,2,8,128]{3,2,1,0:T(8,128)S(1)} %get-tuple-element.140), channel_id=1, source_target_pairs={{0,1},{1,2},{2,3},{3,4},{4,5},{5,6},{6,7},{7,8},{8,9},{9,10},{10,1... | collective-permute-start | bytes 786440 | tf_op jit(solution)/shard_map/ppermute | solution.py:558
  44.6 4.8 %collective-permute-done.26.halo.mine = f32[32,2,8,128]{3,2,1,0:T(8,128)S(1)} collective-permute-done((f32[32,2,8,128]{3,2,1,0:T(8,128)S(1)}, f32[32,2,8,128]{3,2,1,0:T(8,128)S(1)}, u32[]{:S(2)}, u32[]{:S(2)}) %collective-permute-start.26) | collective-permute-done | bytes 262176 | tf_op jit(solution)/shard_map/ppermute | solution.py:558
  49.3 0.0 collective-permute-start.31
  49.3 5.2 %shard_map.61.dots.refs_7_ = f32[8,128]{1,0:T(8,128)S(1)} custom-call(f32[32,16,256]{2,1,0:T(8,128)S(1)} %copy.69.u.refs_5_.far_u, f32[7,32,2,16,128]{4,3,2,1,0:T(8,128)S(1)} %get-tuple-element.139.basis.first.refs_6_.far_first), custom_call_target="tpu_custom_call" | custom-call | tf_op jit(solution)/shard_map/pallas_call | solution.py:492
  54.6 3.4 %collective-permute-start.27 = (f32[6,2,16,128]{3,2,1,0:T(8,128)S(1)}, f32[6,2,16,128]{3,2,1,0:T(8,128)S(1)}, u32[]{:S(2)}, u32[]{:S(2)}) collective-permute-start(f32[6,2,16,128]{3,2,1,0:T(8,128)S(1)} %get-tuple-element.141), channel_id=1, source_target_pairs={{0,32},{32,64},{64,96},{1,33},{33,65},{65,97},{2,34},{34,66},{66,9... | collective-permute-start | bytes 294920 | tf_op jit(solution)/shard_map/ppermute | solution.py:506
  58.0 1.3 %collective-permute-start.28 = (f32[6,2,16,128]{3,2,1,0:T(8,128)S(1)}, f32[6,2,16,128]{3,2,1,0:T(8,128)S(1)}, u32[]{:S(2)}, u32[]{:S(2)}) collective-permute-start(f32[6,2,16,128]{3,2,1,0:T(8,128)S(1)} %get-tuple-element.142), channel_id=1, source_target_pairs={{32,0},{64,32},{96,64},{33,1},{65,33},{97,65},{34,2},{66,34},{98,6... | collective-permute-start | bytes 294920 | tf_op jit(solution)/shard_map/ppermute | solution.py:507
  59.3 1.4 %collective-permute-done.27.refs_0_ = f32[6,2,16,128]{3,2,1,0:T(8,128)S(1)} collective-permute-done((f32[6,2,16,128]{3,2,1,0:T(8,128)S(1)}, f32[6,2,16,128]{3,2,1,0:T(8,128)S(1)}, u32[]{:S(2)}, u32[]{:S(2)}) %collective-permute-start.27) | collective-permute-done | bytes 98336 | tf_op jit(solution)/shard_map/ppermute | solution.py:506
  60.7 4.1 %collective-permute-done.28.refs_1_ = f32[6,2,16,128]{3,2,1,0:T(8,128)S(1)} collective-permute-done((f32[6,2,16,128]{3,2,1,0:T(8,128)S(1)}, f32[6,2,16,128]{3,2,1,0:T(8,128)S(1)}, u32[]{:S(2)}, u32[]{:S(2)}) %collective-permute-start.28) | collective-permute-done | bytes 98336 | tf_op jit(solution)/shard_map/ppermute | solution.py:507
  64.8 7.3 %shard_map.63 = (f32[5,32,2,16,128]{4,3,2,1,0:T(8,128)S(1)}, f32[46,2,48,128]{3,2,1,0:T(8,128)S(1)}, f32[46,2,48,128]{3,2,1,0:T(8,128)S(1)}, f32[6,4,2,16,128]{4,3,2,1,0:T(8,128)S(1)}) custom-call(f32[32,2,8,128]{3,2,1,0:T(8,128)S(1)} %collective-permute-done.26.halo.mine, f32[32,2,8,128]{3,2,1,0:T(8,128)S(1)} %collective-permute-done.31.theirs, ...), custom_call_target="tpu_custom_call" | custom-call | tf_op jit(solution)/shard_map/pallas_call | solution.py:492
  72.2 0.0 copy-start.2
  72.2 0.0 copy-start.3
  72.3 4.0 %shard_map.64 = (f32[5,32,2,16,128]{4,3,2,1,0:T(8,128)S(1)}, f32[46,2,48,128]{3,2,1,0:T(8,128)S(1)}, f32[46,2,48,128]{3,2,1,0:T(8,128)S(1)}, f32[128,128]{1,0:T(8,128)}) custom-call(f32[6,2,16,128]{3,2,1,0:T(8,128)S(1)} %collective-permute-done.27.refs_0_, ...), custom_call_target="tpu_custom_call", output_to_operand_aliasing={{0}: (9, {}), {1}: (10, {}), {2}: (11, {})} | custom-call | tf_op jit(solution)/shard_map/pallas_call | solution.py:492
  76.3 17.9 %all-to-all-start = ((f32[128,1,128]{2,1,0:T(1,128)}), f32[128,1,128]{2,1,0:T(1,128)S(1)}, u32[]{:S(2)}, u32[]{:S(2)}) async-start(f32[128,1,128]{2,1,0:T(1,128)} %bitcast.3), calls=%async_computation | async-start | bytes 131072 | tf_op jit(solution)/shard_map/all_to_all | solution.py:606
  94.2 11.1 %all-to-all-done = f32[128,1,128]{2,1,0:T(1,128)S(1)} async-done(((f32[128,1,128]{2,1,0:T(1,128)}), f32[128,1,128]{2,1,0:T(1,128)S(1)}, u32[]{:S(2)}, u32[]{:S(2)}) %all-to-all-start) | async-done | bytes 65568 | tf_op jit(solution)/shard_map/all_to_all | solution.py:606
  105.3 2.0 %copy-done.1 = f32[7,32,2,16,128]{4,3,2,1,0:T(8,128)S(1)} copy-done((f32[7,32,2,16,128]{4,3,2,1,0:T(8,128)S(1)}, f32[7,32,2,16,128]{4,3,2,1,0:T(8,128)}, u32[]{:S(2)}) %copy-start.1) | copy-done | bytes 3670040
  107.3 3.8 %shard_map.65 = (f32[32,16,256]{2,1,0:T(8,128)}, s32[1,1]{1,0:T(1,128)}) custom-call(f32[128,128]{1,0:T(8,128)S(1)} %bitcast.8, f32[128,128]{1,0:T(8,128)S(1)} %copy-done.2, f32[1,128]{1,0:T(1,128)S(1)} %copy-done.3, f32[5,32,2,16,128]{4,3,2,1,0:T(8,128)S(1)} %get-tuple-element.149.second, f32[32,16,256]{2,1,0:T(8,128)} %copy-done.8, ...), custom_call_target="tpu_custom_call" | custom-call | tf_op jit(solution)/shard_map/pallas_call | solution.py:492
  (21 shorter events, 0.1 us)
Async XLA Ops:
  0.0 16.3 %copy-start.13 = (f32[32,16,256]{2,1,0:T(8,128)S(1)}, f32[32,16,256]{2,1,0:T(8,128)}, u32[]{:S(2)}) copy-start(f32[32,16,256]{2,1,0:T(8,128)} %f.5) | copy-start | bytes 1572868
  0.0 16.3 %copy-start.4 = (f32[32,16,256]{2,1,0:T(8,128)S(1)}, f32[32,16,256]{2,1,0:T(8,128)}, u32[]{:S(2)}) copy-start(f32[32,16,256]{2,1,0:T(8,128)} %d.5) | copy-start | bytes 1572868
  1.1 71.1 %copy-start.8 = (f32[32,16,256]{2,1,0:T(8,128)}, f32[32,16,256]{2,1,0:T(8,128)S(1)}, u32[]{:S(2)}) copy-start(f32[32,16,256]{2,1,0:T(8,128)S(1)} %copy.69.u.refs_5_.far_u) | copy-start | bytes 1572868
  2.4 13.9 %collective-permute-start.20 = (f32[96,2,8,128]{3,2,1,0:T(8,128)S(1)}, f32[96,2,8,128]{3,2,1,0:T(8,128)S(1)}, u32[]{:S(2)}, u32[]{:S(2)}) collective-permute-start(f32[96,2,8,128]{3,2,1,0:T(8,128)S(1)} %shard_map.57), channel_id=1, source_target_pairs={{0,1},{1,2},{2,3},{3,4},{4,5},{5,6},{6,7},{7,8},{8,9},{9,10},{10,1... | collective-permute-start | bytes 2359304 | tf_op jit(solution)/shard_map/ppermute | solution.py:558
  16.3 14.9 %collective-permute-start.25 = (f32[96,2,8,128]{3,2,1,0:T(8,128)S(1)}, f32[96,2,8,128]{3,2,1,0:T(8,128)S(1)}, u32[]{:S(2)}, u32[]{:S(2)}) collective-permute-start(f32[96,2,8,128]{3,2,1,0:T(8,128)S(1)} %collective-permute-done.20.halo.mine), channel_id=1, source_target_pairs={{0,128},{128,0},{1,129},{129,1},{2,130},{130,2},{3,131},{131,3},{4... | collective-permute-start | bytes 2359304 | tf_op jit(solution)/shard_map/ppermute | solution.py:562
  16.4 10.7 %collective-permute-start.21 = (f32[19,2,16,128]{3,2,1,0:T(8,128)S(1)}, f32[19,2,16,128]{3,2,1,0:T(8,128)S(1)}, u32[]{:S(2)}, u32[]{:S(2)}) collective-permute-start(f32[19,2,16,128]{3,2,1,0:T(8,128)S(1)} %get-tuple-element.132), channel_id=1, source_target_pairs={{0,32},{32,64},{64,96},{1,33},{33,65},{65,97},{2,34},{34,66},{66,9... | collective-permute-start | bytes 933896 | tf_op jit(solution)/shard_map/ppermute | solution.py:506
  19.8 11.4 %collective-permute-start.22 = (f32[19,2,16,128]{3,2,1,0:T(8,128)S(1)}, f32[19,2,16,128]{3,2,1,0:T(8,128)S(1)}, u32[]{:S(2)}, u32[]{:S(2)}) collective-permute-start(f32[19,2,16,128]{3,2,1,0:T(8,128)S(1)} %get-tuple-element.133), channel_id=1, source_target_pairs={{32,0},{64,32},{96,64},{33,1},{65,33},{97,65},{34,2},{66,34},{98,6... | collective-permute-start | bytes 933896 | tf_op jit(solution)/shard_map/ppermute | solution.py:507
  27.1 12.2 %collective-permute-start.23 = (f32[19,2,16,128]{3,2,1,0:T(8,128)S(1)}, f32[19,2,16,128]{3,2,1,0:T(8,128)S(1)}, u32[]{:S(2)}, u32[]{:S(2)}) collective-permute-start(f32[19,2,16,128]{3,2,1,0:T(8,128)S(1)} %collective-permute-done.21.refs_0_), channel_id=1, source_target_pairs={{0,128},{128,0},{1,129},{129,1},{2,130},{130,2},{3,131},{131,3},{4... | collective-permute-start | bytes 933896 | tf_op jit(solution)/shard_map/ppermute | solution.py:562
  31.2 8.0 %collective-permute-start.24 = (f32[19,2,16,128]{3,2,1,0:T(8,128)S(1)}, f32[19,2,16,128]{3,2,1,0:T(8,128)S(1)}, u32[]{:S(2)}, u32[]{:S(2)}) collective-permute-start(f32[19,2,16,128]{3,2,1,0:T(8,128)S(1)} %collective-permute-done.22.refs_1_), channel_id=1, source_target_pairs={{0,128},{128,0},{1,129},{129,1},{2,130},{130,2},{3,131},{131,3},{4... | collective-permute-start | bytes 933896 | tf_op jit(solution)/shard_map/ppermute | solution.py:562
  41.1 31.2 %copy-start = (f32[7,32,2,16,128]{4,3,2,1,0:T(8,128)}, f32[7,32,2,16,128]{4,3,2,1,0:T(8,128)S(1)}, u32[]{:S(2)}) copy-start(f32[7,32,2,16,128]{4,3,2,1,0:T(8,128)S(1)} %get-tuple-element.139.basis.first.refs_6_.far_first) | copy-start | bytes 11010052
  41.1 8.3 %collective-permute-start.26 = (f32[32,2,8,128]{3,2,1,0:T(8,128)S(1)}, f32[32,2,8,128]{3,2,1,0:T(8,128)S(1)}, u32[]{:S(2)}, u32[]{:S(2)}) collective-permute-start(f32[32,2,8,128]{3,2,1,0:T(8,128)S(1)} %get-tuple-element.140), channel_id=1, source_target_pairs={{0,1},{1,2},{2,3},{3,4},{4,5},{5,6},{6,7},{7,8},{8,9},{9,10},{10,1... | collective-permute-start | bytes 786440 | tf_op jit(solution)/shard_map/ppermute | solution.py:558
  49.3 15.5 %collective-permute-start.31 = (f32[32,2,8,128]{3,2,1,0:T(8,128)S(1)}, f32[32,2,8,128]{3,2,1,0:T(8,128)S(1)}, u32[]{:S(2)}, u32[]{:S(2)}) collective-permute-start(f32[32,2,8,128]{3,2,1,0:T(8,128)S(1)} %collective-permute-done.26.halo.mine), channel_id=1, source_target_pairs={{0,128},{128,0},{1,129},{129,1},{2,130},{130,2},{3,131},{131,3},{4... | collective-permute-start | bytes 786440 | tf_op jit(solution)/shard_map/ppermute | solution.py:562
  54.6 6.1 %collective-permute-start.27 = (f32[6,2,16,128]{3,2,1,0:T(8,128)S(1)}, f32[6,2,16,128]{3,2,1,0:T(8,128)S(1)}, u32[]{:S(2)}, u32[]{:S(2)}) collective-permute-start(f32[6,2,16,128]{3,2,1,0:T(8,128)S(1)} %get-tuple-element.141), channel_id=1, source_target_pairs={{0,32},{32,64},{64,96},{1,33},{33,65},{65,97},{2,34},{34,66},{66,9... | collective-permute-start | bytes 294920 | tf_op jit(solution)/shard_map/ppermute | solution.py:506
  58.0 6.8 %collective-permute-start.28 = (f32[6,2,16,128]{3,2,1,0:T(8,128)S(1)}, f32[6,2,16,128]{3,2,1,0:T(8,128)S(1)}, u32[]{:S(2)}, u32[]{:S(2)}) collective-permute-start(f32[6,2,16,128]{3,2,1,0:T(8,128)S(1)} %get-tuple-element.142), channel_id=1, source_target_pairs={{32,0},{64,32},{96,64},{33,1},{65,33},{97,65},{34,2},{66,34},{98,6... | collective-permute-start | bytes 294920 | tf_op jit(solution)/shard_map/ppermute | solution.py:507
  60.7 11.5 %collective-permute-start.29 = (f32[6,2,16,128]{3,2,1,0:T(8,128)S(1)}, f32[6,2,16,128]{3,2,1,0:T(8,128)S(1)}, u32[]{:S(2)}, u32[]{:S(2)}) collective-permute-start(f32[6,2,16,128]{3,2,1,0:T(8,128)S(1)} %collective-permute-done.27.refs_0_), channel_id=1, source_target_pairs={{0,128},{128,0},{1,129},{129,1},{2,130},{130,2},{3,131},{131,3},{4... | collective-permute-start | bytes 294920 | tf_op jit(solution)/shard_map/ppermute | solution.py:562
  64.8 7.4 %collective-permute-start.30 = (f32[6,2,16,128]{3,2,1,0:T(8,128)S(1)}, f32[6,2,16,128]{3,2,1,0:T(8,128)S(1)}, u32[]{:S(2)}, u32[]{:S(2)}) collective-permute-start(f32[6,2,16,128]{3,2,1,0:T(8,128)S(1)} %collective-permute-done.28.refs_1_), channel_id=1, source_target_pairs={{0,128},{128,0},{1,129},{129,1},{2,130},{130,2},{3,131},{131,3},{4... | collective-permute-start | bytes 294920 | tf_op jit(solution)/shard_map/ppermute | solution.py:562
  72.2 33.0 %copy-start.2 = (f32[128,128]{1,0:T(8,128)S(1)}, f32[128,128]{1,0:T(8,128)}, u32[]{:S(2)}) copy-start(f32[128,128]{1,0:T(8,128)} %constant.48.clone.tables) | copy-start | bytes 196612
  72.2 33.0 %copy-start.3 = (f32[1,128]{1,0:T(1,128)S(1)}, f32[1,128]{1,0:T(1,128)}, u32[]{:S(2)}) copy-start(f32[1,128]{1,0:T(1,128)} %constant.49.clone.nodes) | copy-start | bytes 1540
  76.3 29.0 %all-to-all-start = ((f32[128,1,128]{2,1,0:T(1,128)}), f32[128,1,128]{2,1,0:T(1,128)S(1)}, u32[]{:S(2)}, u32[]{:S(2)}) async-start(f32[128,1,128]{2,1,0:T(1,128)} %bitcast.3), calls=%async_computation | async-start | bytes 131072 | tf_op jit(solution)/shard_map/all_to_all | solution.py:606
  105.3 2.0 %copy-start.1 = (f32[7,32,2,16,128]{4,3,2,1,0:T(8,128)S(1)}, f32[7,32,2,16,128]{4,3,2,1,0:T(8,128)}, u32[]{:S(2)}) copy-start(f32[7,32,2,16,128]{4,3,2,1,0:T(8,128)} %copy-done) | copy-start | bytes 11010052
  107.3 4.5 %copy-start.9 = (f32[32,16,256]{2,1,0:T(8,128)S(1)}, f32[32,16,256]{2,1,0:T(8,128)}, u32[]{:S(2)}) copy-start(f32[32,16,256]{2,1,0:T(8,128)} %copy-done.8) | copy-start | bytes 1572868

commit v5 on v4

--- a/solution.py
+++ b/solution.py
@@ -1,3 +1,5 @@
+import functools
+
 import jax
 import jax.numpy as jnp
 import numpy as np
@@ -58,10 +60,9 @@
     return high, values - high
 
 
-def split_sum(values, axis=None):
-    count = values.size if axis is None else values.shape[axis]
+def split_sum(values, axis):
     most = jnp.max(jnp.abs(values), axis=axis, keepdims=True)
-    unit = (4.0 * count) * most
+    unit = (4.0 * values.shape[axis]) * most
     high = (values + unit) - unit
     return jnp.sum(high, axis=axis, keepdims=True), jnp.sum(values - high, axis=axis, keepdims=True)
 
@@ -155,32 +156,34 @@
     return jnp.where(lax.axis_index("level") == 0, lower, upper)
 
 
-def pack_rows_kernel(u, f, d, out, rows, arrived):
+def pack_first_kernel(u, f, d, rows_out, planes_out, rows, planes, arrived):
     nx, ny, _ = u.shape
-    start = pl.multiple_of((ny - ROWS) * (1 - lax.axis_index("level")), ROWS)
-    copies = [
-        pltpu.make_async_copy(ref.at[:, pl.ds(start, ROWS), :], rows.at[n], arrived.at[n])
-        for n, ref in enumerate((u, f, d))
-    ]
+    level = lax.axis_index("level")
+    start = pl.multiple_of((ny - ROWS) * (1 - level), ROWS)
+    copies = []
+    for n, (ref, width) in enumerate(((u, WIDE), (f, HALF), (d, HALF))):
+        begin = (nx - width) * (1 - level)
+        copies += [
+            pltpu.make_async_copy(ref.at[:, pl.ds(start, ROWS), :], rows.at[n], arrived.at[2 * n]),
+            pltpu.make_async_copy(ref.at[pl.ds(begin, width)], planes.at[n, :width], arrived.at[2 * n + 1]),
+        ]
     for copy in copies:
         copy.start()
-    for n, copy in enumerate(copies):
-        copy.wait()
+    at = 0
+    for n, width in enumerate((WIDE, HALF, HALF)):
+        copies[2 * n].wait()
+        copies[2 * n + 1].wait()
         for c in range(2):
-            out[n * nx : (n + 1) * nx, c] = rows[n, :, :, c * 128 : (c + 1) * 128]
-
-
-def pack_planes_kernel(u, f, d, halo, to_high, to_low):
-    nx, ny, _ = u.shape
-    at = 0
-    for n, (ref, width) in enumerate(((u, WIDE), (f, HALF), (d, HALF))):
-        for out, start in ((to_high, nx - width), (to_low, 0)):
-            for c in range(2):
-                lanes = slice(c * 128, (c + 1) * 128)
-                outer = halo[n * nx + start : n * nx + start + width, c]
-                out[at : at + width, c, :ROWS] = by_level(outer, ref[start : start + width, ny - ROWS :, lanes])
-                out[at : at + width, c, ROWS:] = by_level(ref[start : start + width, :ROWS, lanes], outer)
+            lanes = slice(c * 128, (c + 1) * 128)
+            rows_out[n * nx : (n + 1) * nx, c] = rows[n, :, :, lanes]
+            planes_out[at : at + width, c] = planes[n, :width, :, lanes]
         at += width
+
+
+def pack_corners_kernel(mine, theirs, out):
+    width, _, ny, _ = mine.shape
+    for n, planes in enumerate((by_level(mine[...], theirs[...]), by_level(theirs[...], mine[...]))):
+        out[n * width : (n + 1) * width] = by_level(planes[:, :, ny - ROWS :], planes[:, :, :ROWS])
 
 
 def pack_vector_kernel(basis, halo, dots, to_high, to_low):
@@ -240,10 +243,16 @@
         body(WIDE + nx - 1 - j, above if j < 0 else None)
 
 
-def put(row, index, values):
+def put(row, entries):
     lane = lax.broadcasted_iota(jnp.int32, row.shape, 1)
-    high, low = split_sum(values)
-    return jnp.where(lane == index, high, jnp.where(lane == index + LOW_AT, low, row))
+    most = functools.reduce(jnp.maximum, [jnp.abs(half) for _, halves_ in entries for half in halves_])
+    unit = (8.0 * most.size) * jnp.max(most, keepdims=True)
+    for at, pair in entries:
+        rounded = [(half + unit) - unit for half in pair]
+        high = jnp.sum(rounded[0] + rounded[1], keepdims=True)
+        low = jnp.sum((pair[0] - rounded[0]) + (pair[1] - rounded[1]), keepdims=True)
+        row = jnp.where(lane == at, high, jnp.where(lane == at + LOW_AT, low, row))
+    return row
 
 
 def clear_margins(refs):
@@ -339,11 +348,14 @@
     _, nx, _, ny, _ = basis.shape
     level = lax.axis_index("level")
     at = 0
+    corner = WIDE + 2 * HALF
     for width, dst in ((WIDE, wide_u), (HALF, va), (HALF, scale)):
-        for (xlow, xhigh), place in ((mine, level), (theirs, 1 - level)):
-            _, part = row_spans(place, ny)
-            dst[WIDE - width : WIDE, :, part] = xlow[at : at + width]
-            dst[WIDE + nx : WIDE + nx + width, :, part] = xhigh[at : at + width]
+        for (planes, corners), place in ((mine, level), (theirs, 1 - level)):
+            outer, _ = row_spans(place, ny)
+            begin = WIDE - width + place * (nx + width)
+            dst[pl.ds(begin, width), :, OWN : OWN + ny] = planes[at : at + width]
+            dst[WIDE - width : WIDE, :, outer] = corners[at : at + width]
+            dst[WIDE + nx : WIDE + nx + width, :, outer] = corners[corner + at : corner + at + width]
         at += width
     over = lambda halo, skip, body: over_wedges(nx, halo, skip, body)
     first_steps(ny, wide_u, va, vb, scale, basis, over)
@@ -353,6 +365,7 @@
 def first_dots_kernel(u, basis, dots):
     count, nx, _, ny, _ = basis.shape
     row = jnp.zeros((8, 128), jnp.float32)
+    entries = []
     for k in range(count):
 
         def body(i, sums, k=k):
@@ -374,9 +387,8 @@
         zero = jnp.zeros((ny, 128), jnp.float32)
         sums = lax.fori_loop(0, nx, body, ((zero, zero),) * (4 if k > 1 else 3), unroll=4)
         where = (FIELD_AT + 1 + k, 2 * k, FIELD_AT if k == 0 else 2 * k - 1, CHECK_AT + k - 1)
-        for at, (a, b) in zip(where, sums):
-            row = put(row, at, jnp.concatenate([a, b], axis=0))
-    dots[...] = row
+        entries += zip(where, sums)
+    dots[...] = put(row, entries)
 
 
 def second_step(j, ny, va, vb, scale, pull, u, first, basis):
@@ -438,7 +450,7 @@
         va[WIDE - HALF : WIDE, :, part] = xlow[...]
         va[WIDE + nx : WIDE + nx + HALF, :, part] = xhigh[...]
     pull = row_mask(ny) * (2.0 / RADIUS * DIFFUSION)
-    row = before[...]
+    entries = []
     for j in range(HALF):
         body, count = second_step(j, ny, va, vb, scale, pull, u, first, basis)
         made = [tuple(tuple(sums[j, n, c] for c in range(2)) for n in range(count))]
@@ -449,8 +461,8 @@
         over_wedges(nx, HALF - 1 - j, j + 1, run)
         k = HALF + j
         where = (2 * k + 1, CHECK_AT + k, 2 * k + 2, FIELD_AT + 2 + k)
-        for at, (a, b) in zip(where, made[0]):
-            row = put(row, at, jnp.concatenate([a, b], axis=0))
+        entries += zip(where, made[0])
+    row = put(before[...], entries)
     dots[...] = jnp.broadcast_to(row[0:1], dots.shape)
 
 
@@ -489,10 +501,12 @@
 def call(kernel, outs, args, limit=16 << 20, flags=(), alias=None, far=0, scratch=()):
     whole = pl.BlockSpec(memory_space=pltpu.VMEM)
     shapes = [jax.ShapeDtypeStruct(s, jnp.float32) for s in outs]
+    near = len(args) - far
+    args = tuple(args[:near]) + tuple(pltpu.with_memory_space_constraint(a, pltpu.HBM) for a in args[near:])
     return pl.pallas_call(
         kernel,
         out_shape=shapes + [jax.ShapeDtypeStruct(s, jnp.int32) for s in flags],
-        in_specs=[whole] * (len(args) - far) + [pl.BlockSpec(memory_space=pltpu.HBM)] * far,
+        in_specs=[whole] * near + [pl.BlockSpec(memory_space=pltpu.HBM)] * far,
         scratch_shapes=scratch,
         out_specs=[whole] * len(outs) + [pl.BlockSpec(memory_space=pltpu.SMEM)] * len(flags),
         input_output_aliases=alias or {},
@@ -548,14 +562,15 @@
         extra = 0.5 * stencil(fresh - lower, damping)
         return fresh, solve(upper + source + extra, upper, damping)
 
-    lower, upper = lax.fori_loop(0, STEPS, body, (init_field, init_field))
+    begin = jnp.minimum(init_field, jnp.finfo(jnp.float32).max)
+    lower, upper = lax.fori_loop(0, STEPS, body, (begin, begin))
     return jnp.where(lax.axis_index("level") == 1, upper, lower)
 
 
-def along_rows(block):
-    size = lax.axis_size("yz")
+def shifted(block, axis):
+    size = lax.axis_size(axis)
     route = [(i, i + 1) for i in range(size - 1)] + [(size + i + 1, size + i) for i in range(size - 1)]
-    return lax.ppermute(block, ("level", "yz"), route)
+    return lax.ppermute(block, ("level", axis), route)
 
 
 def swapped(block):
@@ -565,28 +580,35 @@
 def per_device(u, f, d):
     nx, ny, nz = u.shape
     tall = 2 * ROWS + ny
-    (edge,) = call(
-        pack_rows_kernel,
-        [(3 * nx, 2, ROWS, 128)],
+    deep = WIDE + 2 * HALF
+    rows, planes = call(
+        pack_first_kernel,
+        [(3 * nx, 2, ROWS, 128), (deep, 2, ny, 128)],
         (u, f, d),
         far=3,
-        scratch=[pltpu.VMEM((3, nx, ROWS, nz), jnp.float32), pltpu.SemaphoreType.DMA((3,))],
+        scratch=[
+            pltpu.VMEM((3, nx, ROWS, nz), jnp.float32),
+            pltpu.VMEM((3, WIDE, ny, nz), jnp.float32),
+            pltpu.SemaphoreType.DMA((6,)),
+        ],
     )
-    halo = along_rows(edge)
-    planes = (WIDE + 2 * HALF, 2, 2 * ROWS, 128)
-    ups, downs = call(pack_planes_kernel, [planes] * 2, (u, f, d, halo))
+    planes = shifted(planes, "gx")
+    halo = shifted(rows, "yz")
+    others = swapped(planes)
+    (corners,) = call(pack_corners_kernel, [(2 * deep, 2, ROWS, 128)], (planes, others))
+    corners = shifted(corners, "yz")
     theirs = swapped(halo)
     wide = (nx + 2 * WIDE, 2, tall + 2 * PAD, 128)
     block = (nx, 2, ny, 128)
-    mine = both_ways(ups, downs, "gx")
+    opposite = swapped(corners)
     buffers = call(first_inner_kernel, [wide] * 4 + [(HALF + 1,) + block], (u, f, d, halo, theirs))
     *_, scale, first, edge = call(
         first_outer_kernel,
         [wide] * 4 + [(HALF + 1,) + block, (nx, 2, ROWS, 128)],
-        mine + tuple(swapped(part) for part in mine) + tuple(buffers),
+        (planes, corners, others, opposite) + tuple(buffers),
         alias={4 + n: n for n in range(5)},
     )
-    halo = along_rows(edge)
+    halo = shifted(edge, "yz")
     theirs = swapped(halo)
     (dots,) = call(first_dots_kernel, [(8, 128)], (u, first))
     ups, downs = call(pack_vector_kernel, [(HALF, 2, 2 * ROWS, 128)] * 2, (first, halo, dots))

time: 113 us -> 104 us (0.920)
  waiting for transfers between devices: 41.9 us -> 33.7 us
  starting transfers between devices: 34.2 us -> 41 us
  Pallas kernels: 31.6 us -> 26.5 us
  local copies, waits for them, and re-layouts: 3.2 us -> 0.03 us
    ppermute x2 -> x4, starting transfers between devices: 6.97 us -> 13.9 us  [shifted(): return lax.ppermute(block, ('level', axis), route)]
    ppermute x2 -> x1, waiting for transfers between devices: 7.35 us -> 1.4 us  [both_ways(): high = lax.ppermute(up, axis, route)]
    pallas_call x9, Pallas kernels: 31.6 us -> 26.5 us  [call(): pl.pallas_call(kernel, out_shape=shapes + [jax.ShapeDtypeStruct(s, jnp.in...]
    all_to_all x1, starting transfers between devices: 17.9 us -> 22.4 us  [per_device(): lax.all_to_all(dots.reshape(parts, 1, 128), AXES, 0, 0).reshape(parts, 128)]
    ppermute x2 -> x1, waiting for transfers between devices: 8.24 us -> 4.11 us  [both_ways(): low = lax.ppermute(down, axis, [(b, a) for a, b in route])]
    ppermute x2 -> x1, starting transfers between devices: 6.8 us -> 3.4 us  [both_ways(): high = lax.ppermute(up, axis, route)]
    unnamed x17 -> x14, local copies, waits for them, and re-layouts: 3.2 us -> 0.03 us
    ppermute x2 -> x4, waiting for transfers between devices: 15.2 us -> 17 us  [shifted(): return lax.ppermute(block, ('level', axis), route)]
  transfers between devices with their start and end apart: 13 -> 13, of which waited for: 7 -> 7; matrix products, arithmetic and copies ran while one was open for 0% -> 0% of each run, Pallas kernels for 18% -> 17%
where the time goes in v5:
time: 104 us; the launch traced here: 102 us
  starting transfers between devices  41 us (39%)
  waiting for transfers between devices  33.7 us (32%)
  Pallas kernels  26.5 us (25%)
    pallas_call x9, Pallas kernels, call(): pl.pallas_call(kernel, out_shape=shapes + [jax.ShapeDtypeStruct(s, jnp.in...  26.5 us
    all_to_all x1, starting transfers between devices, per_device(): lax.all_to_all(dots.reshape(parts, 1, 128), AXES, 0, 0).reshape(parts, 128)  22.4 us
    ppermute x4, waiting for transfers between devices, shifted(): return lax.ppermute(block, ('level', axis), route)  17 us
    ppermute x4, starting transfers between devices, shifted(): return lax.ppermute(block, ('level', axis), route)  13.9 us
    all_to_all x1, waiting for transfers between devices, per_device(): lax.all_to_all(dots.reshape(parts, 1, 128), AXES, 0, 0).reshape(parts, 128)  11.1 us
    ppermute x1, waiting for transfers between devices, both_ways(): low = lax.ppermute(down, axis, [(b, a) for a, b in route])  4.11 us
    ppermute x1, starting transfers between devices, both_ways(): high = lax.ppermute(up, axis, route)  3.4 us
  transfers between devices with their start and end apart: 13, of which 7 were waited for; matrix products, arithmetic and copies ran while one was open for 0% of the time, Pallas kernels for 17%

profile of v5, /device:TPU:8, one launch (start us, length us, event | category | flops | bytes accessed | tf_op | source)
XLA Modules:
  0.0 102.4 jit_solution(15274515542643422994)
XLA Ops:
  0.0 1.4 %shard_map.57 = (f32[96,2,8,128]{3,2,1,0:T(8,128)S(1)}, f32[19,2,16,128]{3,2,1,0:T(8,128)S(1)}) custom-call(f32[32,16,256]{2,1,0:T(8,128)} %far_u.1, f32[32,16,256]{2,1,0:T(8,128)} %f.3, f32[32,16,256]{2,1,0:T(8,128)} %d.3), custom_call_target="tpu_custom_call" | custom-call | tf_op jit(solution)/shard_map/pallas_call | solution.py:506
  1.4 3.5 %collective-permute-start.24 = (f32[96,2,8,128]{3,2,1,0:T(8,128)S(1)}, f32[96,2,8,128]{3,2,1,0:T(8,128)S(1)}, u32[]{:S(2)}, u32[]{:S(2)}) collective-permute-start(f32[96,2,8,128]{3,2,1,0:T(8,128)S(1)} %get-tuple-element.133), channel_id=1, source_target_pairs={{0,1},{1,2},{2,3},{3,4},{4,5},{5,6},{6,7},{7,8},{8,9},{9,10},{10,1... | collective-permute-start | bytes 2359304 | tf_op jit(solution)/shard_map/ppermute | solution.py:573
  4.9 3.4 %collective-permute-start.20 = (f32[19,2,16,128]{3,2,1,0:T(8,128)S(1)}, f32[19,2,16,128]{3,2,1,0:T(8,128)S(1)}, u32[]{:S(2)}, u32[]{:S(2)}) collective-permute-start(f32[19,2,16,128]{3,2,1,0:T(8,128)S(1)} %get-tuple-element.132), channel_id=1, source_target_pairs={{0,32},{32,64},{64,96},{160,128},{192,160},{224,192},{1,33},{33,65... | collective-permute-start | bytes 933896 | tf_op jit(solution)/shard_map/ppermute | solution.py:573
  8.3 4.4 %collective-permute-done.20.mine.refs_0_ = f32[19,2,16,128]{3,2,1,0:T(8,128)S(1)} collective-permute-done((f32[19,2,16,128]{3,2,1,0:T(8,128)S(1)}, f32[19,2,16,128]{3,2,1,0:T(8,128)S(1)}, u32[]{:S(2)}, u32[]{:S(2)}) %collective-permute-start.20) | collective-permute-done | bytes 311328 | tf_op jit(solution)/shard_map/ppermute | solution.py:573
  12.7 2.6 %collective-permute-done.24.mine = f32[96,2,8,128]{3,2,1,0:T(8,128)S(1)} collective-permute-done((f32[96,2,8,128]{3,2,1,0:T(8,128)S(1)}, f32[96,2,8,128]{3,2,1,0:T(8,128)S(1)}, u32[]{:S(2)}, u32[]{:S(2)}) %collective-permute-start.24) | collective-permute-done | bytes 786464 | tf_op jit(solution)/shard_map/ppermute | solution.py:573
  15.3 0.1 shard_map.58
  15.4 3.5 %collective-permute-start.22 = (f32[38,2,8,128]{3,2,1,0:T(8,128)S(1)}, f32[38,2,8,128]{3,2,1,0:T(8,128)S(1)}, u32[]{:S(2)}, u32[]{:S(2)}) collective-permute-start(f32[38,2,8,128]{3,2,1,0:T(8,128)S(1)} %shard_map.58), channel_id=1, source_target_pairs={{0,1},{1,2},{2,3},{3,4},{4,5},{5,6},{6,7},{7,8},{8,9},{9,10},{10,1... | collective-permute-start | bytes 933896 | tf_op jit(solution)/shard_map/ppermute | solution.py:573
  18.9 5.3 %collective-permute-done.22.refs_1_ = f32[38,2,8,128]{3,2,1,0:T(8,128)S(1)} collective-permute-done((f32[38,2,8,128]{3,2,1,0:T(8,128)S(1)}, f32[38,2,8,128]{3,2,1,0:T(8,128)S(1)}, u32[]{:S(2)}, u32[]{:S(2)}) %collective-permute-start.22) | collective-permute-done | bytes 311328 | tf_op jit(solution)/shard_map/ppermute | solution.py:573
  24.2 0.0 collective-permute-start.23
  24.2 0.0 collective-permute-done.25.theirs
  24.2 8.0 %shard_map.59 = (f32[46,2,48,128]{3,2,1,0:T(8,128)S(1)}, f32[46,2,48,128]{3,2,1,0:T(8,128)S(1)}, f32[46,2,48,128]{3,2,1,0:T(8,128)S(1)}, f32[46,2,48,128]{3,2,1,0:T(8,128)S(1)}, f32[7,32,2,16,128]{4,3,2,1,0:T(8,128)S(1)}) custom-call(f32[32,16,256]{2,1,0:T(8,128)S(1)} %copy-done.10, f32[32,16,256]{2,1,0:T(8,128)S(1)} %copy-done.7, ...), custom_call_target="tpu_custom_call" | custom-call | tf_op jit(solution)/shard_map/pallas_call | solution.py:506
  32.3 1.8 %shard_map.60 = (f32[46,2,48,128]{3,2,1,0:T(8,128)S(1)}, f32[46,2,48,128]{3,2,1,0:T(8,128)S(1)}, f32[46,2,48,128]{3,2,1,0:T(8,128)S(1)}, f32[46,2,48,128]{3,2,1,...) custom-call(f32[19,2,16,128]{3,2,1,0:T(8,128)S(1)} %collective-permu, ...), custom_call_target="tpu_custom_call", output_to_operand_aliasing={{0}: (4, {}), {1}: (5, {}), {2}: (6, {}), {3}: (7, {}), {4}... | custom-call | tf_op jit(solution)/shard_map/pallas_call | solution.py:506
  34.1 3.5 %collective-permute-start.26 = (f32[32,2,8,128]{3,2,1,0:T(8,128)S(1)}, f32[32,2,8,128]{3,2,1,0:T(8,128)S(1)}, u32[]{:S(2)}, u32[]{:S(2)}) collective-permute-start(f32[32,2,8,128]{3,2,1,0:T(8,128)S(1)} %get-tuple-element.140), channel_id=1, source_target_pairs={{0,1},{1,2},{2,3},{3,4},{4,5},{5,6},{6,7},{7,8},{8,9},{9,10},{10,1... | collective-permute-start | bytes 786440 | tf_op jit(solution)/shard_map/ppermute | solution.py:573
  37.6 4.8 %collective-permute-done.26.halo.mine = f32[32,2,8,128]{3,2,1,0:T(8,128)S(1)} collective-permute-done((f32[32,2,8,128]{3,2,1,0:T(8,128)S(1)}, f32[32,2,8,128]{3,2,1,0:T(8,128)S(1)}, u32[]{:S(2)}, u32[]{:S(2)}) %collective-permute-start.26) | collective-permute-done | bytes 262176 | tf_op jit(solution)/shard_map/ppermute | solution.py:573
  42.4 0.0 collective-permute-start.31
  42.4 1.6 %shard_map.61.dots.refs_7_ = f32[8,128]{1,0:T(8,128)S(1)} custom-call(f32[32,16,256]{2,1,0:T(8,128)S(1)} %copy-done.10, f32[7,32,2,16,128]{4,3,2,1,0:T(8,128)S(1)} %get-tuple-element.139.basis.first.refs_6_.far_first), custom_call_target="tpu_custom_call" | custom-call | tf_op jit(solution)/shard_map/pallas_call | solution.py:506
  44.0 3.4 %collective-permute-start.27 = (f32[6,2,16,128]{3,2,1,0:T(8,128)S(1)}, f32[6,2,16,128]{3,2,1,0:T(8,128)S(1)}, u32[]{:S(2)}, u32[]{:S(2)}) collective-permute-start(f32[6,2,16,128]{3,2,1,0:T(8,128)S(1)} %get-tuple-element.141), channel_id=1, source_target_pairs={{0,32},{32,64},{64,96},{1,33},{33,65},{65,97},{2,34},{34,66},{66,9... | collective-permute-start | bytes 294920 | tf_op jit(solution)/shard_map/ppermute | solution.py:520
  47.4 1.3 %collective-permute-start.28 = (f32[6,2,16,128]{3,2,1,0:T(8,128)S(1)}, f32[6,2,16,128]{3,2,1,0:T(8,128)S(1)}, u32[]{:S(2)}, u32[]{:S(2)}) collective-permute-start(f32[6,2,16,128]{3,2,1,0:T(8,128)S(1)} %get-tuple-element.142), channel_id=1, source_target_pairs={{32,0},{64,32},{96,64},{33,1},{65,33},{97,65},{34,2},{66,34},{98,6... | collective-permute-start | bytes 294920 | tf_op jit(solution)/shard_map/ppermute | solution.py:521
  48.7 1.4 %collective-permute-done.27.refs_0_ = f32[6,2,16,128]{3,2,1,0:T(8,128)S(1)} collective-permute-done((f32[6,2,16,128]{3,2,1,0:T(8,128)S(1)}, f32[6,2,16,128]{3,2,1,0:T(8,128)S(1)}, u32[]{:S(2)}, u32[]{:S(2)}) %collective-permute-start.27) | collective-permute-done | bytes 98336 | tf_op jit(solution)/shard_map/ppermute | solution.py:520
  50.1 0.0 collective-permute-start.29
  50.1 4.1 %collective-permute-done.28.refs_1_ = f32[6,2,16,128]{3,2,1,0:T(8,128)S(1)} collective-permute-done((f32[6,2,16,128]{3,2,1,0:T(8,128)S(1)}, f32[6,2,16,128]{3,2,1,0:T(8,128)S(1)}, u32[]{:S(2)}, u32[]{:S(2)}) %collective-permute-start.28) | collective-permute-done | bytes 98336 | tf_op jit(solution)/shard_map/ppermute | solution.py:521
  54.2 0.0 collective-permute-start.30
  54.2 0.0 collective-permute-done.31.theirs
  54.2 7.3 %shard_map.63 = (f32[5,32,2,16,128]{4,3,2,1,0:T(8,128)S(1)}, f32[46,2,48,128]{3,2,1,0:T(8,128)S(1)}, f32[46,2,48,128]{3,2,1,0:T(8,128)S(1)}, f32[6,4,2,16,128]{4,3,2,1,0:T(8,128)S(1)}) custom-call(f32[32,2,8,128]{3,2,1,0:T(8,128)S(1)} %collective-permute-done.26.halo.mine, f32[32,2,8,128]{3,2,1,0:T(8,128)S(1)} %collective-permute-done.31.theirs, ...), custom_call_target="tpu_custom_call" | custom-call | tf_op jit(solution)/shard_map/pallas_call | solution.py:506
  61.6 0.0 collective-permute-done.30.refs_3_
  61.6 0.0 copy-start.1
  61.6 0.0 copy-start.2
  61.6 2.6 %shard_map.64 = (f32[5,32,2,16,128]{4,3,2,1,0:T(8,128)S(1)}, f32[46,2,48,128]{3,2,1,0:T(8,128)S(1)}, f32[46,2,48,128]{3,2,1,0:T(8,128)S(1)}, f32[128,128]{1,0:T(8,128)}) custom-call(f32[6,2,16,128]{3,2,1,0:T(8,128)S(1)} %collective-permute-done.27.refs_0_, ...), custom_call_target="tpu_custom_call", output_to_operand_aliasing={{0}: (9, {}), {1}: (10, {}), {2}: (11, {})} | custom-call | tf_op jit(solution)/shard_map/pallas_call | solution.py:506
  64.2 22.4 %all-to-all-start = ((f32[128,1,128]{2,1,0:T(1,128)}), f32[128,1,128]{2,1,0:T(1,128)S(1)}, u32[]{:S(2)}, u32[]{:S(2)}) async-start(f32[128,1,128]{2,1,0:T(1,128)} %bitcast.3), calls=%async_computation | async-start | bytes 131072 | tf_op jit(solution)/shard_map/all_to_all | solution.py:628
  86.6 11.1 %all-to-all-done = f32[128,1,128]{2,1,0:T(1,128)S(1)} async-done(((f32[128,1,128]{2,1,0:T(1,128)}), f32[128,1,128]{2,1,0:T(1,128)S(1)}, u32[]{:S(2)}, u32[]{:S(2)}) %all-to-all-start) | async-done | bytes 65568 | tf_op jit(solution)/shard_map/all_to_all | solution.py:628
  97.8 3.6 %shard_map.65 = (f32[32,16,256]{2,1,0:T(8,128)}, s32[1,1]{1,0:T(1,128)}) custom-call(f32[128,128]{1,0:T(8,128)S(1)} %bitcast.8, f32[128,128]{1,0:T(8,128)S(1)} %copy-done.1, f32[1,128]{1,0:T(1,128)S(1)} %copy-done.2, f32[5,32,2,16,128]{4,3,2,1,0:T(8,128)S(1)} %get-tuple-element.149.second, f32[32,16,256]{2,1,0:T(8,128)} %far_u.1, f32[7,32,2,16,128]{4,3,2,1,0:T(8,128)} %copy-done), custom_call_target="tpu_custom_call" | custom-call | tf_op jit(solution)/shard_map/pallas_call | solution.py:506
  102.0 0.2 conditional.1
  (18 shorter events, 0.1 us)
Async XLA Ops:
  0.0 24.2 %copy-start.10 = (f32[32,16,256]{2,1,0:T(8,128)S(1)}, f32[32,16,256]{2,1,0:T(8,128)}, u32[]{:S(2)}) copy-start(f32[32,16,256]{2,1,0:T(8,128)} %far_u.1) | copy-start | bytes 1572868
  0.0 24.2 %copy-start.7 = (f32[32,16,256]{2,1,0:T(8,128)S(1)}, f32[32,16,256]{2,1,0:T(8,128)}, u32[]{:S(2)}) copy-start(f32[32,16,256]{2,1,0:T(8,128)} %f.3) | copy-start | bytes 1572868
  0.0 24.2 %copy-start.3 = (f32[32,16,256]{2,1,0:T(8,128)S(1)}, f32[32,16,256]{2,1,0:T(8,128)}, u32[]{:S(2)}) copy-start(f32[32,16,256]{2,1,0:T(8,128)} %d.3) | copy-start | bytes 1572868
  1.4 13.9 %collective-permute-start.24 = (f32[96,2,8,128]{3,2,1,0:T(8,128)S(1)}, f32[96,2,8,128]{3,2,1,0:T(8,128)S(1)}, u32[]{:S(2)}, u32[]{:S(2)}) collective-permute-start(f32[96,2,8,128]{3,2,1,0:T(8,128)S(1)} %get-tuple-element.133), channel_id=1, source_target_pairs={{0,1},{1,2},{2,3},{3,4},{4,5},{5,6},{6,7},{7,8},{8,9},{9,10},{10,1... | collective-permute-start | bytes 2359304 | tf_op jit(solution)/shard_map/ppermute | solution.py:573
  4.9 7.8 %collective-permute-start.20 = (f32[19,2,16,128]{3,2,1,0:T(8,128)S(1)}, f32[19,2,16,128]{3,2,1,0:T(8,128)S(1)}, u32[]{:S(2)}, u32[]{:S(2)}) collective-permute-start(f32[19,2,16,128]{3,2,1,0:T(8,128)S(1)} %get-tuple-element.132), channel_id=1, source_target_pairs={{0,32},{32,64},{64,96},{160,128},{192,160},{224,192},{1,33},{33,65... | collective-permute-start | bytes 933896 | tf_op jit(solution)/shard_map/ppermute | solution.py:573
  12.7 2.6 %collective-permute-start.21 = (f32[19,2,16,128]{3,2,1,0:T(8,128)S(1)}, f32[19,2,16,128]{3,2,1,0:T(8,128)S(1)}, u32[]{:S(2)}, u32[]{:S(2)}) collective-permute-start(f32[19,2,16,128]{3,2,1,0:T(8,128)S(1)} %collective-permute-done.20.mine.refs_0_), channel_id=1, source_target_pairs={{0,128},{128,0},{1,129},{129,1},{2,130},{130,2},{3,131},{131,3},{4... | collective-permute-start | bytes 933896 | tf_op jit(solution)/shard_map/ppermute | solution.py:577
  15.3 8.9 %collective-permute-start.25 = (f32[96,2,8,128]{3,2,1,0:T(8,128)S(1)}, f32[96,2,8,128]{3,2,1,0:T(8,128)S(1)}, u32[]{:S(2)}, u32[]{:S(2)}) collective-permute-start(f32[96,2,8,128]{3,2,1,0:T(8,128)S(1)} %collective-permute-done.24.mine), channel_id=1, source_target_pairs={{0,128},{128,0},{1,129},{129,1},{2,130},{130,2},{3,131},{131,3},{4... | collective-permute-start | bytes 2359304 | tf_op jit(solution)/shard_map/ppermute | solution.py:577
  15.4 8.8 %collective-permute-start.22 = (f32[38,2,8,128]{3,2,1,0:T(8,128)S(1)}, f32[38,2,8,128]{3,2,1,0:T(8,128)S(1)}, u32[]{:S(2)}, u32[]{:S(2)}) collective-permute-start(f32[38,2,8,128]{3,2,1,0:T(8,128)S(1)} %shard_map.58), channel_id=1, source_target_pairs={{0,1},{1,2},{2,3},{3,4},{4,5},{5,6},{6,7},{7,8},{8,9},{9,10},{10,1... | collective-permute-start | bytes 933896 | tf_op jit(solution)/shard_map/ppermute | solution.py:573
  24.2 8.1 %collective-permute-start.23 = (f32[38,2,8,128]{3,2,1,0:T(8,128)S(1)}, f32[38,2,8,128]{3,2,1,0:T(8,128)S(1)}, u32[]{:S(2)}, u32[]{:S(2)}) collective-permute-start(f32[38,2,8,128]{3,2,1,0:T(8,128)S(1)} %collective-permute-done.22.refs_1_), channel_id=1, source_target_pairs={{0,128},{128,0},{1,129},{129,1},{2,130},{130,2},{3,131},{131,3},{4... | collective-permute-start | bytes 933896 | tf_op jit(solution)/shard_map/ppermute | solution.py:577
  34.1 27.5 %copy-start = (f32[7,32,2,16,128]{4,3,2,1,0:T(8,128)}, f32[7,32,2,16,128]{4,3,2,1,0:T(8,128)S(1)}, u32[]{:S(2)}) copy-start(f32[7,32,2,16,128]{4,3,2,1,0:T(8,128)S(1)} %get-tuple-element.139.basis.first.refs_6_.far_first) | copy-start | bytes 11010052
  34.1 8.3 %collective-permute-start.26 = (f32[32,2,8,128]{3,2,1,0:T(8,128)S(1)}, f32[32,2,8,128]{3,2,1,0:T(8,128)S(1)}, u32[]{:S(2)}, u32[]{:S(2)}) collective-permute-start(f32[32,2,8,128]{3,2,1,0:T(8,128)S(1)} %get-tuple-element.140), channel_id=1, source_target_pairs={{0,1},{1,2},{2,3},{3,4},{4,5},{5,6},{6,7},{7,8},{8,9},{9,10},{10,1... | collective-permute-start | bytes 786440 | tf_op jit(solution)/shard_map/ppermute | solution.py:573
  42.4 11.9 %collective-permute-start.31 = (f32[32,2,8,128]{3,2,1,0:T(8,128)S(1)}, f32[32,2,8,128]{3,2,1,0:T(8,128)S(1)}, u32[]{:S(2)}, u32[]{:S(2)}) collective-permute-start(f32[32,2,8,128]{3,2,1,0:T(8,128)S(1)} %collective-permute-done.26.halo.mine), channel_id=1, source_target_pairs={{0,128},{128,0},{1,129},{129,1},{2,130},{130,2},{3,131},{131,3},{4... | collective-permute-start | bytes 786440 | tf_op jit(solution)/shard_map/ppermute | solution.py:577
  44.0 6.1 %collective-permute-start.27 = (f32[6,2,16,128]{3,2,1,0:T(8,128)S(1)}, f32[6,2,16,128]{3,2,1,0:T(8,128)S(1)}, u32[]{:S(2)}, u32[]{:S(2)}) collective-permute-start(f32[6,2,16,128]{3,2,1,0:T(8,128)S(1)} %get-tuple-element.141), channel_id=1, source_target_pairs={{0,32},{32,64},{64,96},{1,33},{33,65},{65,97},{2,34},{34,66},{66,9... | collective-permute-start | bytes 294920 | tf_op jit(solution)/shard_map/ppermute | solution.py:520
  47.4 6.8 %collective-permute-start.28 = (f32[6,2,16,128]{3,2,1,0:T(8,128)S(1)}, f32[6,2,16,128]{3,2,1,0:T(8,128)S(1)}, u32[]{:S(2)}, u32[]{:S(2)}) collective-permute-start(f32[6,2,16,128]{3,2,1,0:T(8,128)S(1)} %get-tuple-element.142), channel_id=1, source_target_pairs={{32,0},{64,32},{96,64},{33,1},{65,33},{97,65},{34,2},{66,34},{98,6... | collective-permute-start | bytes 294920 | tf_op jit(solution)/shard_map/ppermute | solution.py:521
  50.1 11.5 %collective-permute-start.29 = (f32[6,2,16,128]{3,2,1,0:T(8,128)S(1)}, f32[6,2,16,128]{3,2,1,0:T(8,128)S(1)}, u32[]{:S(2)}, u32[]{:S(2)}) collective-permute-start(f32[6,2,16,128]{3,2,1,0:T(8,128)S(1)} %collective-permute-done.27.refs_0_), channel_id=1, source_target_pairs={{0,128},{128,0},{1,129},{129,1},{2,130},{130,2},{3,131},{131,3},{4... | collective-permute-start | bytes 294920 | tf_op jit(solution)/shard_map/ppermute | solution.py:577
  54.2 7.4 %collective-permute-start.30 = (f32[6,2,16,128]{3,2,1,0:T(8,128)S(1)}, f32[6,2,16,128]{3,2,1,0:T(8,128)S(1)}, u32[]{:S(2)}, u32[]{:S(2)}) collective-permute-start(f32[6,2,16,128]{3,2,1,0:T(8,128)S(1)} %collective-permute-done.28.refs_1_), channel_id=1, source_target_pairs={{0,128},{128,0},{1,129},{129,1},{2,130},{130,2},{3,131},{131,3},{4... | collective-permute-start | bytes 294920 | tf_op jit(solution)/shard_map/ppermute | solution.py:577
  61.6 36.1 %copy-start.1 = (f32[128,128]{1,0:T(8,128)S(1)}, f32[128,128]{1,0:T(8,128)}, u32[]{:S(2)}) copy-start(f32[128,128]{1,0:T(8,128)} %constant.50.clone.tables) | copy-start | bytes 196612
  61.6 36.1 %copy-start.2 = (f32[1,128]{1,0:T(1,128)S(1)}, f32[1,128]{1,0:T(1,128)}, u32[]{:S(2)}) copy-start(f32[1,128]{1,0:T(1,128)} %constant.51.clone.nodes) | copy-start | bytes 1540
  64.2 33.5 %all-to-all-start = ((f32[128,1,128]{2,1,0:T(1,128)}), f32[128,1,128]{2,1,0:T(1,128)S(1)}, u32[]{:S(2)}, u32[]{:S(2)}) async-start(f32[128,1,128]{2,1,0:T(1,128)} %bitcast.3), calls=%async_computation | async-start | bytes 131072 | tf_op jit(solution)/shard_map/all_to_all | solution.py:628
  97.7 4.3 %copy-start.11 = (f32[32,16,256]{2,1,0:T(8,128)S(1)}, f32[32,16,256]{2,1,0:T(8,128)}, u32[]{:S(2)}) copy-start(f32[32,16,256]{2,1,0:T(8,128)} %far_u.1) | copy-start | bytes 1572868

commit v6 on v5

--- a/solution.py
+++ b/solution.py
@@ -18,6 +18,7 @@
 NODES = 128
 WIDE = HALF + 1
 ROWS = 8
+FIRST_CUT, SECOND_CUT = 2, 2
 NOISE_GAIN = 4.0
 ERROR_BOUND = 4e-5
 
@@ -186,19 +187,8 @@
         out[n * width : (n + 1) * width] = by_level(planes[:, :, ny - ROWS :], planes[:, :, :ROWS])
 
 
-def pack_vector_kernel(basis, halo, dots, to_high, to_low):
-    _, nx, _, ny, _ = basis.shape
-    for out, start in ((to_high, nx - HALF), (to_low, 0)):
-        outer = halo[start : start + HALF]
-        own = slice(start, start + HALF)
-        out[:, :, :ROWS] = by_level(outer, basis[HALF, own, :, ny - ROWS :])
-        out[:, :, ROWS:] = by_level(basis[HALF, own, :, :ROWS], outer)
-
-
-def row_spans(level, ny):
-    halo = pl.multiple_of(PAD + level * (ROWS + ny), 8)
-    half = pl.multiple_of(PAD + level * (2 * ROWS), 8)
-    return pl.ds(halo, ROWS), pl.ds(half, 2 * ROWS)
+def row_span(level, ny):
+    return pl.ds(pl.multiple_of(PAD + level * (ROWS + ny), 8), ROWS)
 
 
 def beside(ref, i, start, count):
@@ -304,7 +294,7 @@
     return body
 
 
-def first_steps(ny, wide_u, va, vb, scale, basis, over):
+def first_steps(ny, wide_u, va, vb, scale, basis, over, steps=range(HALF + 1)):
     pull = row_mask(ny) * (2.0 / RADIUS * DIFFUSION)
     rows = (PAD, ny + 2 * ROWS)
     begin = first_start(wide_u, va, scale, ny)
@@ -314,8 +304,11 @@
         if mask is None:
             basis[0, i - WIDE] = va[i, :, OWN : OWN + ny]
 
-    over(HALF, 1, start)
+    if 0 in steps:
+        over(HALF, 1, start)
     for k in range(HALF):
+        if k + 1 not in steps:
+            continue
         src, dst = (va, vb) if k % 2 == 0 else (vb, va)
         last = k == HALF - 1
         step = recur(src, dst, scale, pull, k == 0, (OWN, ny) if last else rows)
@@ -335,23 +328,31 @@
     clear_margins((wide_u, va, vb))
     for n, (ref, dst) in enumerate(((u, wide_u), (f, va), (d, scale))):
         for halo, place in ((mine, level), (theirs, 1 - level)):
-            outer, _ = row_spans(place, ny)
+            outer = row_span(place, ny)
             dst[WIDE : WIDE + nx, :, outer] = halo[n * nx : (n + 1) * nx]
         for c in range(2):
             dst[WIDE : WIDE + nx, c, OWN : OWN + ny] = ref[:, :, c * 128 : (c + 1) * 128]
-    first_steps(ny, wide_u, va, vb, scale, basis, lambda halo, skip, body: over_inner(nx, skip, body))
+    over = lambda halo, skip, body: over_inner(nx, skip, body)
+    first_steps(ny, wide_u, va, vb, scale, basis, over, range(FIRST_CUT))
+
+
+def first_rest_kernel(*refs):
+    wide_u, va, vb, scale, basis = refs[5:]
+    _, nx, _, ny, _ = basis.shape
+    over = lambda halo, skip, body: over_inner(nx, skip, body)
+    first_steps(ny, wide_u, va, vb, scale, basis, over, range(FIRST_CUT, HALF + 1))
 
 
 def first_outer_kernel(*refs):
     mine, theirs = refs[:2], refs[2:4]
-    wide_u, va, vb, scale, basis, edge = refs[9:]
+    wide_u, va, vb, scale, basis, edge_rows, edge_planes = refs[9:]
     _, nx, _, ny, _ = basis.shape
     level = lax.axis_index("level")
     at = 0
     corner = WIDE + 2 * HALF
     for width, dst in ((WIDE, wide_u), (HALF, va), (HALF, scale)):
         for (planes, corners), place in ((mine, level), (theirs, 1 - level)):
-            outer, _ = row_spans(place, ny)
+            outer = row_span(place, ny)
             begin = WIDE - width + place * (nx + width)
             dst[pl.ds(begin, width), :, OWN : OWN + ny] = planes[at : at + width]
             dst[WIDE - width : WIDE, :, outer] = corners[at : at + width]
@@ -359,7 +360,8 @@
         at += width
     over = lambda halo, skip, body: over_wedges(nx, halo, skip, body)
     first_steps(ny, wide_u, va, vb, scale, basis, over)
-    edge[...] = by_level(basis[HALF, :, :, ny - ROWS :, :], basis[HALF, :, :, :ROWS, :])
+    edge_rows[...] = by_level(basis[HALF, :, :, ny - ROWS :, :], basis[HALF, :, :, :ROWS, :])
+    edge_planes[...] = by_level(basis[HALF, nx - HALF :], basis[HALF, :HALF])
 
 
 def first_dots_kernel(u, basis, dots):
@@ -423,11 +425,20 @@
     level = lax.axis_index("level")
     clear_margins((va, vb))
     for halo, place in ((mine, level), (theirs, 1 - level)):
-        outer, _ = row_spans(place, ny)
+        outer = row_span(place, ny)
         va[WIDE : WIDE + nx, :, outer] = halo[...]
     va[WIDE : WIDE + nx, :, OWN : OWN + ny] = first[HALF]
+    second_inner_steps(range(SECOND_CUT), scale, u, first, basis, va, vb, sums)
+
+
+def second_rest_kernel(scale, u, first, *refs):
+    second_inner_steps(range(SECOND_CUT, HALF), scale, u, first, *refs[4:])
+
+
+def second_inner_steps(steps, scale, u, first, basis, va, vb, sums):
+    _, nx, _, ny, _ = basis.shape
     pull = row_mask(ny) * (2.0 / RADIUS * DIFFUSION)
-    for j in range(HALF):
+    for j in steps:
         body, count = second_step(j, ny, va, vb, scale, pull, u, first, basis)
         zero = jnp.zeros((ny, 128), jnp.float32)
         low, high = WIDE + j + 1, WIDE + nx - j - 1
@@ -445,10 +456,11 @@
     basis, va, vb, dots = refs[12:]
     _, nx, _, ny, _ = basis.shape
     level = lax.axis_index("level")
-    for (xlow, xhigh), place in ((mine, level), (theirs, 1 - level)):
-        _, part = row_spans(place, ny)
-        va[WIDE - HALF : WIDE, :, part] = xlow[...]
-        va[WIDE + nx : WIDE + nx + HALF, :, part] = xhigh[...]
+    for (planes, corners), place in ((mine, level), (theirs, 1 - level)):
+        outer = row_span(place, ny)
+        va[pl.ds(WIDE - HALF + place * (nx + HALF), HALF), :, OWN : OWN + ny] = planes[...]
+        va[WIDE - HALF : WIDE, :, outer] = corners[:HALF]
+        va[WIDE + nx : WIDE + nx + HALF, :, outer] = corners[HALF:]
     pull = row_mask(ny) * (2.0 / RADIUS * DIFFUSION)
     entries = []
     for j in range(HALF):
@@ -577,6 +589,18 @@
     return lax.ppermute(block, "level", [(0, 1), (1, 0)])
 
 
+def exchange(rows, planes):
+    planes = shifted(planes, "gx")
+    halo = shifted(rows, "yz")
+    others = swapped(planes)
+    width = planes.shape[0]
+    (corners,) = call(pack_corners_kernel, [(2 * width, 2, ROWS, 128)], (planes, others))
+    corners = shifted(corners, "yz")
+    theirs = swapped(halo)
+    opposite = swapped(corners)
+    return halo, theirs, (planes, corners, others, opposite)
+
+
 def per_device(u, f, d):
     nx, ny, nz = u.shape
     tall = 2 * ROWS + ny
@@ -592,37 +616,33 @@
             pltpu.SemaphoreType.DMA((6,)),
         ],
     )
-    planes = shifted(planes, "gx")
-    halo = shifted(rows, "yz")
-    others = swapped(planes)
-    (corners,) = call(pack_corners_kernel, [(2 * deep, 2, ROWS, 128)], (planes, others))
-    corners = shifted(corners, "yz")
-    theirs = swapped(halo)
+    halo, theirs, outside = exchange(rows, planes)
     wide = (nx + 2 * WIDE, 2, tall + 2 * PAD, 128)
     block = (nx, 2, ny, 128)
-    opposite = swapped(corners)
     buffers = call(first_inner_kernel, [wide] * 4 + [(HALF + 1,) + block], (u, f, d, halo, theirs))
-    *_, scale, first, edge = call(
+    shapes = [b.shape for b in buffers]
+    buffers = call(first_rest_kernel, shapes, buffers, alias={n: n for n in range(5)})
+    *_, scale, first, rows, planes = call(
         first_outer_kernel,
-        [wide] * 4 + [(HALF + 1,) + block, (nx, 2, ROWS, 128)],
-        (planes, corners, others, opposite) + tuple(buffers),
+        [wide] * 4 + [(HALF + 1,) + block, (nx, 2, ROWS, 128), (HALF, 2, ny, 128)],
+        outside + tuple(buffers),
         alias={4 + n: n for n in range(5)},
     )
-    halo = shifted(edge, "yz")
-    theirs = swapped(halo)
+    halo, theirs, outside = exchange(rows, planes)
     (dots,) = call(first_dots_kernel, [(8, 128)], (u, first))
-    ups, downs = call(pack_vector_kernel, [(HALF, 2, 2 * ROWS, 128)] * 2, (first, halo, dots))
-    mine = both_ways(ups, downs, "gx")
-    second, va, vb, sums = call(
+    buffers = call(
         second_inner_kernel,
         [(HALF - 1,) + block, wide, wide, (HALF, 4, 2, ny, 128)],
         (halo, theirs, scale, u, first),
     )
+    shapes = [b.shape for b in buffers]
+    args = (scale, u, first) + tuple(buffers)
+    second, va, vb, sums = call(second_rest_kernel, shapes, args, alias={3 + n: n for n in range(4)})
     parts = lax.axis_size(AXES)
     second, _, _, dots = call(
         second_outer_kernel,
         [(HALF - 1,) + block, wide, wide, (parts, 128)],
-        mine + tuple(swapped(part) for part in mine) + (scale, u, first, dots, sums, second, va, vb),
+        outside + (scale, u, first, dots, sums, second, va, vb),
         alias={9: 0, 10: 1, 11: 2},
     )
     gathered = lax.all_to_all(dots.reshape(parts, 1, 128), AXES, 0, 0).reshape(parts, 128)

time: 104 us -> 104 us (level)
  waiting for transfers between devices: 33.7 us -> 28.6 us
  starting transfers between devices: 41 us -> 46 us
    ppermute x4 -> x6, starting transfers between devices: 13.9 us -> 22.2 us  [shifted(): return lax.ppermute(block, ('level', axis), route)]
    ppermute x2 -> x0, waiting for transfers between devices: 5.52 us -> none  [the longest x1 4.11 us: both_ways(): low = lax.ppermute(down, axis, [(b, a) for a, b in route])]
    ppermute x2 -> x0, starting transfers between devices: 4.69 us -> none  [the longest x1 3.4 us: both_ways(): high = lax.ppermute(up, axis, route)]
    ppermute x4 -> x6, waiting for transfers between devices: 17 us -> 16.6 us  [shifted(): return lax.ppermute(block, ('level', axis), route)]
    pallas_call x9 -> x11, Pallas kernels: 26.5 us -> 26.4 us  [call(): pl.pallas_call(kernel, out_shape=shapes + [jax.ShapeDtypeStruct(s, jnp.in...]
where the time goes in v6:
time: 104 us; the launch traced here: 102 us
  starting transfers between devices  46 us (44%)
  waiting for transfers between devices  28.6 us (28%)
  Pallas kernels  26.4 us (25%)
  between operations  1.08 us (1%)
    pallas_call x11, Pallas kernels, call(): pl.pallas_call(kernel, out_shape=shapes + [jax.ShapeDtypeStruct(s, jnp.in...  26.4 us
    all_to_all x1, starting transfers between devices, per_device(): lax.all_to_all(dots.reshape(parts, 1, 128), AXES, 0, 0).reshape(parts, 128)  23.2 us
    ppermute x6, starting transfers between devices, shifted(): return lax.ppermute(block, ('level', axis), route)  22.2 us
    ppermute x6, waiting for transfers between devices, shifted(): return lax.ppermute(block, ('level', axis), route)  16.6 us
    all_to_all x1, waiting for transfers between devices, per_device(): lax.all_to_all(dots.reshape(parts, 1, 128), AXES, 0, 0).reshape(parts, 128)  11.1 us
  transfers between devices with their start and end apart: 13, of which 7 were waited for; matrix products, arithmetic and copies ran while one was open for 0% of the time, Pallas kernels for 17%

profile of v6, /device:TPU:8, one launch (start us, length us, event | category | flops | bytes accessed | tf_op | source)
XLA Modules:
  0.0 102.3 jit_solution(42095285677164453)
XLA Ops:
  0.0 1.4 %shard_map.57 = (f32[96,2,8,128]{3,2,1,0:T(8,128)S(1)}, f32[19,2,16,128]{3,2,1,0:T(8,128)S(1)}) custom-call(f32[32,16,256]{2,1,0:T(8,128)} %far_u.1, f32[32,16,256]{2,1,0:T(8,128)} %f.3, f32[32,16,256]{2,1,0:T(8,128)} %d.3), custom_call_target="tpu_custom_call" | custom-call | tf_op jit(solution)/shard_map/pallas_call | solution.py:518
  1.4 3.5 %collective-permute-start.24 = (f32[96,2,8,128]{3,2,1,0:T(8,128)S(1)}, f32[96,2,8,128]{3,2,1,0:T(8,128)S(1)}, u32[]{:S(2)}, u32[]{:S(2)}) collective-permute-start(f32[96,2,8,128]{3,2,1,0:T(8,128)S(1)} %get-tuple-element.141), channel_id=1, source_target_pairs={{0,1},{1,2},{2,3},{3,4},{4,5},{5,6},{6,7},{7,8},{8,9},{9,10},{10,1... | collective-permute-start | bytes 2359304 | tf_op jit(solution)/shard_map/ppermute | solution.py:585
  4.9 3.4 %collective-permute-start.20 = (f32[19,2,16,128]{3,2,1,0:T(8,128)S(1)}, f32[19,2,16,128]{3,2,1,0:T(8,128)S(1)}, u32[]{:S(2)}, u32[]{:S(2)}) collective-permute-start(f32[19,2,16,128]{3,2,1,0:T(8,128)S(1)} %get-tuple-element.140), channel_id=1, source_target_pairs={{0,32},{32,64},{64,96},{160,128},{192,160},{224,192},{1,33},{33,65... | collective-permute-start | bytes 933896 | tf_op jit(solution)/shard_map/ppermute | solution.py:585
  8.3 4.4 %collective-permute-done.20.mine.refs_0_ = f32[19,2,16,128]{3,2,1,0:T(8,128)S(1)} collective-permute-done((f32[19,2,16,128]{3,2,1,0:T(8,128)S(1)}, f32[19,2,16,128]{3,2,1,0:T(8,128)S(1)}, u32[]{:S(2)}, u32[]{:S(2)}) %collective-permute-start.20) | collective-permute-done | bytes 311328 | tf_op jit(solution)/shard_map/ppermute | solution.py:585
  12.7 2.6 %collective-permute-done.24.mine = f32[96,2,8,128]{3,2,1,0:T(8,128)S(1)} collective-permute-done((f32[96,2,8,128]{3,2,1,0:T(8,128)S(1)}, f32[96,2,8,128]{3,2,1,0:T(8,128)S(1)}, u32[]{:S(2)}, u32[]{:S(2)}) %collective-permute-start.24) | collective-permute-done | bytes 786464 | tf_op jit(solution)/shard_map/ppermute | solution.py:585
  15.3 0.1 shard_map.58
  15.4 3.5 %collective-permute-start.22 = (f32[38,2,8,128]{3,2,1,0:T(8,128)S(1)}, f32[38,2,8,128]{3,2,1,0:T(8,128)S(1)}, u32[]{:S(2)}, u32[]{:S(2)}) collective-permute-start(f32[38,2,8,128]{3,2,1,0:T(8,128)S(1)} %shard_map.58), channel_id=1, source_target_pairs={{0,1},{1,2},{2,3},{3,4},{4,5},{5,6},{6,7},{7,8},{8,9},{9,10},{10,1... | collective-permute-start | bytes 933896 | tf_op jit(solution)/shard_map/ppermute | solution.py:585
  18.9 5.3 %collective-permute-done.22.refs_1_ = f32[38,2,8,128]{3,2,1,0:T(8,128)S(1)} collective-permute-done((f32[38,2,8,128]{3,2,1,0:T(8,128)S(1)}, f32[38,2,8,128]{3,2,1,0:T(8,128)S(1)}, u32[]{:S(2)}, u32[]{:S(2)}) %collective-permute-start.22) | collective-permute-done | bytes 311328 | tf_op jit(solution)/shard_map/ppermute | solution.py:585
  24.2 0.0 collective-permute-start.23
  24.2 0.0 collective-permute-done.25.theirs
  24.2 3.0 %shard_map.59 = (f32[46,2,48,128]{3,2,1,0:T(8,128)S(1)}, f32[46,2,48,128]{3,2,1,0:T(8,128)S(1)}, f32[46,2,48,128]{3,2,1,0:T(8,128)S(1)}, f32[46,2,48,128]{3,2,1,0:T(8,128)S(1)}, f32[7,32,2,16,128]{4,3,2,1,0:T(8,128)S(1)}) custom-call(f32[32,16,256]{2,1,0:T(8,128)S(1)} %copy-done.10, f32[32,16,256]{2,1,0:T(8,128)S(1)} %copy-done.7, ...), custom_call_target="tpu_custom_call" | custom-call | tf_op jit(solution)/shard_map/pallas_call | solution.py:518
  27.2 5.0 %shard_map.60 = (f32[46,2,48,128]{3,2,1,0:T(8,128)S(1)}, f32[46,2,48,128]{3,2,1,0:T(8,128)S(1)}, f32[46,2,48,128]{3,2,1,0:T(8,128)S(1)}, f32[46,2,48,128]{3,2,1,0:T(8,128)S(1)}, f32[7,32,2,16,128]{4,3,2,1,0:T(8,128)S(1)}) custom-call(f32[46,2,48,128]{3,2,1,0:T(8,128)S(1)} %get-tuple-elemen, ...), custom_call_target="tpu_custom_call", output_to_operand_aliasing={{0}: (0, {}), {1}: (1, {}), {2}: (2, {}), {3}: (3, {}), {4}... | custom-call | tf_op jit(solution)/shard_map/pallas_call | solution.py:518
  32.2 0.0 collective-permute-done.23.refs_3_
  32.2 1.8 %shard_map.61 = (f32[46,2,48,128]{3,2,1,0:T(8,128)S(1)}, f32[46,2,48,128]{3,2,1,0:T(8,128)S(1)}, f32[46,2,48,128]{3,2,1,0:T(8,128)S(1)}, f32[46,2,48,128]{3,2,1,...) custom-call(f32[19,2,16,128]{3,2,1,0:T(8,128)S(1)} %collective-permu, ...), custom_call_target="tpu_custom_call", output_to_operand_aliasing={{0}: (4, {}), {1}: (5, {}), {2}: (6, {}), {3}: (7, {}), {4}... | custom-call | tf_op jit(solution)/shard_map/pallas_call | solution.py:518
  34.0 3.5 %collective-permute-start.30 = (f32[32,2,8,128]{3,2,1,0:T(8,128)S(1)}, f32[32,2,8,128]{3,2,1,0:T(8,128)S(1)}, u32[]{:S(2)}, u32[]{:S(2)}) collective-permute-start(f32[32,2,8,128]{3,2,1,0:T(8,128)S(1)} %get-tuple-element.155), channel_id=1, source_target_pairs={{0,1},{1,2},{2,3},{3,4},{4,5},{5,6},{6,7},{7,8},{8,9},{9,10},{10,1... | collective-permute-start | bytes 786440 | tf_op jit(solution)/shard_map/ppermute | solution.py:585
  37.5 3.4 %collective-permute-start.26 = (f32[6,2,16,128]{3,2,1,0:T(8,128)S(1)}, f32[6,2,16,128]{3,2,1,0:T(8,128)S(1)}, u32[]{:S(2)}, u32[]{:S(2)}) collective-permute-start(f32[6,2,16,128]{3,2,1,0:T(8,128)S(1)} %get-tuple-element.152), channel_id=1, source_target_pairs={{0,32},{32,64},{64,96},{160,128},{192,160},{224,192},{1,33},{33,65... | collective-permute-start | bytes 294920 | tf_op jit(solution)/shard_map/ppermute | solution.py:585
  40.9 2.2 %collective-permute-done.26.mine.refs_0_ = f32[6,2,16,128]{3,2,1,0:T(8,128)S(1)} collective-permute-done((f32[6,2,16,128]{3,2,1,0:T(8,128)S(1)}, f32[6,2,16,128]{3,2,1,0:T(8,128)S(1)}, u32[]{:S(2)}, u32[]{:S(2)}) %collective-permute-start.26) | collective-permute-done | bytes 98336 | tf_op jit(solution)/shard_map/ppermute | solution.py:585
  43.1 0.5 collective-permute-start.31
  43.6 0.8 collective-permute-done.27.theirs.refs_2_
  44.4 4.9 %collective-permute-start.28 = (f32[12,2,8,128]{3,2,1,0:T(8,128)S(1)}, f32[12,2,8,128]{3,2,1,0:T(8,128)S(1)}, u32[]{:S(2)}, u32[]{:S(2)}) collective-permute-start(f32[12,2,8,128]{3,2,1,0:T(8,128)S(1)} %shard_map.62), channel_id=1, source_target_pairs={{0,1},{1,2},{2,3},{3,4},{4,5},{5,6},{6,7},{7,8},{8,9},{9,10},{10,1... | collective-permute-start | bytes 294920 | tf_op jit(solution)/shard_map/ppermute | solution.py:585
  49.4 2.2 %collective-permute-done.28.refs_1_ = f32[12,2,8,128]{3,2,1,0:T(8,128)S(1)} collective-permute-done((f32[12,2,8,128]{3,2,1,0:T(8,128)S(1)}, f32[12,2,8,128]{3,2,1,0:T(8,128)S(1)}, u32[]{:S(2)}, u32[]{:S(2)}) %collective-permute-start.28) | collective-permute-done | bytes 98336 | tf_op jit(solution)/shard_map/ppermute | solution.py:585
  51.6 1.6 %shard_map.63.refs_7_ = f32[8,128]{1,0:T(8,128)S(1)} custom-call(f32[32,16,256]{2,1,0:T(8,128)S(1)} %copy-done.10, f32[7,32,2,16,128]{4,3,2,1,0:T(8,128)S(1)} %get-tuple-element.154.basis.first.refs_6_.far_first), custom_call_target="tpu_custom_call" | custom-call | tf_op jit(solution)/shard_map/pallas_call | solution.py:518
  53.2 3.0 %shard_map.64 = (f32[5,32,2,16,128]{4,3,2,1,0:T(8,128)S(1)}, f32[46,2,48,128]{3,2,1,0:T(8,128)S(1)}, f32[46,2,48,128]{3,2,1,0:T(8,128)S(1)}, f32[6,4,2,16,128]{4,3,2,1,0:T(8,128)S(1)}) custom-call(f32[32,2,8,128]{3,2,1,0:T(8,128)S(1)} %collective-permute-done.30.mine, f32[32,2,8,128]{3,2,1,0:T(8,128)S(1)} %collective-permute-done.31.theirs, ...), custom_call_target="tpu_custom_call" | custom-call | tf_op jit(solution)/shard_map/pallas_call | solution.py:518
  56.2 4.3 %shard_map.65 = (f32[5,32,2,16,128]{4,3,2,1,0:T(8,128)S(1)}, f32[46,2,48,128]{3,2,1,0:T(8,128)S(1)}, f32[46,2,48,128]{3,2,1,0:T(8,128)S(1)}, f32[6,4,2,16,128]{4,3,2,1,0:T(8,128)S(1)}) custom-call(f32[46,2,48,128]{3,2,1,0:T(8,128)S(1)} %get-tuple-element.153.scale.refs_4_, ...), custom_call_target="tpu_custom_call", output_to_operand_aliasing={{0}: (3, {}), {1}: (4, {}), {2}: (5, {}), {3}: (6, {})} | custom-call | tf_op jit(solution)/shard_map/pallas_call | solution.py:518
  60.6 0.0 collective-permute-done.29.refs_3_
  60.6 0.0 copy-start.1
  60.6 0.0 copy-start.2
  60.6 2.6 %shard_map.66 = (f32[5,32,2,16,128]{4,3,2,1,0:T(8,128)S(1)}, f32[46,2,48,128]{3,2,1,0:T(8,128)S(1)}, f32[46,2,48,128]{3,2,1,0:T(8,128)S(1)}, f32[128,128]{1,0:T(8,128)}) custom-call(f32[6,2,16,128]{3,2,1,0:T(8,128)S(1)} %collective-permute-done.26.mine.refs_0_, ...), custom_call_target="tpu_custom_call", output_to_operand_aliasing={{0}: (9, {}), {1}: (10, {}), {2}: (11, {})} | custom-call | tf_op jit(solution)/shard_map/pallas_call | solution.py:518
  63.2 23.2 %all-to-all-start = ((f32[128,1,128]{2,1,0:T(1,128)}), f32[128,1,128]{2,1,0:T(1,128)S(1)}, u32[]{:S(2)}, u32[]{:S(2)}) async-start(f32[128,1,128]{2,1,0:T(1,128)} %bitcast.3), calls=%async_computation | async-start | bytes 131072 | tf_op jit(solution)/shard_map/all_to_all | solution.py:648
  86.5 11.1 %all-to-all-done = f32[128,1,128]{2,1,0:T(1,128)S(1)} async-done(((f32[128,1,128]{2,1,0:T(1,128)}), f32[128,1,128]{2,1,0:T(1,128)S(1)}, u32[]{:S(2)}, u32[]{:S(2)}) %all-to-all-start) | async-done | bytes 65568 | tf_op jit(solution)/shard_map/all_to_all | solution.py:648
  97.6 3.6 %shard_map.67 = (f32[32,16,256]{2,1,0:T(8,128)}, s32[1,1]{1,0:T(1,128)}) custom-call(f32[128,128]{1,0:T(8,128)S(1)} %bitcast.8, f32[128,128]{1,0:T(8,128)S(1)} %copy-done.1, f32[1,128]{1,0:T(1,128)S(1)} %copy-done.2, f32[5,32,2,16,128]{4,3,2,1,0:T(8,128)S(1)} %get-tuple-element.165.second, f32[32,16,256]{2,1,0:T(8,128)} %far_u.1, f32[7,32,2,16,128]{4,3,2,1,0:T(8,128)} %copy-done), custom_call_target="tpu_custom_call" | custom-call | tf_op jit(solution)/shard_map/pallas_call | solution.py:518
  101.9 0.2 conditional.1
  (20 shorter events, 0.1 us)
Async XLA Ops:
  0.0 24.2 %copy-start.10 = (f32[32,16,256]{2,1,0:T(8,128)S(1)}, f32[32,16,256]{2,1,0:T(8,128)}, u32[]{:S(2)}) copy-start(f32[32,16,256]{2,1,0:T(8,128)} %far_u.1) | copy-start | bytes 1572868
  0.0 24.2 %copy-start.7 = (f32[32,16,256]{2,1,0:T(8,128)S(1)}, f32[32,16,256]{2,1,0:T(8,128)}, u32[]{:S(2)}) copy-start(f32[32,16,256]{2,1,0:T(8,128)} %f.3) | copy-start | bytes 1572868
  0.0 24.2 %copy-start.3 = (f32[32,16,256]{2,1,0:T(8,128)S(1)}, f32[32,16,256]{2,1,0:T(8,128)}, u32[]{:S(2)}) copy-start(f32[32,16,256]{2,1,0:T(8,128)} %d.3) | copy-start | bytes 1572868
  1.4 13.9 %collective-permute-start.24 = (f32[96,2,8,128]{3,2,1,0:T(8,128)S(1)}, f32[96,2,8,128]{3,2,1,0:T(8,128)S(1)}, u32[]{:S(2)}, u32[]{:S(2)}) collective-permute-start(f32[96,2,8,128]{3,2,1,0:T(8,128)S(1)} %get-tuple-element.141), channel_id=1, source_target_pairs={{0,1},{1,2},{2,3},{3,4},{4,5},{5,6},{6,7},{7,8},{8,9},{9,10},{10,1... | collective-permute-start | bytes 2359304 | tf_op jit(solution)/shard_map/ppermute | solution.py:585
  4.9 7.8 %collective-permute-start.20 = (f32[19,2,16,128]{3,2,1,0:T(8,128)S(1)}, f32[19,2,16,128]{3,2,1,0:T(8,128)S(1)}, u32[]{:S(2)}, u32[]{:S(2)}) collective-permute-start(f32[19,2,16,128]{3,2,1,0:T(8,128)S(1)} %get-tuple-element.140), channel_id=1, source_target_pairs={{0,32},{32,64},{64,96},{160,128},{192,160},{224,192},{1,33},{33,65... | collective-permute-start | bytes 933896 | tf_op jit(solution)/shard_map/ppermute | solution.py:585
  12.7 2.6 %collective-permute-start.21 = (f32[19,2,16,128]{3,2,1,0:T(8,128)S(1)}, f32[19,2,16,128]{3,2,1,0:T(8,128)S(1)}, u32[]{:S(2)}, u32[]{:S(2)}) collective-permute-start(f32[19,2,16,128]{3,2,1,0:T(8,128)S(1)} %collective-permute-done.20.mine.refs_0_), channel_id=1, source_target_pairs={{0,128},{128,0},{1,129},{129,1},{2,130},{130,2},{3,131},{131,3},{4... | collective-permute-start | bytes 933896 | tf_op jit(solution)/shard_map/ppermute | solution.py:589
  15.3 8.9 %collective-permute-start.25 = (f32[96,2,8,128]{3,2,1,0:T(8,128)S(1)}, f32[96,2,8,128]{3,2,1,0:T(8,128)S(1)}, u32[]{:S(2)}, u32[]{:S(2)}) collective-permute-start(f32[96,2,8,128]{3,2,1,0:T(8,128)S(1)} %collective-permute-done.24.mine), channel_id=1, source_target_pairs={{0,128},{128,0},{1,129},{129,1},{2,130},{130,2},{3,131},{131,3},{4... | collective-permute-start | bytes 2359304 | tf_op jit(solution)/shard_map/ppermute | solution.py:589
  15.4 8.8 %collective-permute-start.22 = (f32[38,2,8,128]{3,2,1,0:T(8,128)S(1)}, f32[38,2,8,128]{3,2,1,0:T(8,128)S(1)}, u32[]{:S(2)}, u32[]{:S(2)}) collective-permute-start(f32[38,2,8,128]{3,2,1,0:T(8,128)S(1)} %shard_map.58), channel_id=1, source_target_pairs={{0,1},{1,2},{2,3},{3,4},{4,5},{5,6},{6,7},{7,8},{8,9},{9,10},{10,1... | collective-permute-start | bytes 933896 | tf_op jit(solution)/shard_map/ppermute | solution.py:585
  24.2 8.0 %collective-permute-start.23 = (f32[38,2,8,128]{3,2,1,0:T(8,128)S(1)}, f32[38,2,8,128]{3,2,1,0:T(8,128)S(1)}, u32[]{:S(2)}, u32[]{:S(2)}) collective-permute-start(f32[38,2,8,128]{3,2,1,0:T(8,128)S(1)} %collective-permute-done.22.refs_1_), channel_id=1, source_target_pairs={{0,128},{128,0},{1,129},{129,1},{2,130},{130,2},{3,131},{131,3},{4... | collective-permute-start | bytes 933896 | tf_op jit(solution)/shard_map/ppermute | solution.py:589
  34.0 26.6 %copy-start = (f32[7,32,2,16,128]{4,3,2,1,0:T(8,128)}, f32[7,32,2,16,128]{4,3,2,1,0:T(8,128)S(1)}, u32[]{:S(2)}) copy-start(f32[7,32,2,16,128]{4,3,2,1,0:T(8,128)S(1)} %get-tuple-element.154.basis.first.refs_6_.far_first) | copy-start | bytes 11010052
  34.0 9.1 %collective-permute-start.30 = (f32[32,2,8,128]{3,2,1,0:T(8,128)S(1)}, f32[32,2,8,128]{3,2,1,0:T(8,128)S(1)}, u32[]{:S(2)}, u32[]{:S(2)}) collective-permute-start(f32[32,2,8,128]{3,2,1,0:T(8,128)S(1)} %get-tuple-element.155), channel_id=1, source_target_pairs={{0,1},{1,2},{2,3},{3,4},{4,5},{5,6},{6,7},{7,8},{8,9},{9,10},{10,1... | collective-permute-start | bytes 786440 | tf_op jit(solution)/shard_map/ppermute | solution.py:585
  37.5 5.6 %collective-permute-start.26 = (f32[6,2,16,128]{3,2,1,0:T(8,128)S(1)}, f32[6,2,16,128]{3,2,1,0:T(8,128)S(1)}, u32[]{:S(2)}, u32[]{:S(2)}) collective-permute-start(f32[6,2,16,128]{3,2,1,0:T(8,128)S(1)} %get-tuple-element.152), channel_id=1, source_target_pairs={{0,32},{32,64},{64,96},{160,128},{192,160},{224,192},{1,33},{33,65... | collective-permute-start | bytes 294920 | tf_op jit(solution)/shard_map/ppermute | solution.py:585
  43.1 1.3 %collective-permute-start.27 = (f32[6,2,16,128]{3,2,1,0:T(8,128)S(1)}, f32[6,2,16,128]{3,2,1,0:T(8,128)S(1)}, u32[]{:S(2)}, u32[]{:S(2)}) collective-permute-start(f32[6,2,16,128]{3,2,1,0:T(8,128)S(1)} %collective-permute-done.26.mine.refs_0_), channel_id=1, source_target_pairs={{0,128},{128,0},{1,129},{129,1},{2,130},{130,2},{3,131},{131,3},{4... | collective-permute-start | bytes 294920 | tf_op jit(solution)/shard_map/ppermute | solution.py:589
  43.1 10.0 %collective-permute-start.31 = (f32[32,2,8,128]{3,2,1,0:T(8,128)S(1)}, f32[32,2,8,128]{3,2,1,0:T(8,128)S(1)}, u32[]{:S(2)}, u32[]{:S(2)}) collective-permute-start(f32[32,2,8,128]{3,2,1,0:T(8,128)S(1)} %collective-permute-done.30.mine), channel_id=1, source_target_pairs={{0,128},{128,0},{1,129},{129,1},{2,130},{130,2},{3,131},{131,3},{4... | collective-permute-start | bytes 786440 | tf_op jit(solution)/shard_map/ppermute | solution.py:589
  44.4 7.1 %collective-permute-start.28 = (f32[12,2,8,128]{3,2,1,0:T(8,128)S(1)}, f32[12,2,8,128]{3,2,1,0:T(8,128)S(1)}, u32[]{:S(2)}, u32[]{:S(2)}) collective-permute-start(f32[12,2,8,128]{3,2,1,0:T(8,128)S(1)} %shard_map.62), channel_id=1, source_target_pairs={{0,1},{1,2},{2,3},{3,4},{4,5},{5,6},{6,7},{7,8},{8,9},{9,10},{10,1... | collective-permute-start | bytes 294920 | tf_op jit(solution)/shard_map/ppermute | solution.py:585
  51.6 9.0 %collective-permute-start.29 = (f32[12,2,8,128]{3,2,1,0:T(8,128)S(1)}, f32[12,2,8,128]{3,2,1,0:T(8,128)S(1)}, u32[]{:S(2)}, u32[]{:S(2)}) collective-permute-start(f32[12,2,8,128]{3,2,1,0:T(8,128)S(1)} %collective-permute-done.28.refs_1_), channel_id=1, source_target_pairs={{0,128},{128,0},{1,129},{129,1},{2,130},{130,2},{3,131},{131,3},{4... | collective-permute-start | bytes 294920 | tf_op jit(solution)/shard_map/ppermute | solution.py:589
  60.6 37.0 %copy-start.1 = (f32[128,128]{1,0:T(8,128)S(1)}, f32[128,128]{1,0:T(8,128)}, u32[]{:S(2)}) copy-start(f32[128,128]{1,0:T(8,128)} %constant.50.clone.tables) | copy-start | bytes 196612
  60.6 37.0 %copy-start.2 = (f32[1,128]{1,0:T(1,128)S(1)}, f32[1,128]{1,0:T(1,128)}, u32[]{:S(2)}) copy-start(f32[1,128]{1,0:T(1,128)} %constant.51.clone.nodes) | copy-start | bytes 1540
  63.2 34.4 %all-to-all-start = ((f32[128,1,128]{2,1,0:T(1,128)}), f32[128,1,128]{2,1,0:T(1,128)S(1)}, u32[]{:S(2)}, u32[]{:S(2)}) async-start(f32[128,1,128]{2,1,0:T(1,128)} %bitcast.3), calls=%async_computation | async-start | bytes 131072 | tf_op jit(solution)/shard_map/all_to_all | solution.py:648
  97.6 4.3 %copy-start.11 = (f32[32,16,256]{2,1,0:T(8,128)S(1)}, f32[32,16,256]{2,1,0:T(8,128)}, u32[]{:S(2)}) copy-start(f32[32,16,256]{2,1,0:T(8,128)} %far_u.1) | copy-start | bytes 1572868

commit v7 on v6

--- a/solution.py
+++ b/solution.py
@@ -322,16 +322,21 @@
         over(HALF - 1 - k, k + 2, body)
 
 
-def first_inner_kernel(u, f, d, mine, theirs, wide_u, va, vb, scale, basis):
+def first_own_kernel(u, f, d, wide_u, va, vb, scale):
     nx, ny, _ = u.shape
-    level = lax.axis_index("level")
     clear_margins((wide_u, va, vb))
-    for n, (ref, dst) in enumerate(((u, wide_u), (f, va), (d, scale))):
-        for halo, place in ((mine, level), (theirs, 1 - level)):
-            outer = row_span(place, ny)
-            dst[WIDE : WIDE + nx, :, outer] = halo[n * nx : (n + 1) * nx]
+    for ref, dst in ((u, wide_u), (f, va), (d, scale)):
         for c in range(2):
             dst[WIDE : WIDE + nx, c, OWN : OWN + ny] = ref[:, :, c * 128 : (c + 1) * 128]
+
+
+def first_inner_kernel(mine, theirs, *refs):
+    wide_u, va, vb, scale, basis = refs[4:]
+    _, nx, _, ny, _ = basis.shape
+    level = lax.axis_index("level")
+    for n, dst in enumerate((wide_u, va, scale)):
+        for halo, place in ((mine, level), (theirs, 1 - level)):
+            dst[WIDE : WIDE + nx, :, row_span(place, ny)] = halo[n * nx : (n + 1) * nx]
     over = lambda halo, skip, body: over_inner(nx, skip, body)
     first_steps(ny, wide_u, va, vb, scale, basis, over, range(FIRST_CUT))
 
@@ -420,14 +425,19 @@
     return body, 2 if last else 4
 
 
-def second_inner_kernel(mine, theirs, scale, u, first, basis, va, vb, sums):
+def second_own_kernel(first, dots, va, vb):
+    _, nx, _, ny, _ = first.shape
+    clear_margins((va, vb))
+    va[WIDE : WIDE + nx, :, OWN : OWN + ny] = first[HALF]
+
+
+def second_inner_kernel(mine, theirs, scale, u, first, *refs):
+    basis, va, vb, sums = refs[2:]
     _, nx, _, ny, _ = basis.shape
     level = lax.axis_index("level")
-    clear_margins((va, vb))
     for halo, place in ((mine, level), (theirs, 1 - level)):
         outer = row_span(place, ny)
         va[WIDE : WIDE + nx, :, outer] = halo[...]
-    va[WIDE : WIDE + nx, :, OWN : OWN + ny] = first[HALF]
     second_inner_steps(range(SECOND_CUT), scale, u, first, basis, va, vb, sums)
 
 
@@ -619,7 +629,10 @@
     halo, theirs, outside = exchange(rows, planes)
     wide = (nx + 2 * WIDE, 2, tall + 2 * PAD, 128)
     block = (nx, 2, ny, 128)
-    buffers = call(first_inner_kernel, [wide] * 4 + [(HALF + 1,) + block], (u, f, d, halo, theirs))
+    own = call(first_own_kernel, [wide] * 4, (u, f, d))
+    args = (halo, theirs) + tuple(own)
+    shapes = [wide] * 4 + [(HALF + 1,) + block]
+    buffers = call(first_inner_kernel, shapes, args, alias={2 + n: n for n in range(4)})
     shapes = [b.shape for b in buffers]
     buffers = call(first_rest_kernel, shapes, buffers, alias={n: n for n in range(5)})
     *_, scale, first, rows, planes = call(
@@ -630,10 +643,12 @@
     )
     halo, theirs, outside = exchange(rows, planes)
     (dots,) = call(first_dots_kernel, [(8, 128)], (u, first))
+    own = call(second_own_kernel, [wide] * 2, (first, dots))
     buffers = call(
         second_inner_kernel,
         [(HALF - 1,) + block, wide, wide, (HALF, 4, 2, ny, 128)],
-        (halo, theirs, scale, u, first),
+        (halo, theirs, scale, u, first) + tuple(own),
+        alias={5: 1, 6: 2},
     )
     shapes = [b.shape for b in buffers]
     args = (scale, u, first) + tuple(buffers)

time: 104 us -> 104 us (level)
    pallas_call x11 -> x13, Pallas kernels: 26.4 us -> 26.4 us  [call(): pl.pallas_call(kernel, out_shape=shapes + [jax.ShapeDtypeStruct(s, jnp.in...]
where the time goes in v7:
time: 104 us; the launch traced here: 102 us
  starting transfers between devices  46 us (44%)
  waiting for transfers between devices  28.6 us (28%)
  Pallas kernels  26.4 us (25%)
    pallas_call x13, Pallas kernels, call(): pl.pallas_call(kernel, out_shape=shapes + [jax.ShapeDtypeStruct(s, jnp.in...  26.4 us
    all_to_all x1, starting transfers between devices, per_device(): lax.all_to_all(dots.reshape(parts, 1, 128), AXES, 0, 0).reshape(parts, 128)  23.3 us
    ppermute x6, starting transfers between devices, shifted(): return lax.ppermute(block, ('level', axis), route)  22.2 us
    ppermute x6, waiting for transfers between devices, shifted(): return lax.ppermute(block, ('level', axis), route)  16.6 us
    all_to_all x1, waiting for transfers between devices, per_device(): lax.all_to_all(dots.reshape(parts, 1, 128), AXES, 0, 0).reshape(parts, 128)  11.1 us
  transfers between devices with their start and end apart: 13, of which 7 were waited for; matrix products, arithmetic and copies ran while one was open for 0% of the time, Pallas kernels for 17%

profile of v7, /device:TPU:8, one launch (start us, length us, event | category | flops | bytes accessed | tf_op | source)
XLA Modules:
  0.0 102.2 jit_solution(16620856752554087019)
XLA Ops:
  0.0 1.4 %shard_map.57 = (f32[96,2,8,128]{3,2,1,0:T(8,128)S(1)}, f32[19,2,16,128]{3,2,1,0:T(8,128)S(1)}) custom-call(f32[32,16,256]{2,1,0:T(8,128)} %far_u.1, f32[32,16,256]{2,1,0:T(8,128)} %f.3, f32[32,16,256]{2,1,0:T(8,128)} %d.3), custom_call_target="tpu_custom_call" | custom-call | tf_op jit(solution)/shard_map/pallas_call | solution.py:528
  1.4 3.5 %collective-permute-start.24 = (f32[96,2,8,128]{3,2,1,0:T(8,128)S(1)}, f32[96,2,8,128]{3,2,1,0:T(8,128)S(1)}, u32[]{:S(2)}, u32[]{:S(2)}) collective-permute-start(f32[96,2,8,128]{3,2,1,0:T(8,128)S(1)} %get-tuple-element.147), channel_id=1, source_target_pairs={{0,1},{1,2},{2,3},{3,4},{4,5},{5,6},{6,7},{7,8},{8,9},{9,10},{10,1... | collective-permute-start | bytes 2359304 | tf_op jit(solution)/shard_map/ppermute | solution.py:595
  4.9 3.4 %collective-permute-start.20 = (f32[19,2,16,128]{3,2,1,0:T(8,128)S(1)}, f32[19,2,16,128]{3,2,1,0:T(8,128)S(1)}, u32[]{:S(2)}, u32[]{:S(2)}) collective-permute-start(f32[19,2,16,128]{3,2,1,0:T(8,128)S(1)} %get-tuple-element.146), channel_id=1, source_target_pairs={{0,32},{32,64},{64,96},{160,128},{192,160},{224,192},{1,33},{33,65... | collective-permute-start | bytes 933896 | tf_op jit(solution)/shard_map/ppermute | solution.py:595
  8.3 4.4 %collective-permute-done.20.mine.refs_0_ = f32[19,2,16,128]{3,2,1,0:T(8,128)S(1)} collective-permute-done((f32[19,2,16,128]{3,2,1,0:T(8,128)S(1)}, f32[19,2,16,128]{3,2,1,0:T(8,128)S(1)}, u32[]{:S(2)}, u32[]{:S(2)}) %collective-permute-start.20) | collective-permute-done | bytes 311328 | tf_op jit(solution)/shard_map/ppermute | solution.py:595
  12.7 2.6 %collective-permute-done.24.mine = f32[96,2,8,128]{3,2,1,0:T(8,128)S(1)} collective-permute-done((f32[96,2,8,128]{3,2,1,0:T(8,128)S(1)}, f32[96,2,8,128]{3,2,1,0:T(8,128)S(1)}, u32[]{:S(2)}, u32[]{:S(2)}) %collective-permute-start.24) | collective-permute-done | bytes 786464 | tf_op jit(solution)/shard_map/ppermute | solution.py:595
  15.3 0.1 shard_map.58
  15.4 3.5 %collective-permute-start.22 = (f32[38,2,8,128]{3,2,1,0:T(8,128)S(1)}, f32[38,2,8,128]{3,2,1,0:T(8,128)S(1)}, u32[]{:S(2)}, u32[]{:S(2)}) collective-permute-start(f32[38,2,8,128]{3,2,1,0:T(8,128)S(1)} %shard_map.58), channel_id=1, source_target_pairs={{0,1},{1,2},{2,3},{3,4},{4,5},{5,6},{6,7},{7,8},{8,9},{9,10},{10,1... | collective-permute-start | bytes 933896 | tf_op jit(solution)/shard_map/ppermute | solution.py:595
  18.9 5.3 %collective-permute-done.22.refs_1_ = f32[38,2,8,128]{3,2,1,0:T(8,128)S(1)} collective-permute-done((f32[38,2,8,128]{3,2,1,0:T(8,128)S(1)}, f32[38,2,8,128]{3,2,1,0:T(8,128)S(1)}, u32[]{:S(2)}, u32[]{:S(2)}) %collective-permute-start.22) | collective-permute-done | bytes 311328 | tf_op jit(solution)/shard_map/ppermute | solution.py:595
  24.2 0.0 collective-permute-start.23
  24.2 0.3 shard_map.59
  24.5 2.7 %shard_map.60 = (f32[46,2,48,128]{3,2,1,0:T(8,128)S(1)}, f32[46,2,48,128]{3,2,1,0:T(8,128)S(1)}, f32[46,2,48,128]{3,2,1,0:T(8,128)S(1)}, f32[46,2,48,128]{3,2,1,0:T(8,128)S(1)}, f32[7,32,2,16,128]{4,3,2,1,0:T(8,128)S(1)}) custom-call(f32[96,2,8,128]{3,2,1,0:T(8,128)S(1)} %collective-permute-d, ...), custom_call_target="tpu_custom_call", output_to_operand_aliasing={{0}: (2, {}), {1}: (3, {}), {2}: (4, {}), {3}: (5, {})} | custom-call | tf_op jit(solution)/shard_map/pallas_call | solution.py:528
  27.2 5.0 %shard_map.61 = (f32[46,2,48,128]{3,2,1,0:T(8,128)S(1)}, f32[46,2,48,128]{3,2,1,0:T(8,128)S(1)}, f32[46,2,48,128]{3,2,1,0:T(8,128)S(1)}, f32[46,2,48,128]{3,2,1,0:T(8,128)S(1)}, f32[7,32,2,16,128]{4,3,2,1,0:T(8,128)S(1)}) custom-call(f32[46,2,48,128]{3,2,1,0:T(8,128)S(1)} %get-tuple-elemen, ...), custom_call_target="tpu_custom_call", output_to_operand_aliasing={{0}: (0, {}), {1}: (1, {}), {2}: (2, {}), {3}: (3, {}), {4}... | custom-call | tf_op jit(solution)/shard_map/pallas_call | solution.py:528
  32.3 1.8 %shard_map.62 = (f32[46,2,48,128]{3,2,1,0:T(8,128)S(1)}, f32[46,2,48,128]{3,2,1,0:T(8,128)S(1)}, f32[46,2,48,128]{3,2,1,0:T(8,128)S(1)}, f32[46,2,48,128]{3,2,1,...) custom-call(f32[19,2,16,128]{3,2,1,0:T(8,128)S(1)} %collective-permu, ...), custom_call_target="tpu_custom_call", output_to_operand_aliasing={{0}: (4, {}), {1}: (5, {}), {2}: (6, {}), {3}: (7, {}), {4}... | custom-call | tf_op jit(solution)/shard_map/pallas_call | solution.py:528
  34.0 3.5 %collective-permute-start.30 = (f32[32,2,8,128]{3,2,1,0:T(8,128)S(1)}, f32[32,2,8,128]{3,2,1,0:T(8,128)S(1)}, u32[]{:S(2)}, u32[]{:S(2)}) collective-permute-start(f32[32,2,8,128]{3,2,1,0:T(8,128)S(1)} %get-tuple-element.165), channel_id=1, source_target_pairs={{0,1},{1,2},{2,3},{3,4},{4,5},{5,6},{6,7},{7,8},{8,9},{9,10},{10,1... | collective-permute-start | bytes 786440 | tf_op jit(solution)/shard_map/ppermute | solution.py:595
  37.5 3.4 %collective-permute-start.26 = (f32[6,2,16,128]{3,2,1,0:T(8,128)S(1)}, f32[6,2,16,128]{3,2,1,0:T(8,128)S(1)}, u32[]{:S(2)}, u32[]{:S(2)}) collective-permute-start(f32[6,2,16,128]{3,2,1,0:T(8,128)S(1)} %get-tuple-element.162), channel_id=1, source_target_pairs={{0,32},{32,64},{64,96},{160,128},{192,160},{224,192},{1,33},{33,65... | collective-permute-start | bytes 294920 | tf_op jit(solution)/shard_map/ppermute | solution.py:595
  40.9 2.2 %collective-permute-done.26.mine.refs_0_ = f32[6,2,16,128]{3,2,1,0:T(8,128)S(1)} collective-permute-done((f32[6,2,16,128]{3,2,1,0:T(8,128)S(1)}, f32[6,2,16,128]{3,2,1,0:T(8,128)S(1)}, u32[]{:S(2)}, u32[]{:S(2)}) %collective-permute-start.26) | collective-permute-done | bytes 98336 | tf_op jit(solution)/shard_map/ppermute | solution.py:595
  43.1 0.5 collective-permute-start.31
  43.6 0.8 collective-permute-done.27.theirs.refs_2_
  44.5 4.9 %collective-permute-start.28 = (f32[12,2,8,128]{3,2,1,0:T(8,128)S(1)}, f32[12,2,8,128]{3,2,1,0:T(8,128)S(1)}, u32[]{:S(2)}, u32[]{:S(2)}) collective-permute-start(f32[12,2,8,128]{3,2,1,0:T(8,128)S(1)} %shard_map.63), channel_id=1, source_target_pairs={{0,1},{1,2},{2,3},{3,4},{4,5},{5,6},{6,7},{7,8},{8,9},{9,10},{10,1... | collective-permute-start | bytes 294920 | tf_op jit(solution)/shard_map/ppermute | solution.py:595
  49.4 2.2 %collective-permute-done.28.refs_1_ = f32[12,2,8,128]{3,2,1,0:T(8,128)S(1)} collective-permute-done((f32[12,2,8,128]{3,2,1,0:T(8,128)S(1)}, f32[12,2,8,128]{3,2,1,0:T(8,128)S(1)}, u32[]{:S(2)}, u32[]{:S(2)}) %collective-permute-start.28) | collective-permute-done | bytes 98336 | tf_op jit(solution)/shard_map/ppermute | solution.py:595
  51.6 0.0 collective-permute-start.29
  51.6 1.6 %shard_map.64.dots.refs_7_ = f32[8,128]{1,0:T(8,128)S(1)} custom-call(f32[32,16,256]{2,1,0:T(8,128)S(1)} %copy-done.10, f32[7,32,2,16,128]{4,3,2,1,0:T(8,128)S(1)} %get-tuple-element.164.basis.first.refs_6_.far_first), custom_call_target="tpu_custom_call" | custom-call | tf_op jit(solution)/shard_map/pallas_call | solution.py:528
  53.2 0.2 shard_map.65
  53.4 2.9 %shard_map.66 = (f32[5,32,2,16,128]{4,3,2,1,0:T(8,128)S(1)}, f32[46,2,48,128]{3,2,1,0:T(8,128)S(1)}, f32[46,2,48,128]{3,2,1,0:T(8,128)S(1)}, f32[6,4,2,16,128]{4,3,2,1,0:T(8,128)S(1)}) custom-call(f32[32,2,8,128]{3,2,1,0:T(8,128)S(1)} %collective-permute-done.30.mine, ...), custom_call_target="tpu_custom_call", output_to_operand_aliasing={{1}: (5, {}), {2}: (6, {})} | custom-call | tf_op jit(solution)/shard_map/pallas_call | solution.py:528
  56.2 4.3 %shard_map.67 = (f32[5,32,2,16,128]{4,3,2,1,0:T(8,128)S(1)}, f32[46,2,48,128]{3,2,1,0:T(8,128)S(1)}, f32[46,2,48,128]{3,2,1,0:T(8,128)S(1)}, f32[6,4,2,16,128]{4,3,2,1,0:T(8,128)S(1)}) custom-call(f32[46,2,48,128]{3,2,1,0:T(8,128)S(1)} %get-tuple-element.163.scale.refs_4_, ...), custom_call_target="tpu_custom_call", output_to_operand_aliasing={{0}: (3, {}), {1}: (4, {}), {2}: (5, {}), {3}: (6, {})} | custom-call | tf_op jit(solution)/shard_map/pallas_call | solution.py:528
  60.6 0.0 copy-start.1
  60.6 0.0 copy-start.2
  60.6 2.6 %shard_map.68 = (f32[5,32,2,16,128]{4,3,2,1,0:T(8,128)S(1)}, f32[46,2,48,128]{3,2,1,0:T(8,128)S(1)}, f32[46,2,48,128]{3,2,1,0:T(8,128)S(1)}, f32[128,128]{1,0:T(8,128)}) custom-call(f32[6,2,16,128]{3,2,1,0:T(8,128)S(1)} %collective-permute-done.26.mine.refs_0_, ...), custom_call_target="tpu_custom_call", output_to_operand_aliasing={{0}: (9, {}), {1}: (10, {}), {2}: (11, {})} | custom-call | tf_op jit(solution)/shard_map/pallas_call | solution.py:528
  63.2 23.3 %all-to-all-start = ((f32[128,1,128]{2,1,0:T(1,128)}), f32[128,1,128]{2,1,0:T(1,128)S(1)}, u32[]{:S(2)}, u32[]{:S(2)}) async-start(f32[128,1,128]{2,1,0:T(1,128)} %bitcast.3), calls=%async_computation | async-start | bytes 131072 | tf_op jit(solution)/shard_map/all_to_all | solution.py:663
  86.5 11.1 %all-to-all-done = f32[128,1,128]{2,1,0:T(1,128)S(1)} async-done(((f32[128,1,128]{2,1,0:T(1,128)}), f32[128,1,128]{2,1,0:T(1,128)S(1)}, u32[]{:S(2)}, u32[]{:S(2)}) %all-to-all-start) | async-done | bytes 65568 | tf_op jit(solution)/shard_map/all_to_all | solution.py:663
  97.6 3.6 %shard_map.69 = (f32[32,16,256]{2,1,0:T(8,128)}, s32[1,1]{1,0:T(1,128)}) custom-call(f32[128,128]{1,0:T(8,128)S(1)} %bitcast.8, f32[128,128]{1,0:T(8,128)S(1)} %copy-done.1, f32[1,128]{1,0:T(1,128)S(1)} %copy-done.2, f32[5,32,2,16,128]{4,3,2,1,0:T(8,128)S(1)} %get-tuple-element.177.second, f32[32,16,256]{2,1,0:T(8,128)} %far_u.1, f32[7,32,2,16,128]{4,3,2,1,0:T(8,128)} %copy-done), custom_call_target="tpu_custom_call" | custom-call | tf_op jit(solution)/shard_map/pallas_call | solution.py:528
  101.8 0.2 conditional.1
  (22 shorter events, 0.1 us)
Async XLA Ops:
  0.0 24.2 %copy-start.10 = (f32[32,16,256]{2,1,0:T(8,128)S(1)}, f32[32,16,256]{2,1,0:T(8,128)}, u32[]{:S(2)}) copy-start(f32[32,16,256]{2,1,0:T(8,128)} %far_u.1) | copy-start | bytes 1572868
  0.0 24.2 %copy-start.7 = (f32[32,16,256]{2,1,0:T(8,128)S(1)}, f32[32,16,256]{2,1,0:T(8,128)}, u32[]{:S(2)}) copy-start(f32[32,16,256]{2,1,0:T(8,128)} %f.3) | copy-start | bytes 1572868
  0.0 24.2 %copy-start.3 = (f32[32,16,256]{2,1,0:T(8,128)S(1)}, f32[32,16,256]{2,1,0:T(8,128)}, u32[]{:S(2)}) copy-start(f32[32,16,256]{2,1,0:T(8,128)} %d.3) | copy-start | bytes 1572868
  1.4 13.9 %collective-permute-start.24 = (f32[96,2,8,128]{3,2,1,0:T(8,128)S(1)}, f32[96,2,8,128]{3,2,1,0:T(8,128)S(1)}, u32[]{:S(2)}, u32[]{:S(2)}) collective-permute-start(f32[96,2,8,128]{3,2,1,0:T(8,128)S(1)} %get-tuple-element.147), channel_id=1, source_target_pairs={{0,1},{1,2},{2,3},{3,4},{4,5},{5,6},{6,7},{7,8},{8,9},{9,10},{10,1... | collective-permute-start | bytes 2359304 | tf_op jit(solution)/shard_map/ppermute | solution.py:595
  4.9 7.8 %collective-permute-start.20 = (f32[19,2,16,128]{3,2,1,0:T(8,128)S(1)}, f32[19,2,16,128]{3,2,1,0:T(8,128)S(1)}, u32[]{:S(2)}, u32[]{:S(2)}) collective-permute-start(f32[19,2,16,128]{3,2,1,0:T(8,128)S(1)} %get-tuple-element.146), channel_id=1, source_target_pairs={{0,32},{32,64},{64,96},{160,128},{192,160},{224,192},{1,33},{33,65... | collective-permute-start | bytes 933896 | tf_op jit(solution)/shard_map/ppermute | solution.py:595
  12.7 2.6 %collective-permute-start.21 = (f32[19,2,16,128]{3,2,1,0:T(8,128)S(1)}, f32[19,2,16,128]{3,2,1,0:T(8,128)S(1)}, u32[]{:S(2)}, u32[]{:S(2)}) collective-permute-start(f32[19,2,16,128]{3,2,1,0:T(8,128)S(1)} %collective-permute-done.20.mine.refs_0_), channel_id=1, source_target_pairs={{0,128},{128,0},{1,129},{129,1},{2,130},{130,2},{3,131},{131,3},{4... | collective-permute-start | bytes 933896 | tf_op jit(solution)/shard_map/ppermute | solution.py:599
  15.3 9.2 %collective-permute-start.25 = (f32[96,2,8,128]{3,2,1,0:T(8,128)S(1)}, f32[96,2,8,128]{3,2,1,0:T(8,128)S(1)}, u32[]{:S(2)}, u32[]{:S(2)}) collective-permute-start(f32[96,2,8,128]{3,2,1,0:T(8,128)S(1)} %collective-permute-done.24.mine), channel_id=1, source_target_pairs={{0,128},{128,0},{1,129},{129,1},{2,130},{130,2},{3,131},{131,3},{4... | collective-permute-start | bytes 2359304 | tf_op jit(solution)/shard_map/ppermute | solution.py:599
  15.4 8.8 %collective-permute-start.22 = (f32[38,2,8,128]{3,2,1,0:T(8,128)S(1)}, f32[38,2,8,128]{3,2,1,0:T(8,128)S(1)}, u32[]{:S(2)}, u32[]{:S(2)}) collective-permute-start(f32[38,2,8,128]{3,2,1,0:T(8,128)S(1)} %shard_map.58), channel_id=1, source_target_pairs={{0,1},{1,2},{2,3},{3,4},{4,5},{5,6},{6,7},{7,8},{8,9},{9,10},{10,1... | collective-permute-start | bytes 933896 | tf_op jit(solution)/shard_map/ppermute | solution.py:595
  24.2 8.1 %collective-permute-start.23 = (f32[38,2,8,128]{3,2,1,0:T(8,128)S(1)}, f32[38,2,8,128]{3,2,1,0:T(8,128)S(1)}, u32[]{:S(2)}, u32[]{:S(2)}) collective-permute-start(f32[38,2,8,128]{3,2,1,0:T(8,128)S(1)} %collective-permute-done.22.refs_1_), channel_id=1, source_target_pairs={{0,128},{128,0},{1,129},{129,1},{2,130},{130,2},{3,131},{131,3},{4... | collective-permute-start | bytes 933896 | tf_op jit(solution)/shard_map/ppermute | solution.py:599
  34.0 26.6 %copy-start = (f32[7,32,2,16,128]{4,3,2,1,0:T(8,128)}, f32[7,32,2,16,128]{4,3,2,1,0:T(8,128)S(1)}, u32[]{:S(2)}) copy-start(f32[7,32,2,16,128]{4,3,2,1,0:T(8,128)S(1)} %get-tuple-element.164.basis.first.refs_6_.far_first) | copy-start | bytes 11010052
  34.0 9.1 %collective-permute-start.30 = (f32[32,2,8,128]{3,2,1,0:T(8,128)S(1)}, f32[32,2,8,128]{3,2,1,0:T(8,128)S(1)}, u32[]{:S(2)}, u32[]{:S(2)}) collective-permute-start(f32[32,2,8,128]{3,2,1,0:T(8,128)S(1)} %get-tuple-element.165), channel_id=1, source_target_pairs={{0,1},{1,2},{2,3},{3,4},{4,5},{5,6},{6,7},{7,8},{8,9},{9,10},{10,1... | collective-permute-start | bytes 786440 | tf_op jit(solution)/shard_map/ppermute | solution.py:595
  37.5 5.6 %collective-permute-start.26 = (f32[6,2,16,128]{3,2,1,0:T(8,128)S(1)}, f32[6,2,16,128]{3,2,1,0:T(8,128)S(1)}, u32[]{:S(2)}, u32[]{:S(2)}) collective-permute-start(f32[6,2,16,128]{3,2,1,0:T(8,128)S(1)} %get-tuple-element.162), channel_id=1, source_target_pairs={{0,32},{32,64},{64,96},{160,128},{192,160},{224,192},{1,33},{33,65... | collective-permute-start | bytes 294920 | tf_op jit(solution)/shard_map/ppermute | solution.py:595
  43.1 1.3 %collective-permute-start.27 = (f32[6,2,16,128]{3,2,1,0:T(8,128)S(1)}, f32[6,2,16,128]{3,2,1,0:T(8,128)S(1)}, u32[]{:S(2)}, u32[]{:S(2)}) collective-permute-start(f32[6,2,16,128]{3,2,1,0:T(8,128)S(1)} %collective-permute-done.26.mine.refs_0_), channel_id=1, source_target_pairs={{0,128},{128,0},{1,129},{129,1},{2,130},{130,2},{3,131},{131,3},{4... | collective-permute-start | bytes 294920 | tf_op jit(solution)/shard_map/ppermute | solution.py:599
  43.1 10.2 %collective-permute-start.31 = (f32[32,2,8,128]{3,2,1,0:T(8,128)S(1)}, f32[32,2,8,128]{3,2,1,0:T(8,128)S(1)}, u32[]{:S(2)}, u32[]{:S(2)}) collective-permute-start(f32[32,2,8,128]{3,2,1,0:T(8,128)S(1)} %collective-permute-done.30.mine), channel_id=1, source_target_pairs={{0,128},{128,0},{1,129},{129,1},{2,130},{130,2},{3,131},{131,3},{4... | collective-permute-start | bytes 786440 | tf_op jit(solution)/shard_map/ppermute | solution.py:599
  44.5 7.1 %collective-permute-start.28 = (f32[12,2,8,128]{3,2,1,0:T(8,128)S(1)}, f32[12,2,8,128]{3,2,1,0:T(8,128)S(1)}, u32[]{:S(2)}, u32[]{:S(2)}) collective-permute-start(f32[12,2,8,128]{3,2,1,0:T(8,128)S(1)} %shard_map.63), channel_id=1, source_target_pairs={{0,1},{1,2},{2,3},{3,4},{4,5},{5,6},{6,7},{7,8},{8,9},{9,10},{10,1... | collective-permute-start | bytes 294920 | tf_op jit(solution)/shard_map/ppermute | solution.py:595
  51.6 9.0 %collective-permute-start.29 = (f32[12,2,8,128]{3,2,1,0:T(8,128)S(1)}, f32[12,2,8,128]{3,2,1,0:T(8,128)S(1)}, u32[]{:S(2)}, u32[]{:S(2)}) collective-permute-start(f32[12,2,8,128]{3,2,1,0:T(8,128)S(1)} %collective-permute-done.28.refs_1_), channel_id=1, source_target_pairs={{0,128},{128,0},{1,129},{129,1},{2,130},{130,2},{3,131},{131,3},{4... | collective-permute-start | bytes 294920 | tf_op jit(solution)/shard_map/ppermute | solution.py:599
  60.6 37.0 %copy-start.1 = (f32[128,128]{1,0:T(8,128)S(1)}, f32[128,128]{1,0:T(8,128)}, u32[]{:S(2)}) copy-start(f32[128,128]{1,0:T(8,128)} %constant.50.clone.tables) | copy-start | bytes 196612
  60.6 37.0 %copy-start.2 = (f32[1,128]{1,0:T(1,128)S(1)}, f32[1,128]{1,0:T(1,128)}, u32[]{:S(2)}) copy-start(f32[1,128]{1,0:T(1,128)} %constant.51.clone.nodes) | copy-start | bytes 1540
  63.2 34.4 %all-to-all-start = ((f32[128,1,128]{2,1,0:T(1,128)}), f32[128,1,128]{2,1,0:T(1,128)S(1)}, u32[]{:S(2)}, u32[]{:S(2)}) async-start(f32[128,1,128]{2,1,0:T(1,128)} %bitcast.3), calls=%async_computation | async-start | bytes 131072 | tf_op jit(solution)/shard_map/all_to_all | solution.py:663
  97.6 4.2 %copy-start.11 = (f32[32,16,256]{2,1,0:T(8,128)S(1)}, f32[32,16,256]{2,1,0:T(8,128)}, u32[]{:S(2)}) copy-start(f32[32,16,256]{2,1,0:T(8,128)} %far_u.1) | copy-start | bytes 1572868

commit v8 on v7

--- a/solution.py
+++ b/solution.py
@@ -221,7 +221,7 @@
         body(i, None)
         return 0
 
-    lax.fori_loop(WIDE + skip, WIDE + nx - skip, inner, 0, unroll=4 if (nx - 2 * skip) % 4 == 0 else 2)
+    lax.fori_loop(WIDE + skip, WIDE + nx - skip, inner, 0, unroll=next(n for n in (6, 5, 4, 3, 2, 1) if (nx - 2 * skip) % n == 0))
 
 
 def over_wedges(nx, halo, skip, body):
@@ -453,7 +453,7 @@
         zero = jnp.zeros((ny, 128), jnp.float32)
         low, high = WIDE + j + 1, WIDE + nx - j - 1
         run = lambda i, made, body=body: body(i, None, made)
-        unroll = 4 if (high - low) % 4 == 0 else 2
+        unroll = next(n for n in (6, 5, 4, 3, 2, 1) if (high - low) % n == 0)
         made = lax.fori_loop(low, high, run, ((zero, zero),) * count, unroll=unroll)
         for n in range(count):
             for c in range(2):
@@ -517,7 +517,7 @@
                 out[i, r : r + 8, c * 128 : (c + 1) * 128] = value
         return 0
 
-    lax.fori_loop(0, nx, body, 0, unroll=2)
+    lax.fori_loop(0, nx, body, 0, unroll=4)
 
 
 def call(kernel, outs, args, limit=16 << 20, flags=(), alias=None, far=0, scratch=()):

time: 104 us -> 101 us (0.971)
  Pallas kernels: 26.4 us -> 24.1 us
    pallas_call x13, Pallas kernels: 26.4 us -> 24.1 us  [call(): pl.pallas_call(kernel, out_shape=shapes + [jax.ShapeDtypeStruct(s, jnp.in...]
  transfers between devices with their start and end apart: 13 -> 13, of which waited for: 7 -> 7; matrix products, arithmetic and copies ran while one was open for 0% -> 0% of each run, Pallas kernels for 17% -> 15%
where the time goes in v8:
time: 101 us; the launch traced here: 99.7 us
  starting transfers between devices  46 us (46%)
  waiting for transfers between devices  28.6 us (28%)
  Pallas kernels  24.1 us (24%)
    pallas_call x13, Pallas kernels, call(): pl.pallas_call(kernel, out_shape=shapes + [jax.ShapeDtypeStruct(s, jnp.in...  24.1 us
    all_to_all x1, starting transfers between devices, per_device(): lax.all_to_all(dots.reshape(parts, 1, 128), AXES, 0, 0).reshape(parts, 128)  23.3 us
    ppermute x6, starting transfers between devices, shifted(): return lax.ppermute(block, ('level', axis), route)  22.2 us
    ppermute x6, waiting for transfers between devices, shifted(): return lax.ppermute(block, ('level', axis), route)  16.6 us
    all_to_all x1, waiting for transfers between devices, per_device(): lax.all_to_all(dots.reshape(parts, 1, 128), AXES, 0, 0).reshape(parts, 128)  11.1 us
  transfers between devices with their start and end apart: 13, of which 7 were waited for; matrix products, arithmetic and copies ran while one was open for 0% of the time, Pallas kernels for 15%

profile of v8, /device:TPU:8, one launch (start us, length us, event | category | flops | bytes accessed | tf_op | source)
XLA Modules:
  0.0 99.7 jit_solution(15875061327139895261)
XLA Ops:
  0.0 1.4 %shard_map.57 = (f32[96,2,8,128]{3,2,1,0:T(8,128)S(1)}, f32[19,2,16,128]{3,2,1,0:T(8,128)S(1)}) custom-call(f32[32,16,256]{2,1,0:T(8,128)} %far_u.1, f32[32,16,256]{2,1,0:T(8,128)} %f.3, f32[32,16,256]{2,1,0:T(8,128)} %d.3), custom_call_target="tpu_custom_call" | custom-call | tf_op jit(solution)/shard_map/pallas_call | solution.py:528
  1.4 3.5 %collective-permute-start.24 = (f32[96,2,8,128]{3,2,1,0:T(8,128)S(1)}, f32[96,2,8,128]{3,2,1,0:T(8,128)S(1)}, u32[]{:S(2)}, u32[]{:S(2)}) collective-permute-start(f32[96,2,8,128]{3,2,1,0:T(8,128)S(1)} %get-tuple-element.147), channel_id=1, source_target_pairs={{0,1},{1,2},{2,3},{3,4},{4,5},{5,6},{6,7},{7,8},{8,9},{9,10},{10,1... | collective-permute-start | bytes 2359304 | tf_op jit(solution)/shard_map/ppermute | solution.py:595
  4.9 3.4 %collective-permute-start.20 = (f32[19,2,16,128]{3,2,1,0:T(8,128)S(1)}, f32[19,2,16,128]{3,2,1,0:T(8,128)S(1)}, u32[]{:S(2)}, u32[]{:S(2)}) collective-permute-start(f32[19,2,16,128]{3,2,1,0:T(8,128)S(1)} %get-tuple-element.146), channel_id=1, source_target_pairs={{0,32},{32,64},{64,96},{160,128},{192,160},{224,192},{1,33},{33,65... | collective-permute-start | bytes 933896 | tf_op jit(solution)/shard_map/ppermute | solution.py:595
  8.3 4.4 %collective-permute-done.20.mine.refs_0_ = f32[19,2,16,128]{3,2,1,0:T(8,128)S(1)} collective-permute-done((f32[19,2,16,128]{3,2,1,0:T(8,128)S(1)}, f32[19,2,16,128]{3,2,1,0:T(8,128)S(1)}, u32[]{:S(2)}, u32[]{:S(2)}) %collective-permute-start.20) | collective-permute-done | bytes 311328 | tf_op jit(solution)/shard_map/ppermute | solution.py:595
  12.7 2.6 %collective-permute-done.24.mine = f32[96,2,8,128]{3,2,1,0:T(8,128)S(1)} collective-permute-done((f32[96,2,8,128]{3,2,1,0:T(8,128)S(1)}, f32[96,2,8,128]{3,2,1,0:T(8,128)S(1)}, u32[]{:S(2)}, u32[]{:S(2)}) %collective-permute-start.24) | collective-permute-done | bytes 786464 | tf_op jit(solution)/shard_map/ppermute | solution.py:595
  15.3 0.1 shard_map.58
  15.4 3.5 %collective-permute-start.22 = (f32[38,2,8,128]{3,2,1,0:T(8,128)S(1)}, f32[38,2,8,128]{3,2,1,0:T(8,128)S(1)}, u32[]{:S(2)}, u32[]{:S(2)}) collective-permute-start(f32[38,2,8,128]{3,2,1,0:T(8,128)S(1)} %shard_map.58), channel_id=1, source_target_pairs={{0,1},{1,2},{2,3},{3,4},{4,5},{5,6},{6,7},{7,8},{8,9},{9,10},{10,1... | collective-permute-start | bytes 933896 | tf_op jit(solution)/shard_map/ppermute | solution.py:595
  18.9 5.3 %collective-permute-done.22.refs_1_ = f32[38,2,8,128]{3,2,1,0:T(8,128)S(1)} collective-permute-done((f32[38,2,8,128]{3,2,1,0:T(8,128)S(1)}, f32[38,2,8,128]{3,2,1,0:T(8,128)S(1)}, u32[]{:S(2)}, u32[]{:S(2)}) %collective-permute-start.22) | collective-permute-done | bytes 311328 | tf_op jit(solution)/shard_map/ppermute | solution.py:595
  24.2 0.0 collective-permute-start.23
  24.2 0.3 shard_map.59
  24.5 2.0 %shard_map.60 = (f32[46,2,48,128]{3,2,1,0:T(8,128)S(1)}, f32[46,2,48,128]{3,2,1,0:T(8,128)S(1)}, f32[46,2,48,128]{3,2,1,0:T(8,128)S(1)}, f32[46,2,48,128]{3,2,1,0:T(8,128)S(1)}, f32[7,32,2,16,128]{4,3,2,1,0:T(8,128)S(1)}) custom-call(f32[96,2,8,128]{3,2,1,0:T(8,128)S(1)} %collective-permute-d, ...), custom_call_target="tpu_custom_call", output_to_operand_aliasing={{0}: (2, {}), {1}: (3, {}), {2}: (4, {}), {3}: (5, {})} | custom-call | tf_op jit(solution)/shard_map/pallas_call | solution.py:528
  26.5 4.3 %shard_map.61 = (f32[46,2,48,128]{3,2,1,0:T(8,128)S(1)}, f32[46,2,48,128]{3,2,1,0:T(8,128)S(1)}, f32[46,2,48,128]{3,2,1,0:T(8,128)S(1)}, f32[46,2,48,128]{3,2,1,0:T(8,128)S(1)}, f32[7,32,2,16,128]{4,3,2,1,0:T(8,128)S(1)}) custom-call(f32[46,2,48,128]{3,2,1,0:T(8,128)S(1)} %get-tuple-elemen, ...), custom_call_target="tpu_custom_call", output_to_operand_aliasing={{0}: (0, {}), {1}: (1, {}), {2}: (2, {}), {3}: (3, {}), {4}... | custom-call | tf_op jit(solution)/shard_map/pallas_call | solution.py:528
  30.9 1.8 %shard_map.62 = (f32[46,2,48,128]{3,2,1,0:T(8,128)S(1)}, f32[46,2,48,128]{3,2,1,0:T(8,128)S(1)}, f32[46,2,48,128]{3,2,1,0:T(8,128)S(1)}, f32[46,2,48,128]{3,2,1,...) custom-call(f32[19,2,16,128]{3,2,1,0:T(8,128)S(1)} %collective-permu, ...), custom_call_target="tpu_custom_call", output_to_operand_aliasing={{0}: (4, {}), {1}: (5, {}), {2}: (6, {}), {3}: (7, {}), {4}... | custom-call | tf_op jit(solution)/shard_map/pallas_call | solution.py:528
  32.6 3.5 %collective-permute-start.30 = (f32[32,2,8,128]{3,2,1,0:T(8,128)S(1)}, f32[32,2,8,128]{3,2,1,0:T(8,128)S(1)}, u32[]{:S(2)}, u32[]{:S(2)}) collective-permute-start(f32[32,2,8,128]{3,2,1,0:T(8,128)S(1)} %get-tuple-element.165), channel_id=1, source_target_pairs={{0,1},{1,2},{2,3},{3,4},{4,5},{5,6},{6,7},{7,8},{8,9},{9,10},{10,1... | collective-permute-start | bytes 786440 | tf_op jit(solution)/shard_map/ppermute | solution.py:595
  36.1 3.4 %collective-permute-start.26 = (f32[6,2,16,128]{3,2,1,0:T(8,128)S(1)}, f32[6,2,16,128]{3,2,1,0:T(8,128)S(1)}, u32[]{:S(2)}, u32[]{:S(2)}) collective-permute-start(f32[6,2,16,128]{3,2,1,0:T(8,128)S(1)} %get-tuple-element.162), channel_id=1, source_target_pairs={{0,32},{32,64},{64,96},{160,128},{192,160},{224,192},{1,33},{33,65... | collective-permute-start | bytes 294920 | tf_op jit(solution)/shard_map/ppermute | solution.py:595
  39.6 2.2 %collective-permute-done.26.mine.refs_0_ = f32[6,2,16,128]{3,2,1,0:T(8,128)S(1)} collective-permute-done((f32[6,2,16,128]{3,2,1,0:T(8,128)S(1)}, f32[6,2,16,128]{3,2,1,0:T(8,128)S(1)}, u32[]{:S(2)}, u32[]{:S(2)}) %collective-permute-start.26) | collective-permute-done | bytes 98336 | tf_op jit(solution)/shard_map/ppermute | solution.py:595
  41.7 0.0 collective-permute-done.30.mine
  41.7 0.5 collective-permute-start.31
  42.3 0.8 collective-permute-done.27.theirs.refs_2_
  43.1 4.9 %collective-permute-start.28 = (f32[12,2,8,128]{3,2,1,0:T(8,128)S(1)}, f32[12,2,8,128]{3,2,1,0:T(8,128)S(1)}, u32[]{:S(2)}, u32[]{:S(2)}) collective-permute-start(f32[12,2,8,128]{3,2,1,0:T(8,128)S(1)} %shard_map.63), channel_id=1, source_target_pairs={{0,1},{1,2},{2,3},{3,4},{4,5},{5,6},{6,7},{7,8},{8,9},{9,10},{10,1... | collective-permute-start | bytes 294920 | tf_op jit(solution)/shard_map/ppermute | solution.py:595
  48.0 2.2 %collective-permute-done.28.refs_1_ = f32[12,2,8,128]{3,2,1,0:T(8,128)S(1)} collective-permute-done((f32[12,2,8,128]{3,2,1,0:T(8,128)S(1)}, f32[12,2,8,128]{3,2,1,0:T(8,128)S(1)}, u32[]{:S(2)}, u32[]{:S(2)}) %collective-permute-start.28) | collective-permute-done | bytes 98336 | tf_op jit(solution)/shard_map/ppermute | solution.py:595
  50.2 0.0 collective-permute-start.29
  50.2 1.6 %shard_map.64.dots.refs_7_ = f32[8,128]{1,0:T(8,128)S(1)} custom-call(f32[32,16,256]{2,1,0:T(8,128)S(1)} %copy-done.10, f32[7,32,2,16,128]{4,3,2,1,0:T(8,128)S(1)} %get-tuple-element.164.basis.first.refs_6_.far_first), custom_call_target="tpu_custom_call" | custom-call | tf_op jit(solution)/shard_map/pallas_call | solution.py:528
  51.8 0.2 shard_map.65
  52.0 2.2 %shard_map.66 = (f32[5,32,2,16,128]{4,3,2,1,0:T(8,128)S(1)}, f32[46,2,48,128]{3,2,1,0:T(8,128)S(1)}, f32[46,2,48,128]{3,2,1,0:T(8,128)S(1)}, f32[6,4,2,16,128]{4,3,2,1,0:T(8,128)S(1)}) custom-call(f32[32,2,8,128]{3,2,1,0:T(8,128)S(1)} %collective-permute-done.30.mine, ...), custom_call_target="tpu_custom_call", output_to_operand_aliasing={{1}: (5, {}), {2}: (6, {})} | custom-call | tf_op jit(solution)/shard_map/pallas_call | solution.py:528
  54.2 4.2 %shard_map.67 = (f32[5,32,2,16,128]{4,3,2,1,0:T(8,128)S(1)}, f32[46,2,48,128]{3,2,1,0:T(8,128)S(1)}, f32[46,2,48,128]{3,2,1,0:T(8,128)S(1)}, f32[6,4,2,16,128]{4,3,2,1,0:T(8,128)S(1)}) custom-call(f32[46,2,48,128]{3,2,1,0:T(8,128)S(1)} %get-tuple-element.163.scale.refs_4_, ...), custom_call_target="tpu_custom_call", output_to_operand_aliasing={{0}: (3, {}), {1}: (4, {}), {2}: (5, {}), {3}: (6, {})} | custom-call | tf_op jit(solution)/shard_map/pallas_call | solution.py:528
  58.4 0.0 copy-start.1
  58.4 0.0 copy-start.2
  58.4 2.6 %shard_map.68 = (f32[5,32,2,16,128]{4,3,2,1,0:T(8,128)S(1)}, f32[46,2,48,128]{3,2,1,0:T(8,128)S(1)}, f32[46,2,48,128]{3,2,1,0:T(8,128)S(1)}, f32[128,128]{1,0:T(8,128)}) custom-call(f32[6,2,16,128]{3,2,1,0:T(8,128)S(1)} %collective-permute-done.26.mine.refs_0_, ...), custom_call_target="tpu_custom_call", output_to_operand_aliasing={{0}: (9, {}), {1}: (10, {}), {2}: (11, {})} | custom-call | tf_op jit(solution)/shard_map/pallas_call | solution.py:528
  61.0 23.3 %all-to-all-start = ((f32[128,1,128]{2,1,0:T(1,128)}), f32[128,1,128]{2,1,0:T(1,128)S(1)}, u32[]{:S(2)}, u32[]{:S(2)}) async-start(f32[128,1,128]{2,1,0:T(1,128)} %bitcast.3), calls=%async_computation | async-start | bytes 131072 | tf_op jit(solution)/shard_map/all_to_all | solution.py:663
  84.3 11.1 %all-to-all-done = f32[128,1,128]{2,1,0:T(1,128)S(1)} async-done(((f32[128,1,128]{2,1,0:T(1,128)}), f32[128,1,128]{2,1,0:T(1,128)S(1)}, u32[]{:S(2)}, u32[]{:S(2)}) %all-to-all-start) | async-done | bytes 65568 | tf_op jit(solution)/shard_map/all_to_all | solution.py:663
  95.4 3.5 %shard_map.69 = (f32[32,16,256]{2,1,0:T(8,128)}, s32[1,1]{1,0:T(1,128)}) custom-call(f32[128,128]{1,0:T(8,128)S(1)} %bitcast.8, f32[128,128]{1,0:T(8,128)S(1)} %copy-done.1, f32[1,128]{1,0:T(1,128)S(1)} %copy-done.2, f32[5,32,2,16,128]{4,3,2,1,0:T(8,128)S(1)} %get-tuple-element.177.second, f32[32,16,256]{2,1,0:T(8,128)} %far_u.1, f32[7,32,2,16,128]{4,3,2,1,0:T(8,128)} %copy-done), custom_call_target="tpu_custom_call" | custom-call | tf_op jit(solution)/shard_map/pallas_call | solution.py:528
  (22 shorter events, 0.1 us)
Async XLA Ops:
  0.0 24.2 %copy-start.10 = (f32[32,16,256]{2,1,0:T(8,128)S(1)}, f32[32,16,256]{2,1,0:T(8,128)}, u32[]{:S(2)}) copy-start(f32[32,16,256]{2,1,0:T(8,128)} %far_u.1) | copy-start | bytes 1572868
  0.0 24.2 %copy-start.7 = (f32[32,16,256]{2,1,0:T(8,128)S(1)}, f32[32,16,256]{2,1,0:T(8,128)}, u32[]{:S(2)}) copy-start(f32[32,16,256]{2,1,0:T(8,128)} %f.3) | copy-start | bytes 1572868
  0.0 24.2 %copy-start.3 = (f32[32,16,256]{2,1,0:T(8,128)S(1)}, f32[32,16,256]{2,1,0:T(8,128)}, u32[]{:S(2)}) copy-start(f32[32,16,256]{2,1,0:T(8,128)} %d.3) | copy-start | bytes 1572868
  1.4 13.9 %collective-permute-start.24 = (f32[96,2,8,128]{3,2,1,0:T(8,128)S(1)}, f32[96,2,8,128]{3,2,1,0:T(8,128)S(1)}, u32[]{:S(2)}, u32[]{:S(2)}) collective-permute-start(f32[96,2,8,128]{3,2,1,0:T(8,128)S(1)} %get-tuple-element.147), channel_id=1, source_target_pairs={{0,1},{1,2},{2,3},{3,4},{4,5},{5,6},{6,7},{7,8},{8,9},{9,10},{10,1... | collective-permute-start | bytes 2359304 | tf_op jit(solution)/shard_map/ppermute | solution.py:595
  4.9 7.8 %collective-permute-start.20 = (f32[19,2,16,128]{3,2,1,0:T(8,128)S(1)}, f32[19,2,16,128]{3,2,1,0:T(8,128)S(1)}, u32[]{:S(2)}, u32[]{:S(2)}) collective-permute-start(f32[19,2,16,128]{3,2,1,0:T(8,128)S(1)} %get-tuple-element.146), channel_id=1, source_target_pairs={{0,32},{32,64},{64,96},{160,128},{192,160},{224,192},{1,33},{33,65... | collective-permute-start | bytes 933896 | tf_op jit(solution)/shard_map/ppermute | solution.py:595
  12.7 2.6 %collective-permute-start.21 = (f32[19,2,16,128]{3,2,1,0:T(8,128)S(1)}, f32[19,2,16,128]{3,2,1,0:T(8,128)S(1)}, u32[]{:S(2)}, u32[]{:S(2)}) collective-permute-start(f32[19,2,16,128]{3,2,1,0:T(8,128)S(1)} %collective-permute-done.20.mine.refs_0_), channel_id=1, source_target_pairs={{0,128},{128,0},{1,129},{129,1},{2,130},{130,2},{3,131},{131,3},{4... | collective-permute-start | bytes 933896 | tf_op jit(solution)/shard_map/ppermute | solution.py:599
  15.3 9.2 %collective-permute-start.25 = (f32[96,2,8,128]{3,2,1,0:T(8,128)S(1)}, f32[96,2,8,128]{3,2,1,0:T(8,128)S(1)}, u32[]{:S(2)}, u32[]{:S(2)}) collective-permute-start(f32[96,2,8,128]{3,2,1,0:T(8,128)S(1)} %collective-permute-done.24.mine), channel_id=1, source_target_pairs={{0,128},{128,0},{1,129},{129,1},{2,130},{130,2},{3,131},{131,3},{4... | collective-permute-start | bytes 2359304 | tf_op jit(solution)/shard_map/ppermute | solution.py:599
  15.4 8.8 %collective-permute-start.22 = (f32[38,2,8,128]{3,2,1,0:T(8,128)S(1)}, f32[38,2,8,128]{3,2,1,0:T(8,128)S(1)}, u32[]{:S(2)}, u32[]{:S(2)}) collective-permute-start(f32[38,2,8,128]{3,2,1,0:T(8,128)S(1)} %shard_map.58), channel_id=1, source_target_pairs={{0,1},{1,2},{2,3},{3,4},{4,5},{5,6},{6,7},{7,8},{8,9},{9,10},{10,1... | collective-permute-start | bytes 933896 | tf_op jit(solution)/shard_map/ppermute | solution.py:595
  24.2 6.7 %collective-permute-start.23 = (f32[38,2,8,128]{3,2,1,0:T(8,128)S(1)}, f32[38,2,8,128]{3,2,1,0:T(8,128)S(1)}, u32[]{:S(2)}, u32[]{:S(2)}) collective-permute-start(f32[38,2,8,128]{3,2,1,0:T(8,128)S(1)} %collective-permute-done.22.refs_1_), channel_id=1, source_target_pairs={{0,128},{128,0},{1,129},{129,1},{2,130},{130,2},{3,131},{131,3},{4... | collective-permute-start | bytes 933896 | tf_op jit(solution)/shard_map/ppermute | solution.py:599
  32.6 25.7 %copy-start = (f32[7,32,2,16,128]{4,3,2,1,0:T(8,128)}, f32[7,32,2,16,128]{4,3,2,1,0:T(8,128)S(1)}, u32[]{:S(2)}) copy-start(f32[7,32,2,16,128]{4,3,2,1,0:T(8,128)S(1)} %get-tuple-element.164.basis.first.refs_6_.far_first) | copy-start | bytes 11010052
  32.6 9.1 %collective-permute-start.30 = (f32[32,2,8,128]{3,2,1,0:T(8,128)S(1)}, f32[32,2,8,128]{3,2,1,0:T(8,128)S(1)}, u32[]{:S(2)}, u32[]{:S(2)}) collective-permute-start(f32[32,2,8,128]{3,2,1,0:T(8,128)S(1)} %get-tuple-element.165), channel_id=1, source_target_pairs={{0,1},{1,2},{2,3},{3,4},{4,5},{5,6},{6,7},{7,8},{8,9},{9,10},{10,1... | collective-permute-start | bytes 786440 | tf_op jit(solution)/shard_map/ppermute | solution.py:595
  36.1 5.6 %collective-permute-start.26 = (f32[6,2,16,128]{3,2,1,0:T(8,128)S(1)}, f32[6,2,16,128]{3,2,1,0:T(8,128)S(1)}, u32[]{:S(2)}, u32[]{:S(2)}) collective-permute-start(f32[6,2,16,128]{3,2,1,0:T(8,128)S(1)} %get-tuple-element.162), channel_id=1, source_target_pairs={{0,32},{32,64},{64,96},{160,128},{192,160},{224,192},{1,33},{33,65... | collective-permute-start | bytes 294920 | tf_op jit(solution)/shard_map/ppermute | solution.py:595
  41.7 1.3 %collective-permute-start.27 = (f32[6,2,16,128]{3,2,1,0:T(8,128)S(1)}, f32[6,2,16,128]{3,2,1,0:T(8,128)S(1)}, u32[]{:S(2)}, u32[]{:S(2)}) collective-permute-start(f32[6,2,16,128]{3,2,1,0:T(8,128)S(1)} %collective-permute-done.26.mine.refs_0_), channel_id=1, source_target_pairs={{0,128},{128,0},{1,129},{129,1},{2,130},{130,2},{3,131},{131,3},{4... | collective-permute-start | bytes 294920 | tf_op jit(solution)/shard_map/ppermute | solution.py:599
  41.7 10.2 %collective-permute-start.31 = (f32[32,2,8,128]{3,2,1,0:T(8,128)S(1)}, f32[32,2,8,128]{3,2,1,0:T(8,128)S(1)}, u32[]{:S(2)}, u32[]{:S(2)}) collective-permute-start(f32[32,2,8,128]{3,2,1,0:T(8,128)S(1)} %collective-permute-done.30.mine), channel_id=1, source_target_pairs={{0,128},{128,0},{1,129},{129,1},{2,130},{130,2},{3,131},{131,3},{4... | collective-permute-start | bytes 786440 | tf_op jit(solution)/shard_map/ppermute | solution.py:599
  43.1 7.1 %collective-permute-start.28 = (f32[12,2,8,128]{3,2,1,0:T(8,128)S(1)}, f32[12,2,8,128]{3,2,1,0:T(8,128)S(1)}, u32[]{:S(2)}, u32[]{:S(2)}) collective-permute-start(f32[12,2,8,128]{3,2,1,0:T(8,128)S(1)} %shard_map.63), channel_id=1, source_target_pairs={{0,1},{1,2},{2,3},{3,4},{4,5},{5,6},{6,7},{7,8},{8,9},{9,10},{10,1... | collective-permute-start | bytes 294920 | tf_op jit(solution)/shard_map/ppermute | solution.py:595
  50.2 8.1 %collective-permute-start.29 = (f32[12,2,8,128]{3,2,1,0:T(8,128)S(1)}, f32[12,2,8,128]{3,2,1,0:T(8,128)S(1)}, u32[]{:S(2)}, u32[]{:S(2)}) collective-permute-start(f32[12,2,8,128]{3,2,1,0:T(8,128)S(1)} %collective-permute-done.28.refs_1_), channel_id=1, source_target_pairs={{0,128},{128,0},{1,129},{129,1},{2,130},{130,2},{3,131},{131,3},{4... | collective-permute-start | bytes 294920 | tf_op jit(solution)/shard_map/ppermute | solution.py:599
  58.4 37.0 %copy-start.1 = (f32[128,128]{1,0:T(8,128)S(1)}, f32[128,128]{1,0:T(8,128)}, u32[]{:S(2)}) copy-start(f32[128,128]{1,0:T(8,128)} %constant.50.clone.tables) | copy-start | bytes 196612
  58.4 37.0 %copy-start.2 = (f32[1,128]{1,0:T(1,128)S(1)}, f32[1,128]{1,0:T(1,128)}, u32[]{:S(2)}) copy-start(f32[1,128]{1,0:T(1,128)} %constant.51.clone.nodes) | copy-start | bytes 1540
  61.0 34.4 %all-to-all-start = ((f32[128,1,128]{2,1,0:T(1,128)}), f32[128,1,128]{2,1,0:T(1,128)S(1)}, u32[]{:S(2)}, u32[]{:S(2)}) async-start(f32[128,1,128]{2,1,0:T(1,128)} %bitcast.3), calls=%async_computation | async-start | bytes 131072 | tf_op jit(solution)/shard_map/all_to_all | solution.py:663
  95.4 4.1 %copy-start.11 = (f32[32,16,256]{2,1,0:T(8,128)S(1)}, f32[32,16,256]{2,1,0:T(8,128)}, u32[]{:S(2)}) copy-start(f32[32,16,256]{2,1,0:T(8,128)} %far_u.1) | copy-start | bytes 1572868
